TPU v7x, 8 devices: a whole 2x2x1 slice. The times are simulated.
8 devices in a mesh: dp: 2 (over z, y), sh: 4 (over x, core).
Axes of the slice: x: 2, y: 2, z: 1, core: 2. Of those that a mesh axis runs over, the one named last changes fastest.
Arguments:
- k_prefill: bfloat16 [24, 10240, 4, 256], P('dp', None, 'sh'), parts along dimension 0
- v_prefill: bfloat16 [24, 10240, 4, 256], P('dp', None, 'sh'), parts along dimension 0
- lengths: int32 [24], P('dp'), parts along dimension 0
- residual: bfloat16 [24, 2304], P(('dp', 'sh')), parts along dimension 0
- norm_gain: bfloat16 [2304], replicated
- w_query: bfloat16 [2304, 2048], replicated
- w_key: bfloat16 [2304, 1024], replicated
- w_value: bfloat16 [2304, 1024], replicated
- w_out: bfloat16 [2048, 2304], replicated
Outputs:
- output 1: bfloat16 [24, 2304], P(('dp', 'sh')), parts along dimension 0
- output 2: bfloat16 [24, 4096, 4, 256], P(('dp', 'sh')), parts along dimension 0
- output 3: bfloat16 [24, 4096, 4, 256], P(('dp', 'sh')), parts along dimension 0
There are 2 independent parts. A program takes and returns all parts, laid end to end along the dimension named above; an argument that names none is the same for every part.
All inputs are finite; a program needn't handle non-finite values.
Results may differ from a plain program's by a relative error of at most 0.0047.
Values are sent between devices in bfloat16 or wider.
A program may use at most 1 GiB of HBM per device.

v0:
```python
import functools

import jax
import jax.numpy as jnp
from jax import lax
from jax.experimental import pallas as pl
from jax.experimental.pallas import tpu as pltpu
from jax.sharding import PartitionSpec as P


WINDOW = 4096
THETA = 10000.0
EPS = 1e-5
GRAN = 64
WIN_G = WINDOW // GRAN
STEP = 8
FIXED = 128
UNITS = (32, 16, 8, 4, 4)
SPARE = sum(UNITS)
QUANTUM = UNITS[-1]
LEVELS = SPARE // QUANTUM + 1
K_PIECES = (8, 24, 96)
V_PIECES = (64, 32, 16, 8, 4, 4)
WAYS, ROWS = 4, 3
VMEM_LIMIT = 67_043_328
ANYWHERE = pl.BlockSpec(memory_space=pl.ANY)


def starts_of(sizes):
    return [sum(sizes[:i]) for i in range(len(sizes))]


def active_units(level):
    full = level == LEVELS - 1
    return [full | ((level & (size // QUANTUM)) != 0) for size in UNITS[:-1]] + [full]


def rotate(heads, positions):
    head_dim = heads.shape[-1]
    half_dim = head_dim // 2
    inv_freq = THETA ** (-2.0 * jnp.arange(half_dim, dtype=jnp.float32) / head_dim)
    angles = positions.astype(jnp.float32).reshape(positions.shape + (1,) * (heads.ndim - 1)) * inv_freq
    cos_part = jnp.cos(angles)
    sin_part = jnp.sin(angles)
    first_half = heads[..., :half_dim].astype(jnp.float32)
    second_half = heads[..., half_dim:].astype(jnp.float32)
    return jnp.concatenate([first_half * cos_part - second_half * sin_part, second_half * cos_part + first_half * sin_part], axis=-1).astype(jnp.bfloat16)


def blank(shape, dtype):
    return pl.pallas_call(
        lambda o_ref: None,
        out_shape=jax.ShapeDtypeStruct(shape, dtype),
        out_specs=ANYWHERE,
        name="blank",
    )()


def cleared_kernel(n_ref, k_ref, v_ref, zeros, sem):
    zeros[...] = jnp.zeros_like(zeros)

    def each(act):
        for r in range(ROWS):
            def one(g, carry):
                for ref in (k_ref, v_ref):
                    act(pltpu.make_async_copy(zeros, ref.at[r, pl.ds(g * GRAN, GRAN)], sem))
                return carry

            lax.fori_loop(jnp.minimum(n_ref[r] // GRAN + 1, WIN_G), WIN_G, one, 0)

    each(lambda copy: copy.start())
    each(lambda copy: copy.wait())


def cleared(n, shape):
    return pl.pallas_call(
        cleared_kernel,
        grid_spec=pltpu.PrefetchScalarGridSpec(
            num_scalar_prefetch=1, grid=(1,), in_specs=[], out_specs=[ANYWHERE, ANYWHERE],
            scratch_shapes=[pltpu.VMEM((GRAN, WAYS, 256), jnp.bfloat16), pltpu.SemaphoreType.DMA]),
        out_shape=[jax.ShapeDtypeStruct(shape, jnp.bfloat16)] * 2,
        compiler_params=pltpu.CompilerParams(vmem_limit_bytes=VMEM_LIMIT),
        cost_estimate=pl.CostEstimate(flops=10_000_000, bytes_accessed=20_000_000, transcendentals=0),
        name="cleared",
    )(n)


class Lists:
    def __init__(self, n, row0, seq_g):
        self.n, self.row0, self.seq_g = n, row0, seq_g
        self.lap = n // WINDOW
        self.cut = n % WINDOW
        width = jnp.minimum(n // GRAN + 1, WIN_G)
        self.off1 = width[..., 0:1]
        self.off2 = self.off1 + width[..., 1:2]
        self.size = self.off2 + width[..., 2:3]

    def of_row(self, x, r):
        return jnp.where(r == 0, x[..., 0:1], jnp.where(r == 1, x[..., 1:2], x[..., 2:3]))

    def at(self, i):
        r = (i >= self.off1).astype(jnp.int32) + (i >= self.off2).astype(jnp.int32)
        return r, i - jnp.where(r == 0, 0, jnp.where(r == 1, self.off1, self.off2))

    def source(self, i):
        r, g = self.at(i)
        lap, cut = self.of_row(self.lap, r), self.of_row(self.cut, r)
        older = jnp.maximum(lap - 1, 0)
        base = (self.row0 + r) * self.seq_g
        src = base + jnp.minimum(jnp.where(g <= cut // GRAN, lap, older) * WIN_G + g, self.seq_g - 1)
        mixed = jnp.where(lap >= 1, base + older * WIN_G + g, -1)
        return src, jnp.where(g == cut // GRAN, (mixed + 1) * GRAN + cut % GRAN, -1)


def pack_kernel(base, size, steps, src_ref, mix_ref, *refs):
    prefills, outs, (older, sem) = refs[:-4], refs[-4:-2], refs[-2:]
    i = pl.program_id(0)
    first = base + lax.rem(i, steps) * size

    def by_tensor(do):
        for k, ref in enumerate(prefills):
            pl.when((i >= k * steps) & (i < (k + 1) * steps))(functools.partial(do, ref))

    def fetch(ref, act):
        def one(t, carry):
            for a in range(2):
                act(pltpu.make_async_copy(ref.at[src_ref[a, first + t]], outs[a].at[t], sem))
            return carry

        lax.fori_loop(0, size, one, 0)

    by_tensor(lambda ref: fetch(ref, lambda copy: copy.start()))
    fetch(prefills[0], lambda copy: copy.wait())

    for a in range(2):
        def patch(t, carry):
            code = mix_ref[a, first + t]

            @pl.when(code >= 0)
            def _():
                granule = code // GRAN - 1

                @pl.when(granule >= 0)
                def _():
                    by_tensor(lambda ref: pltpu.make_async_copy(ref.at[granule], older, sem).start())
                    pltpu.make_async_copy(prefills[0].at[0], older, sem).wait()

                @pl.when(granule < 0)
                def _():
                    older[...] = jnp.zeros_like(older)

                newer = lax.broadcasted_iota(jnp.int32, (GRAN, 256), 0) < lax.rem(code, GRAN)
                outs[a][t] = jnp.where(newer, outs[a][t].astype(jnp.float32), older[...].astype(jnp.float32)).astype(jnp.bfloat16)

            return carry

        lax.fori_loop(0, size, patch, 0)


def pack(prefills, src, mix, base, count):
    size = next(x for x in (16, 8, 4) if count % x == 0)
    steps = count // size
    total = count * len(prefills)
    return pl.pallas_call(
        functools.partial(pack_kernel, base, size, steps),
        grid_spec=pltpu.PrefetchScalarGridSpec(
            num_scalar_prefetch=2,
            grid=(steps * len(prefills),),
            in_specs=[ANYWHERE] * len(prefills),
            out_specs=[pl.BlockSpec((size, GRAN, 256), lambda i, src_ref, mix_ref: (i, 0, 0))] * 2,
            scratch_shapes=[pltpu.VMEM((GRAN, 256), jnp.bfloat16), pltpu.SemaphoreType.DMA],
        ),
        out_shape=[jax.ShapeDtypeStruct((total, GRAN, 256), jnp.bfloat16)] * 2,
        compiler_params=pltpu.CompilerParams(dimension_semantics=("arbitrary",), vmem_limit_bytes=VMEM_LIMIT),
        cost_estimate=pl.CostEstimate(flops=10_000_000, bytes_accessed=total * 130_000, transcendentals=0),
        name="pack",
    )(src, mix, *prefills)


def assemble_kernel(is_key, base, size, steps, segments, code_ref, idx_ref, n_ref, me_ref, *refs):
    num_far = 2 * (1 + max(s[2] for s in segments))
    far_refs = refs[:num_far]
    near_ref, own_ref, new_ref, qp_ref, prev_ref, _, cache_ref, res_ref, xb, mix, ob, acc, sems = refs[num_far:]
    i = pl.program_id(0)
    me = me_ref[0]
    slot = lax.rem(i, 2)

    def code_at(step, t):
        return code_ref[0, base + step * size + t]

    def active_at(step):
        return functools.reduce(jnp.maximum, [code_at(step, t) for t in range(size)]) >= 0

    def reads(step, buf, act):
        @pl.when(active_at(step))
        def _():
            for begin, end, entry, offset, count, place in segments:
                @pl.when((step >= begin) & (step < end))
                def _():
                    for d in range(2):
                        act(pltpu.make_async_copy(far_refs[2 * entry + d].at[pl.ds(offset + (step - begin) * size, count)], xb.at[buf, me ^ (2 + d), pl.ds(place, count)], sems.at[0, buf]))

            def one(t, carry):
                at = idx_ref[0, base + step * size + t]
                act(pltpu.make_async_copy(near_ref.at[at], xb.at[buf, me ^ 1, t], sems.at[0, buf]))
                act(pltpu.make_async_copy(own_ref.at[at], xb.at[buf, me, t], sems.at[0, buf]))
                return carry

            lax.fori_loop(0, size, one, 0)

    def write(step, t, buf):
        code = code_at(step, t)
        return pltpu.make_async_copy(ob.at[buf, t], cache_ref.at[code // WIN_G, pl.ds(lax.rem(code, WIN_G) * GRAN, GRAN)], sems.at[1, buf])

    def written(step, buf):
        def one(t, carry):
            @pl.when(code_at(step, t) >= 0)
            def _():
                write(step, t, buf).wait()

            return carry

        lax.fori_loop(0, size, one, 0)

    @pl.when(i == 0)
    def _():
        reads(i, slot, lambda copy: copy.start())
        if not is_key:
            acc[...] = prev_ref[...]

    if steps > 1:
        @pl.when(i + 1 < steps)
        def _():
            reads(i + 1, 1 - slot, lambda copy: copy.start())

    if steps > 2:
        @pl.when(i >= 2)
        def _():
            written(i - 2, slot)

    reads(i, slot, lambda copy: copy.wait())
    active = active_at(i)

    @pl.when(active)
    def _():
        def one(t, carry):
            code = code_at(i, t)

            @pl.when(code < 0)
            def _():
                for h in range(WAYS):
                    xb[slot, h, t] = jnp.zeros((GRAN, 256), jnp.bfloat16)

            for r in range(ROWS):
                cut = lax.rem(n_ref[r], WINDOW)

                @pl.when(code == r * WIN_G + cut // GRAN)
                def _():
                    here = lax.broadcasted_iota(jnp.int32, (GRAN, 256), 0) == lax.rem(cut, GRAN)
                    for h in range(WAYS):
                        new = jnp.broadcast_to(new_ref[r * WAYS + h], (GRAN, 256))
                        xb[slot, h, t] = jnp.where(here, new, xb[slot, h, t].astype(jnp.float32)).astype(jnp.bfloat16)

            @pl.when(code >= 0)
            def _():
                for h in range(WAYS):
                    x = xb[slot, h, t].astype(jnp.float32)
                    for half in range(2):
                        mix[half, pl.ds(h, GRAN, stride=WAYS), :] = x[:, half * 128:(half + 1) * 128]
                joined = jnp.concatenate([mix[half].astype(jnp.bfloat16) for half in range(2)], axis=1)
                ob[slot, t] = joined.reshape(GRAN, WAYS, 256)
                write(i, t, slot).start()

            return carry

        lax.fori_loop(0, size, one, 0)

        lanes = size * GRAN
        if is_key:
            lane = lax.broadcasted_iota(jnp.int32, (8, lanes), 1)
            row = lax.broadcasted_iota(jnp.int32, (8, lanes), 0) // 2
            code = jnp.full((8, lanes), -1, jnp.int32)
            for t in range(size):
                code = jnp.where(lane // GRAN == t, code_at(i, t), code)
            length = jnp.where(row == 0, n_ref[0], jnp.where(row == 1, n_ref[1], n_ref[2]))
            place = (code % WIN_G) * GRAN + lane % GRAN
            live = (code >= 0) & (code // WIN_G == row) & ((length >= WINDOW) | (place <= length))
            for h in range(WAYS):
                s = lax.dot_general(qp_ref[h], xb[slot, h].reshape(lanes, 256), (((1,), (1,)), ((), ())), preferred_element_type=jnp.float32)
                res_ref[h] = jnp.where(live, s / 16.0, -jnp.inf)
        else:
            for h in range(WAYS):
                acc[h] += jnp.dot(qp_ref[h], xb[slot, h].reshape(lanes, 256), preferred_element_type=jnp.float32)

    if is_key:
        @pl.when(jnp.logical_not(active))
        def _():
            res_ref[...] = jnp.full_like(res_ref, -jnp.inf)

    @pl.when(i == steps - 1)
    def _():
        if not is_key:
            res_ref[...] = acc[...]
        if steps >= 2:
            written(i - 1, 1 - slot)
        written(i, slot)


def assemble(is_key, base, codes, places, n, me, far, near, own, new, qp, prev, cache):
    total = sum(f[3] for f in far)
    size = min(STEP, total)
    steps = total // size
    segments, at = [], 0
    for entry, (_, _, offset, count) in enumerate(far):
        if count >= size:
            segments.append((at // size, (at + count) // size, entry, offset, size, 0))
        else:
            segments.append((at // size, at // size + 1, entry, offset, count, at % size))
        at += count
    whole = lambda *shape: pl.BlockSpec(shape, lambda i, *_: (0,) * len(shape))
    by_step = pl.BlockSpec((WAYS, 8, size * GRAN), lambda i, *_: (0, 0, base // size + i))
    if is_key:
        qp_spec, prev_spec, res_spec = whole(WAYS, 8, 256), ANYWHERE, by_step
    else:
        qp_spec, prev_spec, res_spec = by_step, whole(WAYS, 8, 256), whole(WAYS, 8, 256)
    after = 4 + 2 * len(far) + 2
    aliases = {after + 3: 0}
    if is_key:
        aliases[after + 2] = 1
    return pl.pallas_call(
        functools.partial(assemble_kernel, is_key, base, size, steps, segments),
        grid_spec=pltpu.PrefetchScalarGridSpec(
            num_scalar_prefetch=4,
            grid=(steps,),
            in_specs=[ANYWHERE] * (2 * len(far) + 2) + [whole(ROWS * WAYS, 1, 256), qp_spec, prev_spec, ANYWHERE],
            out_specs=[ANYWHERE, res_spec],
            scratch_shapes=[
                pltpu.VMEM((2, WAYS, size, GRAN, 256), jnp.bfloat16),
                pltpu.VMEM((2, WAYS * GRAN, 128), jnp.float32),
                pltpu.VMEM((2, size, GRAN, WAYS, 256), jnp.bfloat16),
                pltpu.VMEM((WAYS, 8, 256), jnp.float32),
                pltpu.SemaphoreType.DMA((2, 2)),
            ],
        ),
        out_shape=[jax.ShapeDtypeStruct(cache.shape, cache.dtype), jax.ShapeDtypeStruct(prev.shape, prev.dtype)],
        input_output_aliases=aliases,
        compiler_params=pltpu.CompilerParams(dimension_semantics=("arbitrary",), vmem_limit_bytes=VMEM_LIMIT),
        cost_estimate=pl.CostEstimate(flops=10_000_000, bytes_accessed=steps * 4_000_000, transcendentals=0),
        name="assemble_keys" if is_key else "assemble_values",
    )(codes, places, n, me, *[x for f in far for x in f[:2]], near, own, new, qp, prev, cache)


def solution(mesh):
    head_spec = P('dp', None, 'sh', None)
    row_spec = P(('dp', 'sh'))
    full_spec = P(None, None)

    def send(x, d):
        return lax.ppermute(x, 'sh', [(i, i ^ d) for i in range(WAYS)])

    def step(k_prefill, v_prefill, lengths, residual, norm_gain, w_query, w_key, w_value, w_out):
        seq_g = k_prefill.shape[1] // GRAN
        me = lax.axis_index('sh').astype(jnp.int32)
        peers = me ^ jnp.arange(WAYS, dtype=jnp.int32)
        by_peer = lengths[(peers[:, None] * ROWS + jnp.arange(ROWS, dtype=jnp.int32)).reshape(-1)].reshape(WAYS, ROWS)
        mine = by_peer[0]
        prefill = {True: k_prefill.reshape(-1, GRAN, 256), False: v_prefill.reshape(-1, GRAN, 256)}

        def lists(*ds):
            return Lists(jnp.stack([by_peer[d] for d in ds]), jnp.stack([(me ^ d) * ROWS for d in ds])[:, None], seq_g)

        def span(count):
            return jnp.arange(count, dtype=jnp.int32)[None, :]

        def held(which, i):
            src, mixed = which.source(i)
            valid = i < which.size
            return jnp.where(valid, src, 0), jnp.where(valid, mixed, -1)

        far, far_other, close, self_list = lists(2, 3), lists(3, 2), lists(1, 0), lists(0)
        fixed_src, fixed_mix = held(far, span(FIXED))
        close_src, close_mix = held(close, span(ROWS * WIN_G))

        sizes = jnp.sum(jnp.minimum(lengths // GRAN + 1, WIN_G).reshape(WAYS, ROWS), axis=1)
        excess = jnp.max(jnp.sum(jnp.maximum(sizes - FIXED, 0).reshape(WAYS // 2, 2), axis=1))
        level = lax.pmax((excess + 2 * QUANTUM - 1) // (2 * QUANTUM), 'dp')
        spare = QUANTUM * level
        on = active_units(level)
        column = span(SPARE)
        unit = functools.reduce(jnp.add, [(column >= s).astype(jnp.int32) for s in starts_of(UNITS)[1:]])
        skipped, used, place = 0, jnp.zeros_like(column, dtype=bool), column
        for u, size in enumerate(UNITS):
            used = jnp.where(unit == u, on[u], used)
            place = jnp.where(unit == u, column - skipped, place)
            skipped = skipped + jnp.where(on[u], 0, size)
        own_at, other_at = FIXED + place, FIXED + 2 * spare - 1 - place
        src_a, mix_a = held(far, own_at)
        src_b, mix_b = held(far_other, other_at)
        is_own = used & (own_at < far.size)
        is_other = used & (own_at >= far.size) & (other_at < far_other.size)
        spare_src = jnp.where(is_own, src_a, jnp.where(is_other, src_b, 0))
        spare_mix = jnp.where(is_own, mix_a, jnp.where(is_other, mix_b, -1))

        def belongs(i, valid):
            r, g = self_list.at(i)
            return jnp.where(valid & (i < self_list.size), r * WIN_G + g, -1), jnp.clip(i, 0, ROWS * WIN_G - 1)

        parts = [belongs(span(FIXED), True), belongs(own_at, used), belongs(other_at, used)]
        codes = jnp.concatenate([p[0] for p in parts], axis=1)
        places = jnp.concatenate([p[1] for p in parts], axis=1)

        fixed_got = {True: [], False: []}
        packed_values = []
        for base, count in zip(starts_of(K_PIECES), K_PIECES):
            out = pack([prefill[True]], fixed_src, fixed_mix, base, count)
            a = send(out[0], 2)
            b = send(out[1], 3)
            fixed_got[True].append((a, b))
        close_got = {}
        for is_key in (True, False):
            near, own = pack([prefill[is_key]], close_src, close_mix, 0, ROWS * WIN_G)
            close_got[is_key] = (send(near, 1), own)
        spare_packed = [pack([prefill[True], prefill[False]], spare_src, spare_mix, base, count) for base, count in zip(starts_of(UNITS), UNITS)]
        for base, count in zip(starts_of(V_PIECES), V_PIECES):
            packed_values.append(pack([prefill[False]], fixed_src, fixed_mix, base, count))

        resid_f32 = residual.astype(jnp.float32)
        inv_rms = lax.rsqrt(jnp.mean(resid_f32 * resid_f32, axis=-1, keepdims=True) + EPS)
        normed = (resid_f32 * inv_rms * norm_gain.astype(jnp.float32)).astype(jnp.bfloat16)
        q_group = w_query.shape[1] // (WAYS * 256)
        q_heads = jnp.dot(normed, w_query, preferred_element_type=jnp.float32).astype(jnp.bfloat16).reshape(ROWS, WAYS, q_group, 256)
        k_new = jnp.dot(normed, w_key, preferred_element_type=jnp.float32).astype(jnp.bfloat16).reshape(ROWS, WAYS, 256)
        v_new = jnp.dot(normed, w_value, preferred_element_type=jnp.float32).astype(jnp.bfloat16).reshape(ROWS, WAYS, 256)
        q_heads = rotate(q_heads, mine)
        k_new = rotate(k_new, mine)
        new = {True: k_new.astype(jnp.float32).reshape(-1, 1, 256), False: v_new.astype(jnp.float32).reshape(-1, 1, 256)}
        q_pad = jnp.pad(q_heads.transpose(1, 0, 2, 3).reshape(WAYS, ROWS * q_group, 256), ((0, 0), (0, 8 - ROWS * q_group), (0, 0)))
        k_cache, v_cache = cleared(mine, (ROWS, WINDOW, WAYS, 256))
        scores = blank((WAYS, 8, codes.shape[1] * GRAN), jnp.float32)

        def branch(lvl):
            keep = [bool(x) for x in active_units(lvl)]

            def run(pairs):
                return [(send(a, 2), send(b, 3)) if k else (blank(a.shape, a.dtype), blank(b.shape, b.dtype)) for k, (a, b) in zip(keep, pairs)]

            return run

        spare_packed, packed_values, ready = lax.optimization_barrier((spare_packed, packed_values, (new, q_pad, k_cache, v_cache, scores, close_got[True][1], close_got[False][1])))
        new, q_pad, k_cache, v_cache, scores, own_k, own_v = ready
        own = {True: own_k, False: own_v}
        spare_got = lax.switch(level, [branch(x) for x in range(LEVELS)], spare_packed)
        spare_got, packed_values = lax.optimization_barrier((spare_got, packed_values))
        for a, b in packed_values:
            a = send(a, 2)
            b = send(b, 3)
            fixed_got[False].append((a, b))
        forwarded = [(send(b, 1), send(a, 1)) for a, b in spare_got]

        me1 = me.reshape(1)

        def run(is_key, base, far_parts, qp, prev, cache):
            return assemble(is_key, base, codes, places, mine, me1, far_parts, close_got[is_key][0], own[is_key], new[is_key], qp, prev, cache)

        def fixed(pieces, got):
            return [(a, b, 0, count) for (a, b), count in zip(got, pieces)]

        def spares(is_key):
            return [(a, b, 0 if is_key else count, count) for got in (spare_got, forwarded) for (a, b), count in zip(got, UNITS)]

        k_cache, scores = run(True, 0, fixed(K_PIECES, fixed_got[True]), q_pad, scores, k_cache)
        k_cache, scores = run(True, FIXED, spares(True), q_pad, scores, k_cache)
        exp_scores = jnp.exp(scores - jnp.max(scores, axis=-1, keepdims=True))
        weights = (exp_scores / jnp.sum(exp_scores, axis=-1, keepdims=True)).astype(jnp.bfloat16)
        sums = jnp.zeros((WAYS, 8, 256), jnp.float32)
        v_cache, sums = run(False, FIXED, spares(False), weights, sums, v_cache)
        for base, part in zip(starts_of(V_PIECES), fixed(V_PIECES, fixed_got[False])):
            v_cache, sums = run(False, base, [part], weights, sums, v_cache)
        attn_out = sums[:, :ROWS * q_group].astype(jnp.bfloat16).reshape(WAYS, ROWS, q_group * 256).transpose(1, 0, 2).reshape(ROWS, WAYS * q_group * 256)
        resid_out = (resid_f32 + jnp.dot(attn_out, w_out, preferred_element_type=jnp.float32)).astype(jnp.bfloat16)
        return resid_out, k_cache, v_cache

    return jax.shard_map(
        step, mesh=mesh, in_specs=(head_spec, head_spec, P('dp'), P(('dp', 'sh'), None), P(None), full_spec, full_spec, full_spec, full_spec),
        out_specs=(P(('dp', 'sh'), None), row_spec, row_spec), check_vma=False)
```

profile of v0, /device:TPU:6, one launch (start us, length us, event | category | flops | bytes accessed | tf_op | source)
XLA Modules:
  0.0 692.4 jit_solution(11147191525477379090)
XLA Ops:
  3.0 4.9 pmax.7
  16.7 10.6 %pack.21 = (bf16[64,64,256]{2,1,0:T(8,128)(2,1)}, bf16[64,64,256]{2,1,0:T(8,128)(2,1)}) custom-call(s32[2,128]{1,0:T(2,128)} %get-tuple-element.495.src_ref, s32[2,128]{1,0:T(2,128)} %get-tuple-element.494.mix_ref, bf16[1920,64,256]{2,1,0:T(8,128)(2,1)} %bitcast.33), custom_call_target="tpu_custom_call" | custom-call | flops 10000000 | bytes 8320000 | tf_op jit(solution)/shard_map/pack/pallas_call | solution.py:164
  27.3 6.1 pack.22
  35.3 27.4 %pack.28 = (bf16[192,64,256]{2,1,0:T(8,128)(2,1)}, bf16[192,64,256]{2,1,0:T(8,128)(2,1)}) custom-call(s32[2,192]{1,0:T(2,128)} %get-tuple-element.493.src_ref, s32[2,192]{1,0:T(2,128)} %get-tuple-element.492.mix_ref, bf16[1920,64,256]{2,1,0:T(8,128)(2,1)} %bitcast.35), custom_call_target="tpu_custom_call" | custom-call | flops 10000000 | bytes 24960000 | tf_op jit(solution)/shard_map/pack/pallas_call | solution.py:164
  62.7 27.6 %pack.27 = (bf16[192,64,256]{2,1,0:T(8,128)(2,1)}, bf16[192,64,256]{2,1,0:T(8,128)(2,1)}) custom-call(s32[2,192]{1,0:T(2,128)} %get-tuple-element.493.src_ref, s32[2,192]{1,0:T(2,128)} %get-tuple-element.492.mix_ref, bf16[1920,64,256]{2,1,0:T(8,128)(2,1)} %bitcast.45), custom_call_target="tpu_custom_call" | custom-call | flops 10000000 | bytes 24960000 | tf_op jit(solution)/shard_map/pack/pallas_call | solution.py:164
  90.3 10.6 %pack.16 = (bf16[64,64,256]{2,1,0:T(8,128)(2,1)}, bf16[64,64,256]{2,1,0:T(8,128)(2,1)}) custom-call(s32[2,64]{1,0:T(2,128)} %fusion.27.src_ref, s32[2,64]{1,0:T(2,128)} %fusion.26.mix_ref, bf16[1920,64,256]{2,1,0:T(8,128)(2,1)} %bitcast.46, bf16[1920,64,256]{2,1,0:T(8,128)(2,1)} %bitcast.36), custom_call_target="tpu_custom_call" | custom-call | flops 10000000 | bytes 8320000 | tf_op jit(solution)/shard_map/pack/pallas_call | solution.py:164
  100.9 6.5 pack.17
  107.4 3.2 pack.23
  110.7 2.5 pack.24
  113.2 2.3 pack.25
  115.5 2.3 pack.26
  117.8 4.6 pack.18
  122.4 3.6 pack.19
  126.0 3.6 pack.20
  130.1 2.5 pack.29
  134.3 5.1 convolution_convert_fusion
  140.2 3.1 convolution_convert_fusion.1
  145.4 3.3 fusion.2
  151.2 96.6 %conditional.1 = (bf16[64,64,256]{2,1,0:T(8,128)(2,1)}, bf16[64,64,256]{2,1,0:T(8,128)(2,1)}, bf16[32,64,256]{2,1,0:T(8,128)(2,1)}, bf16[32,64,256]{2,1,0:T(8,12...) conditional(s32[]{:T(128)} %clamp.30, () %tuple.78, ...), branch_computations={%region_5.6_spmd, %region_6.7_spmd, %region_7.8_spmd, %region_8.9_... | conditional | bytes 33554912 | solution.py:452
  151.2 7.8 %collective-permute-start.24 = (bf16[64,64,256]{2,1,0:T(8,128)(2,1)S(1)}, bf16[64,64,256]{2,1,0:T(8,128)(2,1)}, u32[]{:S(2)}, u32[]{:S(2)}) collective-permute-start(bf16[64,64,256]{2,1,0:T(8,128)(2,1)S(1)} %get-tuple-element.172), channel_id=1, source_target_pairs={{0,2},{1,3},{2,0},{3,1},{4,6},{5,7},{6,4},{7,5}} | collective-permute-start | bytes 6291464 | tf_op jit(solution)/shard_map/cond/branch_8_fun/ppermute | solution.py:359
  159.0 46.5 %collective-permute-done.24 = bf16[64,64,256]{2,1,0:T(8,128)(2,1)} collective-permute-done((bf16[64,64,256]{2,1,0:T(8,128)(2,1)S(1)}, bf16[64,64,256]{2,1,0:T(8,128)(2,1)}, u32[]{:S(2)}, u32[]{:S(2)}) %collective-permute-start.24) | collective-permute-done | bytes 2097184 | tf_op jit(solution)/shard_map/cond/branch_8_fun/ppermute | solution.py:359
  205.6 42.2 %collective-permute-done.25 = bf16[64,64,256]{2,1,0:T(8,128)(2,1)} collective-permute-done((bf16[64,64,256]{2,1,0:T(8,128)(2,1)}, bf16[64,64,256]{2,1,0:T(8,128)(2,1)}, u32[]{:S(2)}, u32[]{:S(2)}) %collective-permute-start.25) | collective-permute-done | bytes 2097184 | tf_op jit(solution)/shard_map/cond/branch_8_fun/ppermute | solution.py:359
  250.8 6.2 collective-permute-done.88.refs_0_
  257.3 5.6 collective-permute-done.89.refs_1_
  263.5 4.9 pack.30
  268.4 2.7 collective-permute-start.90
  274.1 27.0 %collective-permute-done.98.refs_0_ = bf16[16,64,256]{2,1,0:T(8,128)(2,1)} collective-permute-done((bf16[16,64,256]{2,1,0:T(8,128)(2,1)}, bf16[16,64,256]{2,1,0:T(8,128)(2,1)}, u32[]{:S(2)}, u32[]{:S(2)}) %collective-permute-start.98) | collective-permute-done | bytes 524320 | tf_op jit(solution)/shard_map/ppermute | solution.py:359
  301.1 9.7 %collective-permute-done.99.refs_1_ = bf16[16,64,256]{2,1,0:T(8,128)(2,1)} collective-permute-done((bf16[16,64,256]{2,1,0:T(8,128)(2,1)}, bf16[16,64,256]{2,1,0:T(8,128)(2,1)}, u32[]{:S(2)}, u32[]{:S(2)}) %collective-permute-start.99) | collective-permute-done | bytes 524320 | tf_op jit(solution)/shard_map/ppermute | solution.py:359
  312.7 18.5 %collective-permute-done.91.refs_3_ = bf16[24,64,256]{2,1,0:T(8,128)(2,1)} collective-permute-done((bf16[24,64,256]{2,1,0:T(8,128)(2,1)}, bf16[24,64,256]{2,1,0:T(8,128)(2,1)}, u32[]{:S(2)}, u32[]{:S(2)}) %collective-permute-start.91) | collective-permute-done | bytes 786464 | tf_op jit(solution)/shard_map/ppermute | solution.py:359
  331.3 15.4 %pack.31 = (bf16[96,64,256]{2,1,0:T(8,128)(2,1)}, bf16[96,64,256]{2,1,0:T(8,128)(2,1)}) custom-call(s32[2,128]{1,0:T(2,128)} %get-tuple-element.495.src_ref, s32[2,128]{1,0:T(2,128)} %get-tuple-element.494.mix_ref, bf16[1920,64,256]{2,1,0:T(8,128)(2,1)} %bitcast.53), custom_call_target="tpu_custom_call" | custom-call | flops 10000000 | bytes 12480000 | tf_op jit(solution)/shard_map/pack/pallas_call | solution.py:164
  348.9 4.1 collective-permute-done.78.refs_11_
  353.4 64.7 %collective-permute-done.92.refs_4_ = bf16[96,64,256]{2,1,0:T(8,128)(2,1)} collective-permute-done((bf16[96,64,256]{2,1,0:T(8,128)(2,1)}, bf16[96,64,256]{2,1,0:T(8,128)(2,1)}, u32[]{:S(2)}, u32[]{:S(2)}) %collective-permute-start.92) | collective-permute-done | bytes 3145760 | tf_op jit(solution)/shard_map/ppermute | solution.py:359
  421.2 62.3 %collective-permute-done.93.refs_5_ = bf16[96,64,256]{2,1,0:T(8,128)(2,1)} collective-permute-done((bf16[96,64,256]{2,1,0:T(8,128)(2,1)}, bf16[96,64,256]{2,1,0:T(8,128)(2,1)}, u32[]{:S(2)}, u32[]{:S(2)}) %collective-permute-start.93) | collective-permute-done | bytes 3145760 | tf_op jit(solution)/shard_map/ppermute | solution.py:359
  485.0 1.6 collective-permute-start.101
  489.3 28.0 %assemble_keys.2 = (bf16[3,4096,4,256]{3,2,1,0:T(4,128)(2,1)}, f32[4,8,16384]{2,1,0:T(8,128)}) custom-call(s32[1,256]{1,0:T(1,128)} %get-tuple-element.522.code_ref, s32[1,256]{1,0:T(1,128)} %get-tuple-element.523.idx_ref, s32[3]{0:T(128)} %get-tuple-element.513.n_ref, s32[1]{0:T(128)} %bitcast.5.me_ref, ...), custom_call_target="tpu_custom_call", output_to_operand_aliasing={{0}: (15, {}), {1}: (14, {})} | custom-call | flops 10000000 | bytes 64000000 | tf_op jit(solution)/shard_map/assemble_keys/pallas_call | solution.py:330
  517.3 18.8 %assemble_keys.3 = (bf16[3,4096,4,256]{3,2,1,0:T(4,128)(2,1)}, f32[4,8,16384]{2,1,0:T(8,128)}) custom-call(s32[1,256]{1,0:T(1,128)} %get-tuple-element.522.code_ref, s32[1,256]{1,0:T(1,128)} %get-tuple-element.523.idx_ref, s32[3]{0:T(128)} %get-tuple-element.513.n_ref, s32[1]{0:T(128)} %bitcast.5.me_ref, ...), custom_call_target="tpu_custom_call", output_to_operand_aliasing={{0}: (29, {}), {1}: (28, {})} | custom-call | flops 10000000 | bytes 64000000 | tf_op jit(solution)/shard_map/assemble_keys/pallas_call | solution.py:330
  536.1 2.0 reduce_max.19
  538.9 59.0 %collective-permute-done.100.refs_0_ = bf16[32,64,256]{2,1,0:T(8,128)(2,1)} collective-permute-done((bf16[32,64,256]{2,1,0:T(8,128)(2,1)}, bf16[32,64,256]{2,1,0:T(8,128)(2,1)}, u32[]{:S(2)}, u32[]{:S(2)}) %collective-permute-start.100) | collective-permute-done | bytes 1048608 | tf_op jit(solution)/shard_map/ppermute | solution.py:359
  597.9 20.5 %collective-permute-done.101.refs_1_ = bf16[32,64,256]{2,1,0:T(8,128)(2,1)} collective-permute-done((bf16[32,64,256]{2,1,0:T(8,128)(2,1)}, bf16[32,64,256]{2,1,0:T(8,128)(2,1)}, u32[]{:S(2)}, u32[]{:S(2)}) %collective-permute-start.101) | collective-permute-done | bytes 1048608 | tf_op jit(solution)/shard_map/ppermute | solution.py:359
  619.9 1.9 collective-permute-start.95
  624.1 18.6 %assemble_values.7 = (bf16[3,4096,4,256]{3,2,1,0:T(4,128)(2,1)}, f32[4,8,256]{2,1,0:T(8,128)}) custom-call(s32[1,256]{1,0:T(1,128)} %get-tuple-element.522.code_ref, s32[1,256]{1,0:T(1,128)} %get-tuple-element.523.idx_ref, s32[3]{0:T(128)} %get-tuple-element.513.n_ref, s32[1]{0:T(128)} %bitcast.5.me_ref, ...), custom_call_target="tpu_custom_call", output_to_operand_aliasing={{0}: (29, {})} | custom-call | flops 10000000 | bytes 64000000 | tf_op jit(solution)/shard_map/assemble_values/pallas_call | solution.py:330
  642.6 14.9 %assemble_values.8 = (bf16[3,4096,4,256]{3,2,1,0:T(4,128)(2,1)}, f32[4,8,256]{2,1,0:T(8,128)}) custom-call(s32[1,256]{1,0:T(1,128)} %get-tuple-element.522.code_ref, s32[1,256]{1,0:T(1,128)} %get-tuple-element.523.idx_ref, s32[3]{0:T(128)} %get-tuple-element.513.n_ref, s32[1]{0:T(128)} %bitcast.5.me_ref, ...), custom_call_target="tpu_custom_call", output_to_operand_aliasing={{0}: (11, {})} | custom-call | flops 10000000 | bytes 32000000 | tf_op jit(solution)/shard_map/assemble_values/pallas_call | solution.py:330
  657.5 9.0 %assemble_values.9 = (bf16[3,4096,4,256]{3,2,1,0:T(4,128)(2,1)}, f32[4,8,256]{2,1,0:T(8,128)}) custom-call(s32[1,256]{1,0:T(1,128)} %get-tuple-element.522.code_ref, s32[1,256]{1,0:T(1,128)} %get-tuple-element.523.idx_ref, s32[3]{0:T(128)} %get-tuple-element.513.n_ref, s32[1]{0:T(128)} %bitcast.5.me_ref, ...), custom_call_target="tpu_custom_call", output_to_operand_aliasing={{0}: (11, {})} | custom-call | flops 10000000 | bytes 16000000 | tf_op jit(solution)/shard_map/assemble_values/pallas_call | solution.py:330
  666.6 6.1 assemble_values.10
  672.7 4.8 assemble_values.11
  677.5 4.2 assemble_values.12
  681.7 4.2 assemble_values.13
  686.7 5.6 fusion
  (141 shorter events, 37.6 us)
Async XLA Ops:
  133.4 6.8 copy-start.2
  134.2 5.9 copy-start.6
  134.2 5.2 copy-start.7
  134.2 5.2 copy-start.8
  134.3 5.9 copy-start.1
  145.3 4.0 copy-start.3
  145.3 4.6 copy-start.4
  145.3 4.6 copy-start.5
  145.3 5.8 copy-start.9
  145.3 5.8 copy-start.10
  151.2 97.5 %copy-start.11 = (bf16[8,64,256]{2,1,0:T(8,128)(2,1)S(1)}, bf16[8,64,256]{2,1,0:T(8,128)(2,1)}, u32[]{:S(2)}) copy-start(bf16[8,64,256]{2,1,0:T(8,128)(2,1)} %get-tuple-element.417) | copy-start | bytes 786436
  151.2 54.4 %collective-permute-start.24 = (bf16[64,64,256]{2,1,0:T(8,128)(2,1)S(1)}, bf16[64,64,256]{2,1,0:T(8,128)(2,1)}, u32[]{:S(2)}, u32[]{:S(2)}) collective-permute-start(bf16[64,64,256]{2,1,0:T(8,128)(2,1)S(1)} %get-tuple-element.172), channel_id=1, source_target_pairs={{0,2},{1,3},{2,0},{3,1},{4,6},{5,7},{6,4},{7,5}} | collective-permute-start | bytes 6291464 | tf_op jit(solution)/shard_map/cond/branch_8_fun/ppermute | solution.py:359
  159.0 88.7 %collective-permute-start.25 = (bf16[64,64,256]{2,1,0:T(8,128)(2,1)}, bf16[64,64,256]{2,1,0:T(8,128)(2,1)}, u32[]{:S(2)}, u32[]{:S(2)}) collective-permute-start(bf16[64,64,256]{2,1,0:T(8,128)(2,1)} %get-tuple-element.173), channel_id=1, source_target_pairs={{0,3},{1,2},{2,1},{3,0},{4,7},{5,6},{6,5},{7,4}} | collective-permute-start | bytes 6291464 | tf_op jit(solution)/shard_map/cond/branch_8_fun/ppermute | solution.py:359
  247.8 9.2 %collective-permute-start.88 = (bf16[8,64,256]{2,1,0:T(8,128)(2,1)}, bf16[8,64,256]{2,1,0:T(8,128)(2,1)}, u32[]{:S(2)}, u32[]{:S(2)}) collective-permute-start(bf16[8,64,256]{2,1,0:T(8,128)(2,1)} %get-tuple-element.416), channel_id=1, source_target_pairs={{0,2},{1,3},{2,0},{3,1},{4,6},{5,7},{6,4},{7,5}} | collective-permute-start | bytes 786440 | tf_op jit(solution)/shard_map/ppermute | solution.py:359
  248.7 14.2 %collective-permute-start.89 = (bf16[8,64,256]{2,1,0:T(8,128)(2,1)S(1)}, bf16[8,64,256]{2,1,0:T(8,128)(2,1)}, u32[]{:S(2)}, u32[]{:S(2)}) collective-permute-start(bf16[8,64,256]{2,1,0:T(8,128)(2,1)S(1)} %copy-done.11), channel_id=1, source_target_pairs={{0,3},{1,2},{2,1},{3,0},{4,7},{5,6},{6,5},{7,4}} | collective-permute-start | bytes 786440 | tf_op jit(solution)/shard_map/ppermute | solution.py:359
  250.3 234.7 %collective-permute-start.87 = (bf16[192,64,256]{2,1,0:T(8,128)(2,1)}, bf16[192,64,256]{2,1,0:T(8,128)(2,1)}, u32[]{:S(2)}, u32[]{:S(2)}) collective-permute-start(bf16[192,64,256]{2,1,0:T(8,128)(2,1)} %get-tuple-element.412), channel_id=1, source_target_pairs={{0,1},{1,0},{2,3},{3,2},{4,5},{5,4},{6,7},{7,6}} | collective-permute-start | bytes 18874376 | tf_op jit(solution)/shard_map/ppermute | solution.py:359
  250.3 12.6 %collective-permute-start.83 = (bf16[8,64,256]{2,1,0:T(8,128)(2,1)}, bf16[8,64,256]{2,1,0:T(8,128)(2,1)}, u32[]{:S(2)}, u32[]{:S(2)}) collective-permute-start(bf16[8,64,256]{2,1,0:T(8,128)(2,1)} %get-tuple-element.409.refs_7_), channel_id=1, source_target_pairs={{0,1},{1,0},{2,3},{3,2},{4,5},{5,4},{6,7},{7,6}} | collective-permute-start | bytes 786440 | tf_op jit(solution)/shard_map/ppermute | solution.py:359
  250.8 12.6 %collective-permute-start.84 = (bf16[8,64,256]{2,1,0:T(8,128)(2,1)}, bf16[8,64,256]{2,1,0:T(8,128)(2,1)}, u32[]{:S(2)}, u32[]{:S(2)}) collective-permute-start(bf16[8,64,256]{2,1,0:T(8,128)(2,1)} %get-tuple-element.408.refs_6_), channel_id=1, source_target_pairs={{0,1},{1,0},{2,3},{3,2},{4,5},{5,4},{6,7},{7,6}} | collective-permute-start | bytes 786440 | tf_op jit(solution)/shard_map/ppermute | solution.py:359
  257.0 15.3 %collective-permute-start.81 = (bf16[16,64,256]{2,1,0:T(8,128)(2,1)}, bf16[16,64,256]{2,1,0:T(8,128)(2,1)}, u32[]{:S(2)}, u32[]{:S(2)}) collective-permute-start(bf16[16,64,256]{2,1,0:T(8,128)(2,1)} %get-tuple-element.407.refs_5_), channel_id=1, source_target_pairs={{0,1},{1,0},{2,3},{3,2},{4,5},{5,4},{6,7},{7,6}} | collective-permute-start | bytes 1572872 | tf_op jit(solution)/shard_map/ppermute | solution.py:359
  262.9 5.6 collective-permute-start.85
  262.9 8.3 %collective-permute-start.86 = (bf16[8,64,256]{2,1,0:T(8,128)(2,1)}, bf16[8,64,256]{2,1,0:T(8,128)(2,1)}, u32[]{:S(2)}, u32[]{:S(2)}) collective-permute-start(bf16[8,64,256]{2,1,0:T(8,128)(2,1)} %get-tuple-element.410.refs_8_), channel_id=1, source_target_pairs={{0,1},{1,0},{2,3},{3,2},{4,5},{5,4},{6,7},{7,6}} | collective-permute-start | bytes 786440 | tf_op jit(solution)/shard_map/ppermute | solution.py:359
  263.4 8.6 %collective-permute-start.96 = (bf16[8,64,256]{2,1,0:T(8,128)(2,1)}, bf16[8,64,256]{2,1,0:T(8,128)(2,1)}, u32[]{:S(2)}, u32[]{:S(2)}) collective-permute-start(bf16[8,64,256]{2,1,0:T(8,128)(2,1)} %get-tuple-element.429), channel_id=1, source_target_pairs={{0,2},{1,3},{2,0},{3,1},{4,6},{5,7},{6,4},{7,5}} | collective-permute-start | bytes 786440 | tf_op jit(solution)/shard_map/ppermute | solution.py:359
  268.4 42.9 %collective-permute-start.90 = (bf16[24,64,256]{2,1,0:T(8,128)(2,1)}, bf16[24,64,256]{2,1,0:T(8,128)(2,1)}, u32[]{:S(2)}, u32[]{:S(2)}) collective-permute-start(bf16[24,64,256]{2,1,0:T(8,128)(2,1)} %get-tuple-element.418), channel_id=1, source_target_pairs={{0,2},{1,3},{2,0},{3,1},{4,6},{5,7},{6,4},{7,5}} | collective-permute-start | bytes 2359304 | tf_op jit(solution)/shard_map/ppermute | solution.py:359
  271.2 2.3 collective-permute-start.82
  271.9 29.2 %collective-permute-start.98 = (bf16[16,64,256]{2,1,0:T(8,128)(2,1)}, bf16[16,64,256]{2,1,0:T(8,128)(2,1)}, u32[]{:S(2)}, u32[]{:S(2)}) collective-permute-start(bf16[16,64,256]{2,1,0:T(8,128)(2,1)} %get-tuple-element.431), channel_id=1, source_target_pairs={{0,2},{1,3},{2,0},{3,1},{4,6},{5,7},{6,4},{7,5}} | collective-permute-start | bytes 1572872 | tf_op jit(solution)/shard_map/ppermute | solution.py:359
  272.3 38.5 %collective-permute-start.99 = (bf16[16,64,256]{2,1,0:T(8,128)(2,1)}, bf16[16,64,256]{2,1,0:T(8,128)(2,1)}, u32[]{:S(2)}, u32[]{:S(2)}) collective-permute-start(bf16[16,64,256]{2,1,0:T(8,128)(2,1)} %get-tuple-element.432), channel_id=1, source_target_pairs={{0,3},{1,2},{2,1},{3,0},{4,7},{5,6},{6,5},{7,4}} | collective-permute-start | bytes 1572872 | tf_op jit(solution)/shard_map/ppermute | solution.py:359
  273.4 74.7 %collective-permute-start.77 = (bf16[64,64,256]{2,1,0:T(8,128)(2,1)}, bf16[64,64,256]{2,1,0:T(8,128)(2,1)}, u32[]{:S(2)}, u32[]{:S(2)}) collective-permute-start(bf16[64,64,256]{2,1,0:T(8,128)(2,1)} %get-tuple-element.403.refs_1_), channel_id=1, source_target_pairs={{0,1},{1,0},{2,3},{3,2},{4,5},{5,4},{6,7},{7,6}} | collective-permute-start | bytes 6291464 | tf_op jit(solution)/shard_map/ppermute | solution.py:359
  301.1 45.7 %collective-permute-start.79 = (bf16[32,64,256]{2,1,0:T(8,128)(2,1)}, bf16[32,64,256]{2,1,0:T(8,128)(2,1)}, u32[]{:S(2)}, u32[]{:S(2)}) collective-permute-start(bf16[32,64,256]{2,1,0:T(8,128)(2,1)} %get-tuple-element.405.refs_3_), channel_id=1, source_target_pairs={{0,1},{1,0},{2,3},{3,2},{4,5},{5,4},{6,7},{7,6}} | collective-permute-start | bytes 3145736 | tf_op jit(solution)/shard_map/ppermute | solution.py:359
  310.8 311.3 %collective-permute-start.76 = (bf16[192,64,256]{2,1,0:T(8,128)(2,1)}, bf16[192,64,256]{2,1,0:T(8,128)(2,1)}, u32[]{:S(2)}, u32[]{:S(2)}) collective-permute-start(bf16[192,64,256]{2,1,0:T(8,128)(2,1)} %get-tuple-element.399), channel_id=1, source_target_pairs={{0,1},{1,0},{2,3},{3,2},{4,5},{5,4},{6,7},{7,6}} | collective-permute-start | bytes 18874376 | tf_op jit(solution)/shard_map/ppermute | solution.py:359
  311.4 19.9 %collective-permute-start.91 = (bf16[24,64,256]{2,1,0:T(8,128)(2,1)}, bf16[24,64,256]{2,1,0:T(8,128)(2,1)}, u32[]{:S(2)}, u32[]{:S(2)}) collective-permute-start(bf16[24,64,256]{2,1,0:T(8,128)(2,1)} %get-tuple-element.419), channel_id=1, source_target_pairs={{0,3},{1,2},{2,1},{3,0},{4,7},{5,6},{6,5},{7,4}} | collective-permute-start | bytes 2359304 | tf_op jit(solution)/shard_map/ppermute | solution.py:359
  331.2 15.6 %collective-permute-start.80 = (bf16[32,64,256]{2,1,0:T(8,128)(2,1)}, bf16[32,64,256]{2,1,0:T(8,128)(2,1)}, u32[]{:S(2)}, u32[]{:S(2)}) collective-permute-start(bf16[32,64,256]{2,1,0:T(8,128)(2,1)} %get-tuple-element.404.refs_2_), channel_id=1, source_target_pairs={{0,1},{1,0},{2,3},{3,2},{4,5},{5,4},{6,7},{7,6}} | collective-permute-start | bytes 3145736 | tf_op jit(solution)/shard_map/ppermute | solution.py:359
  346.8 71.3 %collective-permute-start.92 = (bf16[96,64,256]{2,1,0:T(8,128)(2,1)}, bf16[96,64,256]{2,1,0:T(8,128)(2,1)}, u32[]{:S(2)}, u32[]{:S(2)}) collective-permute-start(bf16[96,64,256]{2,1,0:T(8,128)(2,1)} %get-tuple-element.420), channel_id=1, source_target_pairs={{0,2},{1,3},{2,0},{3,1},{4,6},{5,7},{6,4},{7,5}} | collective-permute-start | bytes 9437192 | tf_op jit(solution)/shard_map/ppermute | solution.py:359
  346.8 136.7 %collective-permute-start.93 = (bf16[96,64,256]{2,1,0:T(8,128)(2,1)}, bf16[96,64,256]{2,1,0:T(8,128)(2,1)}, u32[]{:S(2)}, u32[]{:S(2)}) collective-permute-start(bf16[96,64,256]{2,1,0:T(8,128)(2,1)} %get-tuple-element.421), channel_id=1, source_target_pairs={{0,3},{1,2},{2,1},{3,0},{4,7},{5,6},{6,5},{7,4}} | collective-permute-start | bytes 9437192 | tf_op jit(solution)/shard_map/ppermute | solution.py:359
  348.1 4.9 collective-permute-start.78
  353.1 266.8 %collective-permute-start.102 = (bf16[64,64,256]{2,1,0:T(8,128)(2,1)}, bf16[64,64,256]{2,1,0:T(8,128)(2,1)}, u32[]{:S(2)}, u32[]{:S(2)}) collective-permute-start(bf16[64,64,256]{2,1,0:T(8,128)(2,1)} %get-tuple-element.435), channel_id=1, source_target_pairs={{0,2},{1,3},{2,0},{3,1},{4,6},{5,7},{6,4},{7,5}} | collective-permute-start | bytes 6291464 | tf_op jit(solution)/shard_map/ppermute | solution.py:359
  418.1 203.7 %collective-permute-start.103 = (bf16[64,64,256]{2,1,0:T(8,128)(2,1)}, bf16[64,64,256]{2,1,0:T(8,128)(2,1)}, u32[]{:S(2)}, u32[]{:S(2)}) collective-permute-start(bf16[64,64,256]{2,1,0:T(8,128)(2,1)} %get-tuple-element.436), channel_id=1, source_target_pairs={{0,3},{1,2},{2,1},{3,0},{4,7},{5,6},{6,5},{7,4}} | collective-permute-start | bytes 6291464 | tf_op jit(solution)/shard_map/ppermute | solution.py:359
  483.5 114.3 %collective-permute-start.100 = (bf16[32,64,256]{2,1,0:T(8,128)(2,1)}, bf16[32,64,256]{2,1,0:T(8,128)(2,1)}, u32[]{:S(2)}, u32[]{:S(2)}) collective-permute-start(bf16[32,64,256]{2,1,0:T(8,128)(2,1)} %get-tuple-element.433), channel_id=1, source_target_pairs={{0,2},{1,3},{2,0},{3,1},{4,6},{5,7},{6,4},{7,5}} | collective-permute-start | bytes 3145736 | tf_op jit(solution)/shard_map/ppermute | solution.py:359
  485.0 133.3 %collective-permute-start.101 = (bf16[32,64,256]{2,1,0:T(8,128)(2,1)}, bf16[32,64,256]{2,1,0:T(8,128)(2,1)}, u32[]{:S(2)}, u32[]{:S(2)}) collective-permute-start(bf16[32,64,256]{2,1,0:T(8,128)(2,1)} %get-tuple-element.434), channel_id=1, source_target_pairs={{0,3},{1,2},{2,1},{3,0},{4,7},{5,6},{6,5},{7,4}} | collective-permute-start | bytes 3145736 | tf_op jit(solution)/shard_map/ppermute | solution.py:359
  536.1 2.2 copy-start
  597.8 74.8 %collective-permute-start.97 = (bf16[8,64,256]{2,1,0:T(8,128)(2,1)}, bf16[8,64,256]{2,1,0:T(8,128)(2,1)}, u32[]{:S(2)}, u32[]{:S(2)}) collective-permute-start(bf16[8,64,256]{2,1,0:T(8,128)(2,1)} %get-tuple-element.430), channel_id=1, source_target_pairs={{0,3},{1,2},{2,1},{3,0},{4,7},{5,6},{6,5},{7,4}} | collective-permute-start | bytes 786440 | tf_op jit(solution)/shard_map/ppermute | solution.py:359
  618.4 59.1 %collective-permute-start.94 = (bf16[4,64,256]{2,1,0:T(8,128)(2,1)}, bf16[4,64,256]{2,1,0:T(8,128)(2,1)}, u32[]{:S(2)}, u32[]{:S(2)}) collective-permute-start(bf16[4,64,256]{2,1,0:T(8,128)(2,1)} %get-tuple-element.427), channel_id=1, source_target_pairs={{0,2},{1,3},{2,0},{3,1},{4,6},{5,7},{6,4},{7,5}} | collective-permute-start | bytes 393224 | tf_op jit(solution)/shard_map/ppermute | solution.py:359
  619.9 57.6 %collective-permute-start.95 = (bf16[4,64,256]{2,1,0:T(8,128)(2,1)}, bf16[4,64,256]{2,1,0:T(8,128)(2,1)}, u32[]{:S(2)}, u32[]{:S(2)}) collective-permute-start(bf16[4,64,256]{2,1,0:T(8,128)(2,1)} %get-tuple-element.428), channel_id=1, source_target_pairs={{0,3},{1,2},{2,1},{3,0},{4,7},{5,6},{6,5},{7,4}} | collective-permute-start | bytes 393224 | tf_op jit(solution)/shard_map/ppermute | solution.py:359
  621.8 59.9 %collective-permute-start.74 = (bf16[4,64,256]{2,1,0:T(8,128)(2,1)}, bf16[4,64,256]{2,1,0:T(8,128)(2,1)}, u32[]{:S(2)}, u32[]{:S(2)}) collective-permute-start(bf16[4,64,256]{2,1,0:T(8,128)(2,1)} %get-tuple-element.397), channel_id=1, source_target_pairs={{0,2},{1,3},{2,0},{3,1},{4,6},{5,7},{6,4},{7,5}} | collective-permute-start | bytes 393224 | tf_op jit(solution)/shard_map/ppermute | solution.py:359
  622.1 59.7 %collective-permute-start.75 = (bf16[4,64,256]{2,1,0:T(8,128)(2,1)}, bf16[4,64,256]{2,1,0:T(8,128)(2,1)}, u32[]{:S(2)}, u32[]{:S(2)}) collective-permute-start(bf16[4,64,256]{2,1,0:T(8,128)(2,1)} %get-tuple-element.398), channel_id=1, source_target_pairs={{0,3},{1,2},{2,1},{3,0},{4,7},{5,6},{6,5},{7,4}} | collective-permute-start | bytes 393224 | tf_op jit(solution)/shard_map/ppermute | solution.py:359
where the time goes:
time: 705 us; the launch traced here: 692 us
  waiting for transfers between devices  368 us (52%)
  Pallas kernels  243 us (34%)
  starting transfers between devices  27.6 us (4%)
  matrix products  17.1 us (2%)
  other arithmetic  15.5 us (2%)
  local copies, waits for them, and re-layouts  8.5 us (1%)
  between operations  8.09 us (1%)
    ppermute x32, waiting for transfers between devices, send(): return lax.ppermute(x, 'sh', [(i, i ^ d) for i in range(WAYS)])  368 us
    pallas_call x16, Pallas kernels, pack(): pl.pallas_call(functools.partial(pack_kernel, base, size, steps), grid_sp...  134 us
    pallas_call x9, Pallas kernels, assemble(): pl.pallas_call(functools.partial(assemble_kernel, is_key, base, size, ste...  109 us
    ppermute x32, starting transfers between devices, send(): return lax.ppermute(x, 'sh', [(i, i ^ d) for i in range(WAYS)])  27.6 us
  transfers between devices with their start and end apart: 32, of which 14 were waited for; matrix products, arithmetic and copies ran while one was open for 1% of the time, Pallas kernels for 18%

commit v1 on v0

--- a/solution.py
+++ b/solution.py
@@ -112,29 +112,57 @@
         return src, jnp.where(g == cut // GRAN, (mixed + 1) * GRAN + cut % GRAN, -1)
 
 
-def pack_kernel(base, size, steps, src_ref, mix_ref, *refs):
-    prefills, outs, (older, sem) = refs[:-4], refs[-4:-2], refs[-2:]
+def pack_kernel(base, size, steps, source, *refs):
+    num = source.num_scalars
+    scalars, refs = refs[:num], refs[num:]
+    prefills, outs, (buf, older, sems) = refs[:-5], refs[-5:-3], refs[-3:]
+    at = source.reader(*scalars)
     i = pl.program_id(0)
+    total = steps * len(prefills)
+    slots = buf.shape[0]
+    slot = lax.rem(i, slots)
+
+    def by_tensor(step, do):
+        for k, ref in enumerate(prefills):
+            pl.when((step >= k * steps) & (step < (k + 1) * steps))(functools.partial(do, ref))
+
+    def fetch(step):
+        first = base + lax.rem(step, steps) * size
+        to = lax.rem(step, slots)
+
+        def from_ref(ref):
+            def one(t, carry):
+                for a in range(2):
+                    pltpu.make_async_copy(ref.at[at(a, first + t)[0]], buf.at[to, a, t], sems.at[0, to]).start()
+                return carry
+
+            lax.fori_loop(0, size, one, 0)
+
+        by_tensor(step, from_ref)
+
+    def stores(step):
+        to = lax.rem(step, slots)
+        return [pltpu.make_async_copy(buf.at[to, a], outs[a].at[pl.ds(step * size, size)], sems.at[1, to]) for a in range(2)]
+
+    @pl.when(i == 0)
+    def _():
+        fetch(i)
+
+    if total > 1:
+        @pl.when(i + 1 < total)
+        def _():
+            if total > slots:
+                @pl.when(i + 1 >= slots)
+                def _():
+                    for copy in stores(i + 1 - slots):
+                        copy.wait()
+            fetch(i + 1)
+
+    pltpu.make_async_copy(buf.at[slot], buf.at[slot], sems.at[0, slot]).wait()
     first = base + lax.rem(i, steps) * size
-
-    def by_tensor(do):
-        for k, ref in enumerate(prefills):
-            pl.when((i >= k * steps) & (i < (k + 1) * steps))(functools.partial(do, ref))
-
-    def fetch(ref, act):
-        def one(t, carry):
-            for a in range(2):
-                act(pltpu.make_async_copy(ref.at[src_ref[a, first + t]], outs[a].at[t], sem))
-            return carry
-
-        lax.fori_loop(0, size, one, 0)
-
-    by_tensor(lambda ref: fetch(ref, lambda copy: copy.start()))
-    fetch(prefills[0], lambda copy: copy.wait())
-
     for a in range(2):
         def patch(t, carry):
-            code = mix_ref[a, first + t]
+            code = at(a, first + t)[1]
 
             @pl.when(code >= 0)
             def _():
@@ -142,39 +170,88 @@
 
                 @pl.when(granule >= 0)
                 def _():
-                    by_tensor(lambda ref: pltpu.make_async_copy(ref.at[granule], older, sem).start())
-                    pltpu.make_async_copy(prefills[0].at[0], older, sem).wait()
+                    by_tensor(i, lambda ref: pltpu.make_async_copy(ref.at[granule], older, sems.at[0, slot]).start())
+                    pltpu.make_async_copy(older, older, sems.at[0, slot]).wait()
 
                 @pl.when(granule < 0)
                 def _():
                     older[...] = jnp.zeros_like(older)
 
                 newer = lax.broadcasted_iota(jnp.int32, (GRAN, 256), 0) < lax.rem(code, GRAN)
-                outs[a][t] = jnp.where(newer, outs[a][t].astype(jnp.float32), older[...].astype(jnp.float32)).astype(jnp.bfloat16)
+                buf[slot, a, t] = jnp.where(newer, buf[slot, a, t].astype(jnp.float32), older[...].astype(jnp.float32)).astype(jnp.bfloat16)
 
             return carry
 
         lax.fori_loop(0, size, patch, 0)
-
-
-def pack(prefills, src, mix, base, count):
+    for copy in stores(i):
+        copy.start()
+
+    @pl.when(i == total - 1)
+    def _():
+        for back in range(min(slots, total)):
+            for copy in stores(i - back):
+                copy.wait()
+
+
+class FromTable:
+    num_scalars = 2
+
+    def __init__(self, src, mix):
+        self.scalars = (src, mix)
+
+    def reader(self, src_ref, mix_ref):
+        return lambda a, i: (src_ref[a, i], mix_ref[a, i])
+
+
+class FromLengths:
+    num_scalars = 1
+
+    def __init__(self, lengths, seq_g):
+        self.scalars = (lengths,)
+        self.seq_g = seq_g
+
+    def reader(self, n_ref):
+        me = lax.axis_index('sh').astype(jnp.int32)
+
+        def at(a, i):
+            row0 = (me ^ (2 + a)) * ROWS
+            n = [n_ref[row0 + r] for r in range(ROWS)]
+            ends, end = [], 0
+            for x in n:
+                end = end + jnp.minimum(x // GRAN + 1, WIN_G)
+                ends.append(end)
+            r = jnp.where(i >= ends[0], 1, 0) + jnp.where(i >= ends[1], 1, 0)
+            g = i - jnp.where(r == 0, 0, jnp.where(r == 1, ends[0], ends[1]))
+            length = jnp.where(r == 0, n[0], jnp.where(r == 1, n[1], n[2]))
+            lap, cut = length // WINDOW, lax.rem(length, WINDOW)
+            older = jnp.maximum(lap - 1, 0)
+            first = (row0 + r) * self.seq_g
+            src = first + jnp.minimum(jnp.where(g <= cut // GRAN, lap, older) * WIN_G + g, self.seq_g - 1)
+            mixed = jnp.where(lap >= 1, first + older * WIN_G + g, -1)
+            valid = i < ends[2]
+            return jnp.where(valid, src, 0), jnp.where(valid & (g == cut // GRAN), (mixed + 1) * GRAN + lax.rem(cut, GRAN), -1)
+
+        return at
+
+
+def pack(prefills, source, base, count):
     size = next(x for x in (16, 8, 4) if count % x == 0)
     steps = count // size
     total = count * len(prefills)
     return pl.pallas_call(
-        functools.partial(pack_kernel, base, size, steps),
+        functools.partial(pack_kernel, base, size, steps, source),
         grid_spec=pltpu.PrefetchScalarGridSpec(
-            num_scalar_prefetch=2,
+            num_scalar_prefetch=source.num_scalars,
             grid=(steps * len(prefills),),
             in_specs=[ANYWHERE] * len(prefills),
-            out_specs=[pl.BlockSpec((size, GRAN, 256), lambda i, src_ref, mix_ref: (i, 0, 0))] * 2,
-            scratch_shapes=[pltpu.VMEM((GRAN, 256), jnp.bfloat16), pltpu.SemaphoreType.DMA],
+            out_specs=[ANYWHERE] * 2,
+            scratch_shapes=[pltpu.VMEM((3, 2, size, GRAN, 256), jnp.bfloat16), pltpu.VMEM((GRAN, 256), jnp.bfloat16), pltpu.SemaphoreType.DMA((2, 3))],
         ),
         out_shape=[jax.ShapeDtypeStruct((total, GRAN, 256), jnp.bfloat16)] * 2,
         compiler_params=pltpu.CompilerParams(dimension_semantics=("arbitrary",), vmem_limit_bytes=VMEM_LIMIT),
         cost_estimate=pl.CostEstimate(flops=10_000_000, bytes_accessed=total * 130_000, transcendentals=0),
         name="pack",
-    )(src, mix, *prefills)
+    )(*source.scalars, *prefills)
 
 
 def assemble_kernel(is_key, base, size, steps, segments, code_ref, idx_ref, n_ref, me_ref, *refs):
@@ -191,19 +268,19 @@
     def active_at(step):
         return functools.reduce(jnp.maximum, [code_at(step, t) for t in range(size)]) >= 0
 
-    def reads(step, buf, act):
+    def read(step, buf):
         @pl.when(active_at(step))
         def _():
             for begin, end, entry, offset, count, place in segments:
                 @pl.when((step >= begin) & (step < end))
                 def _():
                     for d in range(2):
-                        act(pltpu.make_async_copy(far_refs[2 * entry + d].at[pl.ds(offset + (step - begin) * size, count)], xb.at[buf, me ^ (2 + d), pl.ds(place, count)], sems.at[0, buf]))
+                        pltpu.make_async_copy(far_refs[2 * entry + d].at[pl.ds(offset + (step - begin) * size, count)], xb.at[buf, me ^ (2 + d), pl.ds(place, count)], sems.at[0, buf]).start()
 
             def one(t, carry):
                 at = idx_ref[0, base + step * size + t]
-                act(pltpu.make_async_copy(near_ref.at[at], xb.at[buf, me ^ 1, t], sems.at[0, buf]))
-                act(pltpu.make_async_copy(own_ref.at[at], xb.at[buf, me, t], sems.at[0, buf]))
+                pltpu.make_async_copy(near_ref.at[at], xb.at[buf, me ^ 1, t], sems.at[0, buf]).start()
+                pltpu.make_async_copy(own_ref.at[at], xb.at[buf, me, t], sems.at[0, buf]).start()
                 return carry
 
             lax.fori_loop(0, size, one, 0)
@@ -224,25 +301,26 @@
 
     @pl.when(i == 0)
     def _():
-        reads(i, slot, lambda copy: copy.start())
+        read(i, slot)
         if not is_key:
             acc[...] = prev_ref[...]
 
     if steps > 1:
         @pl.when(i + 1 < steps)
         def _():
-            reads(i + 1, 1 - slot, lambda copy: copy.start())
+            read(i + 1, 1 - slot)
 
     if steps > 2:
         @pl.when(i >= 2)
         def _():
             written(i - 2, slot)
 
-    reads(i, slot, lambda copy: copy.wait())
     active = active_at(i)
 
     @pl.when(active)
     def _():
+        pltpu.make_async_copy(xb.at[slot], xb.at[slot], sems.at[0, slot]).wait()
+
         def one(t, carry):
             code = code_at(i, t)
 
@@ -409,20 +487,21 @@
         codes = jnp.concatenate([p[0] for p in parts], axis=1)
         places = jnp.concatenate([p[1] for p in parts], axis=1)
 
+        fixed_from, close_from, spare_from = FromTable(fixed_src, fixed_mix), FromTable(close_src, close_mix), FromTable(spare_src, spare_mix)
         fixed_got = {True: [], False: []}
         packed_values = []
-        for base, count in zip(starts_of(K_PIECES), K_PIECES):
-            out = pack([prefill[True]], fixed_src, fixed_mix, base, count)
+        for i, (base, count) in enumerate(zip(starts_of(K_PIECES), K_PIECES)):
+            out = pack([prefill[True]], FromLengths(lengths, seq_g) if i == 0 else fixed_from, base, count)
             a = send(out[0], 2)
             b = send(out[1], 3)
             fixed_got[True].append((a, b))
         close_got = {}
         for is_key in (True, False):
-            near, own = pack([prefill[is_key]], close_src, close_mix, 0, ROWS * WIN_G)
+            near, own = pack([prefill[is_key]], close_from, 0, ROWS * WIN_G)
             close_got[is_key] = (send(near, 1), own)
-        spare_packed = [pack([prefill[True], prefill[False]], spare_src, spare_mix, base, count) for base, count in zip(starts_of(UNITS), UNITS)]
+        spare_packed = [pack([prefill[True], prefill[False]], spare_from, base, count) for base, count in zip(starts_of(UNITS), UNITS)]
         for base, count in zip(starts_of(V_PIECES), V_PIECES):
-            packed_values.append(pack([prefill[False]], fixed_src, fixed_mix, base, count))
+            packed_values.append(pack([prefill[False]], fixed_from, base, count))
 
         resid_f32 = residual.astype(jnp.float32)
         inv_rms = lax.rsqrt(jnp.mean(resid_f32 * resid_f32, axis=-1, keepdims=True) + EPS)

time: 705 us -> 667 us (0.946)
  Pallas kernels: 243 us -> 205 us
    pallas_call x16, Pallas kernels: 134 us -> 98.5 us  [pack(): pl.pallas_call(functools.partial(pack_kernel, base, size, steps, source),...]
  transfers between devices with their start and end apart: 32 -> 32, of which waited for: 14 -> 13; matrix products, arithmetic and copies ran while one was open for 1% -> 1% of each run, Pallas kernels for 18% -> 18%
where the time goes in v1:
time: 667 us; the launch traced here: 658 us
  waiting for transfers between devices  372 us (56%)
  Pallas kernels  205 us (31%)
  starting transfers between devices  26.6 us (4%)
  matrix products  17.1 us (3%)
  other arithmetic  15.5 us (2%)
  local copies, waits for them, and re-layouts  8.5 us (1%)
  between operations  8.1 us (1%)
    ppermute x32, waiting for transfers between devices, send(): return lax.ppermute(x, 'sh', [(i, i ^ d) for i in range(WAYS)])  372 us
    pallas_call x9, Pallas kernels, assemble(): pl.pallas_call(functools.partial(assemble_kernel, is_key, base, size, ste...  106 us
    pallas_call x16, Pallas kernels, pack(): pl.pallas_call(functools.partial(pack_kernel, base, size, steps, source),...  98.5 us
    ppermute x32, starting transfers between devices, send(): return lax.ppermute(x, 'sh', [(i, i ^ d) for i in range(WAYS)])  26.6 us
  transfers between devices with their start and end apart: 32, of which 13 were waited for; matrix products, arithmetic and copies ran while one was open for 1% of the time, Pallas kernels for 18%

profile of v1, /device:TPU:6, one launch (start us, length us, event | category | flops | bytes accessed | tf_op | source)
XLA Modules:
  0.0 657.9 jit_solution(6341043884122776492)
XLA Ops:
  3.0 4.9 pmax.7
  16.7 7.4 %pack.21 = (bf16[64,64,256]{2,1,0:T(8,128)(2,1)}, bf16[64,64,256]{2,1,0:T(8,128)(2,1)}) custom-call(s32[2,128]{1,0:T(2,128)} %get-tuple-element.495.refs_0_, s32[2,128]{1,0:T(2,128)} %get-tuple-element.494.refs_1_, bf16[1920,64,256]{2,1,0:T(8,128)(2,1)} %bitcast.33), custom_call_target="tpu_custom_call" | custom-call | flops 10000000 | bytes 8320000 | tf_op jit(solution)/shard_map/pack/pallas_call | solution.py:241
  24.2 4.8 pack.22
  30.9 16.3 %pack.28 = (bf16[192,64,256]{2,1,0:T(8,128)(2,1)}, bf16[192,64,256]{2,1,0:T(8,128)(2,1)}) custom-call(s32[2,192]{1,0:T(2,128)} %get-tuple-element.493.refs_0_, s32[2,192]{1,0:T(2,128)} %get-tuple-element.492.refs_1_, bf16[1920,64,256]{2,1,0:T(8,128)(2,1)} %bitcast.35), custom_call_target="tpu_custom_call" | custom-call | flops 10000000 | bytes 24960000 | tf_op jit(solution)/shard_map/pack/pallas_call | solution.py:241
  47.1 18.3 %pack.27 = (bf16[192,64,256]{2,1,0:T(8,128)(2,1)}, bf16[192,64,256]{2,1,0:T(8,128)(2,1)}) custom-call(s32[2,192]{1,0:T(2,128)} %get-tuple-element.493.refs_0_, s32[2,192]{1,0:T(2,128)} %get-tuple-element.492.refs_1_, bf16[1920,64,256]{2,1,0:T(8,128)(2,1)} %bitcast.45), custom_call_target="tpu_custom_call" | custom-call | flops 10000000 | bytes 24960000 | tf_op jit(solution)/shard_map/pack/pallas_call | solution.py:241
  65.5 8.1 %pack.16 = (bf16[64,64,256]{2,1,0:T(8,128)(2,1)}, bf16[64,64,256]{2,1,0:T(8,128)(2,1)}) custom-call(s32[2,64]{1,0:T(2,128)} %fusion.27.refs_0_, s32[2,64]{1,0:T(2,128)} %fusion.26.refs_1_, bf16[1920,64,256]{2,1,0:T(8,128)(2,1)} %bitcast.46, bf16[1920,64,256]{2,1,0:T(8,128)(2,1)} %bitcast.36), custom_call_target="tpu_custom_call" | custom-call | flops 10000000 | bytes 8320000 | tf_op jit(solution)/shard_map/pack/pallas_call | solution.py:241
  73.6 6.1 pack.17
  79.7 2.9 pack.23
  82.6 2.6 pack.24
  85.2 2.3 pack.25
  87.6 2.3 pack.26
  89.9 4.0 pack.18
  93.9 3.0 pack.19
  96.9 3.0 pack.20
  100.4 2.9 pack.29
  105.0 5.1 convolution_convert_fusion
  110.9 3.1 convolution_convert_fusion.1
  116.0 3.3 fusion.2
  121.8 97.5 %conditional.1 = (bf16[64,64,256]{2,1,0:T(8,128)(2,1)}, bf16[64,64,256]{2,1,0:T(8,128)(2,1)}, bf16[32,64,256]{2,1,0:T(8,128)(2,1)}, bf16[32,64,256]{2,1,0:T(8,12...) conditional(s32[]{:T(128)} %clamp.30, () %tuple.78, ...), branch_computations={%region_5.6_spmd, %region_6.7_spmd, %region_7.8_spmd, %region_8.9_... | conditional | bytes 33554912 | solution.py:531
  121.9 8.2 %collective-permute-start.24 = (bf16[64,64,256]{2,1,0:T(8,128)(2,1)S(1)}, bf16[64,64,256]{2,1,0:T(8,128)(2,1)}, u32[]{:S(2)}, u32[]{:S(2)}) collective-permute-start(bf16[64,64,256]{2,1,0:T(8,128)(2,1)S(1)} %get-tuple-element.172), channel_id=1, source_target_pairs={{0,2},{1,3},{2,0},{3,1},{4,6},{5,7},{6,4},{7,5}} | collective-permute-start | bytes 6291464 | tf_op jit(solution)/shard_map/cond/branch_8_fun/ppermute | solution.py:437
  130.1 46.6 %collective-permute-done.24 = bf16[64,64,256]{2,1,0:T(8,128)(2,1)} collective-permute-done((bf16[64,64,256]{2,1,0:T(8,128)(2,1)S(1)}, bf16[64,64,256]{2,1,0:T(8,128)(2,1)}, u32[]{:S(2)}, u32[]{:S(2)}) %collective-permute-start.24) | collective-permute-done | bytes 2097184 | tf_op jit(solution)/shard_map/cond/branch_8_fun/ppermute | solution.py:437
  176.6 42.7 %collective-permute-done.25 = bf16[64,64,256]{2,1,0:T(8,128)(2,1)} collective-permute-done((bf16[64,64,256]{2,1,0:T(8,128)(2,1)}, bf16[64,64,256]{2,1,0:T(8,128)(2,1)}, u32[]{:S(2)}, u32[]{:S(2)}) %collective-permute-start.25) | collective-permute-done | bytes 2097184 | tf_op jit(solution)/shard_map/cond/branch_8_fun/ppermute | solution.py:437
  222.2 6.7 %collective-permute-done.88.refs_0_ = bf16[8,64,256]{2,1,0:T(8,128)(2,1)} collective-permute-done((bf16[8,64,256]{2,1,0:T(8,128)(2,1)}, bf16[8,64,256]{2,1,0:T(8,128)(2,1)}, u32[]{:S(2)}, u32[]{:S(2)}) %collective-permute-start.88) | collective-permute-done | bytes 262176 | tf_op jit(solution)/shard_map/ppermute | solution.py:437
  228.9 5.5 collective-permute-done.89.refs_1_
  234.9 3.9 pack.30
  238.9 2.8 collective-permute-start.90
  241.7 2.5 collective-permute-done.96.refs_0_
  244.3 2.1 collective-permute-start.77
  246.4 25.9 %collective-permute-done.98.refs_0_ = bf16[16,64,256]{2,1,0:T(8,128)(2,1)} collective-permute-done((bf16[16,64,256]{2,1,0:T(8,128)(2,1)}, bf16[16,64,256]{2,1,0:T(8,128)(2,1)}, u32[]{:S(2)}, u32[]{:S(2)}) %collective-permute-start.98) | collective-permute-done | bytes 524320 | tf_op jit(solution)/shard_map/ppermute | solution.py:437
  272.4 9.8 %collective-permute-done.99.refs_1_ = bf16[16,64,256]{2,1,0:T(8,128)(2,1)} collective-permute-done((bf16[16,64,256]{2,1,0:T(8,128)(2,1)}, bf16[16,64,256]{2,1,0:T(8,128)(2,1)}, u32[]{:S(2)}, u32[]{:S(2)}) %collective-permute-start.99) | collective-permute-done | bytes 524320 | tf_op jit(solution)/shard_map/ppermute | solution.py:437
  283.4 19.3 %collective-permute-done.91.refs_3_ = bf16[24,64,256]{2,1,0:T(8,128)(2,1)} collective-permute-done((bf16[24,64,256]{2,1,0:T(8,128)(2,1)}, bf16[24,64,256]{2,1,0:T(8,128)(2,1)}, u32[]{:S(2)}, u32[]{:S(2)}) %collective-permute-start.91) | collective-permute-done | bytes 786464 | tf_op jit(solution)/shard_map/ppermute | solution.py:437
  302.8 10.5 %pack.31 = (bf16[96,64,256]{2,1,0:T(8,128)(2,1)}, bf16[96,64,256]{2,1,0:T(8,128)(2,1)}) custom-call(s32[2,128]{1,0:T(2,128)} %get-tuple-element.495.refs_0_, s32[2,128]{1,0:T(2,128)} %get-tuple-element.494.refs_1_, bf16[1920,64,256]{2,1,0:T(8,128)(2,1)} %bitcast.53), custom_call_target="tpu_custom_call" | custom-call | flops 10000000 | bytes 12480000 | tf_op jit(solution)/shard_map/pack/pallas_call | solution.py:241
  315.5 4.1 collective-permute-done.78.refs_11_
  319.9 64.7 %collective-permute-done.92.refs_4_ = bf16[96,64,256]{2,1,0:T(8,128)(2,1)} collective-permute-done((bf16[96,64,256]{2,1,0:T(8,128)(2,1)}, bf16[96,64,256]{2,1,0:T(8,128)(2,1)}, u32[]{:S(2)}, u32[]{:S(2)}) %collective-permute-start.92) | collective-permute-done | bytes 3145760 | tf_op jit(solution)/shard_map/ppermute | solution.py:437
  387.8 62.6 %collective-permute-done.93.refs_5_ = bf16[96,64,256]{2,1,0:T(8,128)(2,1)} collective-permute-done((bf16[96,64,256]{2,1,0:T(8,128)(2,1)}, bf16[96,64,256]{2,1,0:T(8,128)(2,1)}, u32[]{:S(2)}, u32[]{:S(2)}) %collective-permute-start.93) | collective-permute-done | bytes 3145760 | tf_op jit(solution)/shard_map/ppermute | solution.py:437
  455.8 27.1 %assemble_keys.2 = (bf16[3,4096,4,256]{3,2,1,0:T(4,128)(2,1)}, f32[4,8,16384]{2,1,0:T(8,128)}) custom-call(s32[1,256]{1,0:T(1,128)} %get-tuple-element.522.code_ref, s32[1,256]{1,0:T(1,128)} %get-tuple-element.523.idx_ref, s32[3]{0:T(128)} %get-tuple-element.513.n_ref, s32[1]{0:T(128)} %bitcast.5.me_ref, ...), custom_call_target="tpu_custom_call", output_to_operand_aliasing={{0}: (15, {}), {1}: (14, {})} | custom-call | flops 10000000 | bytes 64000000 | tf_op jit(solution)/shard_map/assemble_keys/pallas_call | solution.py:408
  482.9 18.4 %assemble_keys.3 = (bf16[3,4096,4,256]{3,2,1,0:T(4,128)(2,1)}, f32[4,8,16384]{2,1,0:T(8,128)}) custom-call(s32[1,256]{1,0:T(1,128)} %get-tuple-element.522.code_ref, s32[1,256]{1,0:T(1,128)} %get-tuple-element.523.idx_ref, s32[3]{0:T(128)} %get-tuple-element.513.n_ref, s32[1]{0:T(128)} %bitcast.5.me_ref, ...), custom_call_target="tpu_custom_call", output_to_operand_aliasing={{0}: (29, {}), {1}: (28, {})} | custom-call | flops 10000000 | bytes 64000000 | tf_op jit(solution)/shard_map/assemble_keys/pallas_call | solution.py:408
  501.3 2.0 reduce_max.19
  504.0 60.4 %collective-permute-done.100.refs_0_ = bf16[32,64,256]{2,1,0:T(8,128)(2,1)} collective-permute-done((bf16[32,64,256]{2,1,0:T(8,128)(2,1)}, bf16[32,64,256]{2,1,0:T(8,128)(2,1)}, u32[]{:S(2)}, u32[]{:S(2)}) %collective-permute-start.100) | collective-permute-done | bytes 1048608 | tf_op jit(solution)/shard_map/ppermute | solution.py:437
  564.4 20.8 %collective-permute-done.101.refs_1_ = bf16[32,64,256]{2,1,0:T(8,128)(2,1)} collective-permute-done((bf16[32,64,256]{2,1,0:T(8,128)(2,1)}, bf16[32,64,256]{2,1,0:T(8,128)(2,1)}, u32[]{:S(2)}, u32[]{:S(2)}) %collective-permute-start.101) | collective-permute-done | bytes 1048608 | tf_op jit(solution)/shard_map/ppermute | solution.py:437
  590.7 18.1 %assemble_values.7 = (bf16[3,4096,4,256]{3,2,1,0:T(4,128)(2,1)}, f32[4,8,256]{2,1,0:T(8,128)}) custom-call(s32[1,256]{1,0:T(1,128)} %get-tuple-element.522.code_ref, s32[1,256]{1,0:T(1,128)} %get-tuple-element.523.idx_ref, s32[3]{0:T(128)} %get-tuple-element.513.n_ref, s32[1]{0:T(128)} %bitcast.5.me_ref, ...), custom_call_target="tpu_custom_call", output_to_operand_aliasing={{0}: (29, {})} | custom-call | flops 10000000 | bytes 64000000 | tf_op jit(solution)/shard_map/assemble_values/pallas_call | solution.py:408
  608.8 14.4 %assemble_values.8 = (bf16[3,4096,4,256]{3,2,1,0:T(4,128)(2,1)}, f32[4,8,256]{2,1,0:T(8,128)}) custom-call(s32[1,256]{1,0:T(1,128)} %get-tuple-element.522.code_ref, s32[1,256]{1,0:T(1,128)} %get-tuple-element.523.idx_ref, s32[3]{0:T(128)} %get-tuple-element.513.n_ref, s32[1]{0:T(128)} %bitcast.5.me_ref, ...), custom_call_target="tpu_custom_call", output_to_operand_aliasing={{0}: (11, {})} | custom-call | flops 10000000 | bytes 32000000 | tf_op jit(solution)/shard_map/assemble_values/pallas_call | solution.py:408
  623.3 8.9 %assemble_values.9 = (bf16[3,4096,4,256]{3,2,1,0:T(4,128)(2,1)}, f32[4,8,256]{2,1,0:T(8,128)}) custom-call(s32[1,256]{1,0:T(1,128)} %get-tuple-element.522.code_ref, s32[1,256]{1,0:T(1,128)} %get-tuple-element.523.idx_ref, s32[3]{0:T(128)} %get-tuple-element.513.n_ref, s32[1]{0:T(128)} %bitcast.5.me_ref, ...), custom_call_target="tpu_custom_call", output_to_operand_aliasing={{0}: (11, {})} | custom-call | flops 10000000 | bytes 16000000 | tf_op jit(solution)/shard_map/assemble_values/pallas_call | solution.py:408
  632.1 6.0 assemble_values.10
  638.2 4.8 assemble_values.11
  643.0 4.2 assemble_values.12
  647.2 4.2 assemble_values.13
  652.3 5.6 fusion
  (141 shorter events, 36.3 us)
Async XLA Ops:
  104.0 6.8 %copy-start.2 = (f32[2304]{0:T(1024)}, f32[2304]{0:T(1024)S(1)}, u32[]{:S(2)}) copy-start(f32[2304]{0:T(1024)S(1)} %convert_element_type.450) | copy-start | bytes 27652
  104.9 5.9 copy-start.6
  104.9 5.2 copy-start.7
  104.9 5.2 copy-start.8
  104.9 5.9 copy-start.1
  116.0 4.0 copy-start.3
  116.0 4.6 copy-start.4
  116.0 4.6 copy-start.5
  116.0 5.8 copy-start.9
  116.0 5.8 copy-start.10
  121.8 98.2 %copy-start.11 = (bf16[8,64,256]{2,1,0:T(8,128)(2,1)S(1)}, bf16[8,64,256]{2,1,0:T(8,128)(2,1)}, u32[]{:S(2)}) copy-start(bf16[8,64,256]{2,1,0:T(8,128)(2,1)} %get-tuple-element.417) | copy-start | bytes 786436
  121.9 54.8 %collective-permute-start.24 = (bf16[64,64,256]{2,1,0:T(8,128)(2,1)S(1)}, bf16[64,64,256]{2,1,0:T(8,128)(2,1)}, u32[]{:S(2)}, u32[]{:S(2)}) collective-permute-start(bf16[64,64,256]{2,1,0:T(8,128)(2,1)S(1)} %get-tuple-element.172), channel_id=1, source_target_pairs={{0,2},{1,3},{2,0},{3,1},{4,6},{5,7},{6,4},{7,5}} | collective-permute-start | bytes 6291464 | tf_op jit(solution)/shard_map/cond/branch_8_fun/ppermute | solution.py:437
  130.1 89.3 %collective-permute-start.25 = (bf16[64,64,256]{2,1,0:T(8,128)(2,1)}, bf16[64,64,256]{2,1,0:T(8,128)(2,1)}, u32[]{:S(2)}, u32[]{:S(2)}) collective-permute-start(bf16[64,64,256]{2,1,0:T(8,128)(2,1)} %get-tuple-element.173), channel_id=1, source_target_pairs={{0,3},{1,2},{2,1},{3,0},{4,7},{5,6},{6,5},{7,4}} | collective-permute-start | bytes 6291464 | tf_op jit(solution)/shard_map/cond/branch_8_fun/ppermute | solution.py:437
  219.4 9.5 %collective-permute-start.88 = (bf16[8,64,256]{2,1,0:T(8,128)(2,1)}, bf16[8,64,256]{2,1,0:T(8,128)(2,1)}, u32[]{:S(2)}, u32[]{:S(2)}) collective-permute-start(bf16[8,64,256]{2,1,0:T(8,128)(2,1)} %get-tuple-element.416), channel_id=1, source_target_pairs={{0,2},{1,3},{2,0},{3,1},{4,6},{5,7},{6,4},{7,5}} | collective-permute-start | bytes 786440 | tf_op jit(solution)/shard_map/ppermute | solution.py:437
  220.0 14.4 %collective-permute-start.89 = (bf16[8,64,256]{2,1,0:T(8,128)(2,1)S(1)}, bf16[8,64,256]{2,1,0:T(8,128)(2,1)}, u32[]{:S(2)}, u32[]{:S(2)}) collective-permute-start(bf16[8,64,256]{2,1,0:T(8,128)(2,1)S(1)} %copy-done.11), channel_id=1, source_target_pairs={{0,3},{1,2},{2,1},{3,0},{4,7},{5,6},{6,5},{7,4}} | collective-permute-start | bytes 786440 | tf_op jit(solution)/shard_map/ppermute | solution.py:437
  221.7 230.0 %collective-permute-start.87 = (bf16[192,64,256]{2,1,0:T(8,128)(2,1)}, bf16[192,64,256]{2,1,0:T(8,128)(2,1)}, u32[]{:S(2)}, u32[]{:S(2)}) collective-permute-start(bf16[192,64,256]{2,1,0:T(8,128)(2,1)} %get-tuple-element.412), channel_id=1, source_target_pairs={{0,1},{1,0},{2,3},{3,2},{4,5},{5,4},{6,7},{7,6}} | collective-permute-start | bytes 18874376 | tf_op jit(solution)/shard_map/ppermute | solution.py:437
  221.7 12.9 %collective-permute-start.83 = (bf16[8,64,256]{2,1,0:T(8,128)(2,1)}, bf16[8,64,256]{2,1,0:T(8,128)(2,1)}, u32[]{:S(2)}, u32[]{:S(2)}) collective-permute-start(bf16[8,64,256]{2,1,0:T(8,128)(2,1)} %get-tuple-element.409.refs_7_), channel_id=1, source_target_pairs={{0,1},{1,0},{2,3},{3,2},{4,5},{5,4},{6,7},{7,6}} | collective-permute-start | bytes 786440 | tf_op jit(solution)/shard_map/ppermute | solution.py:437
  222.2 12.8 %collective-permute-start.84 = (bf16[8,64,256]{2,1,0:T(8,128)(2,1)}, bf16[8,64,256]{2,1,0:T(8,128)(2,1)}, u32[]{:S(2)}, u32[]{:S(2)}) collective-permute-start(bf16[8,64,256]{2,1,0:T(8,128)(2,1)} %get-tuple-element.408.refs_6_), channel_id=1, source_target_pairs={{0,1},{1,0},{2,3},{3,2},{4,5},{5,4},{6,7},{7,6}} | collective-permute-start | bytes 786440 | tf_op jit(solution)/shard_map/ppermute | solution.py:437
  228.9 15.4 %collective-permute-start.81 = (bf16[16,64,256]{2,1,0:T(8,128)(2,1)}, bf16[16,64,256]{2,1,0:T(8,128)(2,1)}, u32[]{:S(2)}, u32[]{:S(2)}) collective-permute-start(bf16[16,64,256]{2,1,0:T(8,128)(2,1)} %get-tuple-element.407.refs_5_), channel_id=1, source_target_pairs={{0,1},{1,0},{2,3},{3,2},{4,5},{5,4},{6,7},{7,6}} | collective-permute-start | bytes 1572872 | tf_op jit(solution)/shard_map/ppermute | solution.py:437
  234.4 4.5 collective-permute-start.85
  234.5 7.2 %collective-permute-start.86 = (bf16[8,64,256]{2,1,0:T(8,128)(2,1)}, bf16[8,64,256]{2,1,0:T(8,128)(2,1)}, u32[]{:S(2)}, u32[]{:S(2)}) collective-permute-start(bf16[8,64,256]{2,1,0:T(8,128)(2,1)} %get-tuple-element.410.refs_8_), channel_id=1, source_target_pairs={{0,1},{1,0},{2,3},{3,2},{4,5},{5,4},{6,7},{7,6}} | collective-permute-start | bytes 786440 | tf_op jit(solution)/shard_map/ppermute | solution.py:437
  234.9 9.3 %collective-permute-start.96 = (bf16[8,64,256]{2,1,0:T(8,128)(2,1)}, bf16[8,64,256]{2,1,0:T(8,128)(2,1)}, u32[]{:S(2)}, u32[]{:S(2)}) collective-permute-start(bf16[8,64,256]{2,1,0:T(8,128)(2,1)} %get-tuple-element.429), channel_id=1, source_target_pairs={{0,2},{1,3},{2,0},{3,1},{4,6},{5,7},{6,4},{7,5}} | collective-permute-start | bytes 786440 | tf_op jit(solution)/shard_map/ppermute | solution.py:437
  238.9 43.8 %collective-permute-start.90 = (bf16[24,64,256]{2,1,0:T(8,128)(2,1)}, bf16[24,64,256]{2,1,0:T(8,128)(2,1)}, u32[]{:S(2)}, u32[]{:S(2)}) collective-permute-start(bf16[24,64,256]{2,1,0:T(8,128)(2,1)} %get-tuple-element.418), channel_id=1, source_target_pairs={{0,2},{1,3},{2,0},{3,1},{4,6},{5,7},{6,4},{7,5}} | collective-permute-start | bytes 2359304 | tf_op jit(solution)/shard_map/ppermute | solution.py:437
  241.7 2.5 collective-permute-start.82
  244.3 28.1 %collective-permute-start.98 = (bf16[16,64,256]{2,1,0:T(8,128)(2,1)}, bf16[16,64,256]{2,1,0:T(8,128)(2,1)}, u32[]{:S(2)}, u32[]{:S(2)}) collective-permute-start(bf16[16,64,256]{2,1,0:T(8,128)(2,1)} %get-tuple-element.431), channel_id=1, source_target_pairs={{0,2},{1,3},{2,0},{3,1},{4,6},{5,7},{6,4},{7,5}} | collective-permute-start | bytes 1572872 | tf_op jit(solution)/shard_map/ppermute | solution.py:437
  244.3 37.9 %collective-permute-start.99 = (bf16[16,64,256]{2,1,0:T(8,128)(2,1)}, bf16[16,64,256]{2,1,0:T(8,128)(2,1)}, u32[]{:S(2)}, u32[]{:S(2)}) collective-permute-start(bf16[16,64,256]{2,1,0:T(8,128)(2,1)} %get-tuple-element.432), channel_id=1, source_target_pairs={{0,3},{1,2},{2,1},{3,0},{4,7},{5,6},{6,5},{7,4}} | collective-permute-start | bytes 1572872 | tf_op jit(solution)/shard_map/ppermute | solution.py:437
  244.3 70.5 %collective-permute-start.77 = (bf16[64,64,256]{2,1,0:T(8,128)(2,1)}, bf16[64,64,256]{2,1,0:T(8,128)(2,1)}, u32[]{:S(2)}, u32[]{:S(2)}) collective-permute-start(bf16[64,64,256]{2,1,0:T(8,128)(2,1)} %get-tuple-element.403.refs_1_), channel_id=1, source_target_pairs={{0,1},{1,0},{2,3},{3,2},{4,5},{5,4},{6,7},{7,6}} | collective-permute-start | bytes 6291464 | tf_op jit(solution)/shard_map/ppermute | solution.py:437
  272.4 41.0 %collective-permute-start.79 = (bf16[32,64,256]{2,1,0:T(8,128)(2,1)}, bf16[32,64,256]{2,1,0:T(8,128)(2,1)}, u32[]{:S(2)}, u32[]{:S(2)}) collective-permute-start(bf16[32,64,256]{2,1,0:T(8,128)(2,1)} %get-tuple-element.405.refs_3_), channel_id=1, source_target_pairs={{0,1},{1,0},{2,3},{3,2},{4,5},{5,4},{6,7},{7,6}} | collective-permute-start | bytes 3145736 | tf_op jit(solution)/shard_map/ppermute | solution.py:437
  282.2 306.5 %collective-permute-start.76 = (bf16[192,64,256]{2,1,0:T(8,128)(2,1)}, bf16[192,64,256]{2,1,0:T(8,128)(2,1)}, u32[]{:S(2)}, u32[]{:S(2)}) collective-permute-start(bf16[192,64,256]{2,1,0:T(8,128)(2,1)} %get-tuple-element.399), channel_id=1, source_target_pairs={{0,1},{1,0},{2,3},{3,2},{4,5},{5,4},{6,7},{7,6}} | collective-permute-start | bytes 18874376 | tf_op jit(solution)/shard_map/ppermute | solution.py:437
  282.7 20.0 %collective-permute-start.91 = (bf16[24,64,256]{2,1,0:T(8,128)(2,1)}, bf16[24,64,256]{2,1,0:T(8,128)(2,1)}, u32[]{:S(2)}, u32[]{:S(2)}) collective-permute-start(bf16[24,64,256]{2,1,0:T(8,128)(2,1)} %get-tuple-element.419), channel_id=1, source_target_pairs={{0,3},{1,2},{2,1},{3,0},{4,7},{5,6},{6,5},{7,4}} | collective-permute-start | bytes 2359304 | tf_op jit(solution)/shard_map/ppermute | solution.py:437
  302.7 10.7 %collective-permute-start.80 = (bf16[32,64,256]{2,1,0:T(8,128)(2,1)}, bf16[32,64,256]{2,1,0:T(8,128)(2,1)}, u32[]{:S(2)}, u32[]{:S(2)}) collective-permute-start(bf16[32,64,256]{2,1,0:T(8,128)(2,1)} %get-tuple-element.404.refs_2_), channel_id=1, source_target_pairs={{0,1},{1,0},{2,3},{3,2},{4,5},{5,4},{6,7},{7,6}} | collective-permute-start | bytes 3145736 | tf_op jit(solution)/shard_map/ppermute | solution.py:437
  313.3 71.3 %collective-permute-start.92 = (bf16[96,64,256]{2,1,0:T(8,128)(2,1)}, bf16[96,64,256]{2,1,0:T(8,128)(2,1)}, u32[]{:S(2)}, u32[]{:S(2)}) collective-permute-start(bf16[96,64,256]{2,1,0:T(8,128)(2,1)} %get-tuple-element.420), channel_id=1, source_target_pairs={{0,2},{1,3},{2,0},{3,1},{4,6},{5,7},{6,4},{7,5}} | collective-permute-start | bytes 9437192 | tf_op jit(solution)/shard_map/ppermute | solution.py:437
  313.4 137.0 %collective-permute-start.93 = (bf16[96,64,256]{2,1,0:T(8,128)(2,1)}, bf16[96,64,256]{2,1,0:T(8,128)(2,1)}, u32[]{:S(2)}, u32[]{:S(2)}) collective-permute-start(bf16[96,64,256]{2,1,0:T(8,128)(2,1)} %get-tuple-element.421), channel_id=1, source_target_pairs={{0,3},{1,2},{2,1},{3,0},{4,7},{5,6},{6,5},{7,4}} | collective-permute-start | bytes 9437192 | tf_op jit(solution)/shard_map/ppermute | solution.py:437
  314.8 4.8 collective-permute-start.78
  319.6 266.8 %collective-permute-start.102 = (bf16[64,64,256]{2,1,0:T(8,128)(2,1)}, bf16[64,64,256]{2,1,0:T(8,128)(2,1)}, u32[]{:S(2)}, u32[]{:S(2)}) collective-permute-start(bf16[64,64,256]{2,1,0:T(8,128)(2,1)} %get-tuple-element.435), channel_id=1, source_target_pairs={{0,2},{1,3},{2,0},{3,1},{4,6},{5,7},{6,4},{7,5}} | collective-permute-start | bytes 6291464 | tf_op jit(solution)/shard_map/ppermute | solution.py:437
  384.6 203.7 %collective-permute-start.103 = (bf16[64,64,256]{2,1,0:T(8,128)(2,1)}, bf16[64,64,256]{2,1,0:T(8,128)(2,1)}, u32[]{:S(2)}, u32[]{:S(2)}) collective-permute-start(bf16[64,64,256]{2,1,0:T(8,128)(2,1)} %get-tuple-element.436), channel_id=1, source_target_pairs={{0,3},{1,2},{2,1},{3,0},{4,7},{5,6},{6,5},{7,4}} | collective-permute-start | bytes 6291464 | tf_op jit(solution)/shard_map/ppermute | solution.py:437
  450.4 114.0 %collective-permute-start.100 = (bf16[32,64,256]{2,1,0:T(8,128)(2,1)}, bf16[32,64,256]{2,1,0:T(8,128)(2,1)}, u32[]{:S(2)}, u32[]{:S(2)}) collective-permute-start(bf16[32,64,256]{2,1,0:T(8,128)(2,1)} %get-tuple-element.433), channel_id=1, source_target_pairs={{0,2},{1,3},{2,0},{3,1},{4,6},{5,7},{6,4},{7,5}} | collective-permute-start | bytes 3145736 | tf_op jit(solution)/shard_map/ppermute | solution.py:437
  451.6 133.6 %collective-permute-start.101 = (bf16[32,64,256]{2,1,0:T(8,128)(2,1)}, bf16[32,64,256]{2,1,0:T(8,128)(2,1)}, u32[]{:S(2)}, u32[]{:S(2)}) collective-permute-start(bf16[32,64,256]{2,1,0:T(8,128)(2,1)} %get-tuple-element.434), channel_id=1, source_target_pairs={{0,3},{1,2},{2,1},{3,0},{4,7},{5,6},{6,5},{7,4}} | collective-permute-start | bytes 3145736 | tf_op jit(solution)/shard_map/ppermute | solution.py:437
  501.3 2.2 copy-start
  564.4 73.8 %collective-permute-start.97 = (bf16[8,64,256]{2,1,0:T(8,128)(2,1)}, bf16[8,64,256]{2,1,0:T(8,128)(2,1)}, u32[]{:S(2)}, u32[]{:S(2)}) collective-permute-start(bf16[8,64,256]{2,1,0:T(8,128)(2,1)} %get-tuple-element.430), channel_id=1, source_target_pairs={{0,3},{1,2},{2,1},{3,0},{4,7},{5,6},{6,5},{7,4}} | collective-permute-start | bytes 786440 | tf_op jit(solution)/shard_map/ppermute | solution.py:437
  585.2 57.8 %collective-permute-start.94 = (bf16[4,64,256]{2,1,0:T(8,128)(2,1)}, bf16[4,64,256]{2,1,0:T(8,128)(2,1)}, u32[]{:S(2)}, u32[]{:S(2)}) collective-permute-start(bf16[4,64,256]{2,1,0:T(8,128)(2,1)} %get-tuple-element.427), channel_id=1, source_target_pairs={{0,2},{1,3},{2,0},{3,1},{4,6},{5,7},{6,4},{7,5}} | collective-permute-start | bytes 393224 | tf_op jit(solution)/shard_map/ppermute | solution.py:437
  586.4 56.6 %collective-permute-start.95 = (bf16[4,64,256]{2,1,0:T(8,128)(2,1)}, bf16[4,64,256]{2,1,0:T(8,128)(2,1)}, u32[]{:S(2)}, u32[]{:S(2)}) collective-permute-start(bf16[4,64,256]{2,1,0:T(8,128)(2,1)} %get-tuple-element.428), channel_id=1, source_target_pairs={{0,3},{1,2},{2,1},{3,0},{4,7},{5,6},{6,5},{7,4}} | collective-permute-start | bytes 393224 | tf_op jit(solution)/shard_map/ppermute | solution.py:437
  588.4 58.9 %collective-permute-start.74 = (bf16[4,64,256]{2,1,0:T(8,128)(2,1)}, bf16[4,64,256]{2,1,0:T(8,128)(2,1)}, u32[]{:S(2)}, u32[]{:S(2)}) collective-permute-start(bf16[4,64,256]{2,1,0:T(8,128)(2,1)} %get-tuple-element.397), channel_id=1, source_target_pairs={{0,2},{1,3},{2,0},{3,1},{4,6},{5,7},{6,4},{7,5}} | collective-permute-start | bytes 393224 | tf_op jit(solution)/shard_map/ppermute | solution.py:437
  588.6 58.6 %collective-permute-start.75 = (bf16[4,64,256]{2,1,0:T(8,128)(2,1)}, bf16[4,64,256]{2,1,0:T(8,128)(2,1)}, u32[]{:S(2)}, u32[]{:S(2)}) collective-permute-start(bf16[4,64,256]{2,1,0:T(8,128)(2,1)} %get-tuple-element.398), channel_id=1, source_target_pairs={{0,3},{1,2},{2,1},{3,0},{4,7},{5,6},{6,5},{7,4}} | collective-permute-start | bytes 393224 | tf_op jit(solution)/shard_map/ppermute | solution.py:437

commit v2 on v1

--- a/solution.py
+++ b/solution.py
@@ -20,7 +20,7 @@
 QUANTUM = UNITS[-1]
 LEVELS = SPARE // QUANTUM + 1
 K_PIECES = (8, 24, 96)
-V_PIECES = (64, 32, 16, 8, 4, 4)
+V_PIECES = (96, 24, 8)
 WAYS, ROWS = 4, 3
 VMEM_LIMIT = 67_043_328
 ANYWHERE = pl.BlockSpec(memory_space=pl.ANY)
@@ -131,12 +131,19 @@
         to = lax.rem(step, slots)
 
         def from_ref(ref):
-            def one(t, carry):
-                for a in range(2):
-                    pltpu.make_async_copy(ref.at[at(a, first + t)[0]], buf.at[to, a, t], sems.at[0, to]).start()
-                return carry
-
-            lax.fori_loop(0, size, one, 0)
+            for a in range(2):
+                def one(t, found):
+                    src, code = at(a, first + t)
+                    pltpu.make_async_copy(ref.at[src], buf.at[to, a, t], sems.at[0, to]).start()
+                    mixed = code >= GRAN
+
+                    @pl.when(mixed)
+                    def _():
+                        pltpu.make_async_copy(ref.at[code // GRAN - 1], older.at[to, a, found], sems.at[2, to]).start()
+
+                    return found + mixed.astype(jnp.int32)
+
+                lax.fori_loop(0, size, one, jnp.int32(0))
 
         by_tensor(step, from_ref)
 
@@ -161,28 +168,23 @@
     pltpu.make_async_copy(buf.at[slot], buf.at[slot], sems.at[0, slot]).wait()
     first = base + lax.rem(i, steps) * size
     for a in range(2):
-        def patch(t, carry):
+        def patch(t, found):
             code = at(a, first + t)[1]
+            mixed = code >= GRAN
 
             @pl.when(code >= 0)
             def _():
-                granule = code // GRAN - 1
-
-                @pl.when(granule >= 0)
+                @pl.when(mixed)
                 def _():
-                    by_tensor(i, lambda ref: pltpu.make_async_copy(ref.at[granule], older, sems.at[0, slot]).start())
-                    pltpu.make_async_copy(older, older, sems.at[0, slot]).wait()
-
-                @pl.when(granule < 0)
-                def _():
-                    older[...] = jnp.zeros_like(older)
+                    pltpu.make_async_copy(older.at[slot, a, found], older.at[slot, a, found], sems.at[2, slot]).wait()
 
                 newer = lax.broadcasted_iota(jnp.int32, (GRAN, 256), 0) < lax.rem(code, GRAN)
-                buf[slot, a, t] = jnp.where(newer, buf[slot, a, t].astype(jnp.float32), older[...].astype(jnp.float32)).astype(jnp.bfloat16)
-
-            return carry
-
-        lax.fori_loop(0, size, patch, 0)
+                rest = jnp.where(mixed, older[slot, a, found].astype(jnp.float32), 0.0)
+                buf[slot, a, t] = jnp.where(newer, buf[slot, a, t].astype(jnp.float32), rest).astype(jnp.bfloat16)
+
+            return found + mixed.astype(jnp.int32)
+
+        lax.fori_loop(0, size, patch, jnp.int32(0))
     for copy in stores(i):
         copy.start()
 
@@ -245,7 +247,7 @@
             grid=(steps * len(prefills),),
             in_specs=[ANYWHERE] * len(prefills),
             out_specs=[ANYWHERE] * 2,
-            scratch_shapes=[pltpu.VMEM((3, 2, size, GRAN, 256), jnp.bfloat16), pltpu.VMEM((GRAN, 256), jnp.bfloat16), pltpu.SemaphoreType.DMA((2, 3))],
+            scratch_shapes=[pltpu.VMEM((3, 2, size, GRAN, 256), jnp.bfloat16), pltpu.VMEM((3, 2, 2 * ROWS + 1, GRAN, 256), jnp.bfloat16), pltpu.SemaphoreType.DMA((3, 3))],
         ),
         out_shape=[jax.ShapeDtypeStruct((total, GRAN, 256), jnp.bfloat16)] * 2,
         compiler_params=pltpu.CompilerParams(dimension_semantics=("arbitrary",), vmem_limit_bytes=VMEM_LIMIT),

time: 667 us -> 607 us (0.910)
  the two profiles are of different devices: /device:TPU:6 before, /device:TPU:0 now
where the time goes in v2:
time: 607 us; the launch traced here: 601 us
  waiting for transfers between devices  353 us (58%)
  Pallas kernels  174 us (29%)
  starting transfers between devices  19.5 us (3%)
  matrix products  17 us (3%)
  other arithmetic  13.6 us (2%)
  local copies, waits for them, and re-layouts  9.2 us (2%)
  between operations  8.24 us (1%)
  blocking collectives  6.14 us (1%)
    ppermute x26, waiting for transfers between devices, send(): return lax.ppermute(x, 'sh', [(i, i ^ d) for i in range(WAYS)])  353 us
    pallas_call x13, Pallas kernels, pack(): pl.pallas_call(functools.partial(pack_kernel, base, size, steps, source),...  89.8 us
    pallas_call x6, Pallas kernels, assemble(): pl.pallas_call(functools.partial(assemble_kernel, is_key, base, size, ste...  77.6 us
    ppermute x26, starting transfers between devices, send(): return lax.ppermute(x, 'sh', [(i, i ^ d) for i in range(WAYS)])  19.5 us
  transfers between devices with their start and end apart: 26, of which 12 were waited for; matrix products, arithmetic and copies ran while one was open for 1% of the time, Pallas kernels for 15%

profile of v2, /device:TPU:0, one launch (start us, length us, event | category | flops | bytes accessed | tf_op | source)
XLA Modules:
  0.0 600.6 jit_solution(3376824545886025748)
XLA Ops:
  3.0 6.1 %pmax.7 = s32[]{:T(128)} all-reduce(s32[]{:T(128)S(6)} %select_n.611), channel_id=1, replica_groups=mesh['dp'=2,'sh'=4] {'dp'}, use_global_device_ids=true, to_apply=%region_3.4 | all-reduce | flops 1 | bytes 8 | tf_op jit(solution)/shard_map/pmax | solution.py:466
  18.1 8.4 %pack.18 = (bf16[96,64,256]{2,1,0:T(8,128)(2,1)}, bf16[96,64,256]{2,1,0:T(8,128)(2,1)}) custom-call(s32[2,128]{1,0:T(2,128)} %get-tuple-element.447.refs_0_, s32[2,128]{1,0:T(2,128)} %get-tuple-element.446.refs_1_, bf16[1920,64,256]{2,1,0:T(8,128)(2,1)} %bitcast.33), custom_call_target="tpu_custom_call" | custom-call | flops 10000000 | bytes 12480000 | tf_op jit(solution)/shard_map/pack/pallas_call | solution.py:243
  26.5 3.8 pack.19
  32.2 15.4 %pack.22 = (bf16[192,64,256]{2,1,0:T(8,128)(2,1)}, bf16[192,64,256]{2,1,0:T(8,128)(2,1)}) custom-call(s32[2,192]{1,0:T(2,128)} %get-tuple-element.445.refs_0_, s32[2,192]{1,0:T(2,128)} %get-tuple-element.444.refs_1_, bf16[1920,64,256]{2,1,0:T(8,128)(2,1)} %bitcast.35), custom_call_target="tpu_custom_call" | custom-call | flops 10000000 | bytes 24960000 | tf_op jit(solution)/shard_map/pack/pallas_call | solution.py:243
  47.6 17.9 %pack.21 = (bf16[192,64,256]{2,1,0:T(8,128)(2,1)}, bf16[192,64,256]{2,1,0:T(8,128)(2,1)}) custom-call(s32[2,192]{1,0:T(2,128)} %get-tuple-element.445.refs_0_, s32[2,192]{1,0:T(2,128)} %get-tuple-element.444.refs_1_, bf16[1920,64,256]{2,1,0:T(8,128)(2,1)} %bitcast.42), custom_call_target="tpu_custom_call" | custom-call | flops 10000000 | bytes 24960000 | tf_op jit(solution)/shard_map/pack/pallas_call | solution.py:243
  65.6 9.4 %pack.13 = (bf16[64,64,256]{2,1,0:T(8,128)(2,1)}, bf16[64,64,256]{2,1,0:T(8,128)(2,1)}) custom-call(s32[2,64]{1,0:T(2,128)} %fusion.27.refs_0_, s32[2,64]{1,0:T(2,128)} %fusion.26.refs_1_, bf16[1920,64,256]{2,1,0:T(8,128)(2,1)} %bitcast.43, bf16[1920,64,256]{2,1,0:T(8,128)(2,1)} %bitcast.36), custom_call_target="tpu_custom_call" | custom-call | flops 10000000 | bytes 8320000 | tf_op jit(solution)/shard_map/pack/pallas_call | solution.py:243
  75.0 6.1 %pack.14 = (bf16[32,64,256]{2,1,0:T(8,128)(2,1)}, bf16[32,64,256]{2,1,0:T(8,128)(2,1)}) custom-call(s32[2,64]{1,0:T(2,128)} %fusion.27.refs_0_, s32[2,64]{1,0:T(2,128)} %fusion.26.refs_1_, bf16[1920,64,256]{2,1,0:T(8,128)(2,1)} %bitcast.44, bf16[1920,64,256]{2,1,0:T(8,128)(2,1)} %bitcast.37), custom_call_target="tpu_custom_call" | custom-call | flops 10000000 | bytes 4160000 | tf_op jit(solution)/shard_map/pack/pallas_call | solution.py:243
  81.1 2.7 pack.20
  83.8 4.0 pack.15
  87.9 3.0 pack.16
  90.9 3.0 pack.17
  94.8 5.0 convolution_convert_fusion
  100.7 3.1 convolution_convert_fusion.1
  105.0 6.3 %cleared.1 = (bf16[3,4096,4,256]{3,2,1,0:T(4,128)(2,1)}, bf16[3,4096,4,256]{3,2,1,0:T(4,128)(2,1)}) custom-call(s32[3]{0:T(128)} %get-tuple-element.465.n_ref), custom_call_target="tpu_custom_call" | custom-call | flops 10000000 | bytes 20000000 | tf_op jit(solution)/shard_map/cleared/pallas_call | solution.py:76
  111.4 3.3 fusion.2
  117.3 90.4 %conditional.1 = (bf16[64,64,256]{2,1,0:T(8,128)(2,1)}, bf16[64,64,256]{2,1,0:T(8,128)(2,1)}, bf16[32,64,256]{2,1,0:T(8,128)(2,1)}, bf16[32,64,256]{2,1,0:T(8,12...) conditional(s32[]{:T(128)} %clamp.30, () %tuple.78, ...), branch_computations={%region_5.6_spmd, %region_6.7_spmd, %region_7.8_spmd, %region_8.9_... | conditional | bytes 33554912 | solution.py:533
  117.3 5.6 collective-permute-start.24
  122.9 46.6 %collective-permute-done.24 = bf16[64,64,256]{2,1,0:T(8,128)(2,1)} collective-permute-done((bf16[64,64,256]{2,1,0:T(8,128)(2,1)S(1)}, bf16[64,64,256]{2,1,0:T(8,128)(2,1)}, u32[]{:S(2)}, u32[]{:S(2)}) %collective-permute-start.24) | collective-permute-done | bytes 2097184 | tf_op jit(solution)/shard_map/cond/branch_8_fun/ppermute | solution.py:439
  169.5 38.2 %collective-permute-done.25 = bf16[64,64,256]{2,1,0:T(8,128)(2,1)} collective-permute-done((bf16[64,64,256]{2,1,0:T(8,128)(2,1)}, bf16[64,64,256]{2,1,0:T(8,128)(2,1)}, u32[]{:S(2)}, u32[]{:S(2)}) %collective-permute-start.25) | collective-permute-done | bytes 2097184 | tf_op jit(solution)/shard_map/cond/branch_8_fun/ppermute | solution.py:439
  208.2 3.2 pack.23
  211.4 1.8 collective-permute-start.88
  213.6 7.2 %collective-permute-done.88.refs_0_ = bf16[8,64,256]{2,1,0:T(8,128)(2,1)} collective-permute-done((bf16[8,64,256]{2,1,0:T(8,128)(2,1)}, bf16[8,64,256]{2,1,0:T(8,128)(2,1)}, u32[]{:S(2)}, u32[]{:S(2)}) %collective-permute-start.88) | collective-permute-done | bytes 262176 | tf_op jit(solution)/shard_map/ppermute | solution.py:439
  220.9 3.9 collective-permute-done.89.refs_1_
  225.4 2.7 collective-permute-done.84.refs_17_
  228.8 4.0 pack.24
  232.8 1.7 collective-permute-start.90
  234.5 8.8 %pack.25 = (bf16[96,64,256]{2,1,0:T(8,128)(2,1)}, bf16[96,64,256]{2,1,0:T(8,128)(2,1)}) custom-call(s32[2,128]{1,0:T(2,128)} %get-tuple-element.447.refs_0_, s32[2,128]{1,0:T(2,128)} %get-tuple-element.446.refs_1_, bf16[1920,64,256]{2,1,0:T(8,128)(2,1)} %bitcast.50), custom_call_target="tpu_custom_call" | custom-call | flops 10000000 | bytes 12480000 | tf_op jit(solution)/shard_map/pack/pallas_call | solution.py:243
  243.4 1.4 collective-permute-start.93
  244.9 8.7 %collective-permute-done.90.refs_2_ = bf16[24,64,256]{2,1,0:T(8,128)(2,1)} collective-permute-done((bf16[24,64,256]{2,1,0:T(8,128)(2,1)}, bf16[24,64,256]{2,1,0:T(8,128)(2,1)}, u32[]{:S(2)}, u32[]{:S(2)}) %collective-permute-start.90) | collective-permute-done | bytes 786464 | tf_op jit(solution)/shard_map/ppermute | solution.py:439
  253.5 150.3 %collective-permute-done.91.refs_3_ = bf16[24,64,256]{2,1,0:T(8,128)(2,1)} collective-permute-done((bf16[24,64,256]{2,1,0:T(8,128)(2,1)}, bf16[24,64,256]{2,1,0:T(8,128)(2,1)}, u32[]{:S(2)}, u32[]{:S(2)}) %collective-permute-start.91) | collective-permute-done | bytes 786464 | tf_op jit(solution)/shard_map/ppermute | solution.py:439
  404.3 2.6 collective-permute-done.79.refs_12_
  407.0 1.7 collective-permute-start.96
  409.2 1.4 fusion.84
  415.2 27.1 %assemble_keys.2 = (bf16[3,4096,4,256]{3,2,1,0:T(4,128)(2,1)}, f32[4,8,16384]{2,1,0:T(8,128)}) custom-call(s32[1,256]{1,0:T(1,128)} %get-tuple-element.474.code_ref, s32[1,256]{1,0:T(1,128)} %get-tuple-element.475.idx_ref, s32[3]{0:T(128)} %get-tuple-element.465.n_ref, s32[1]{0:T(128)} %bitcast.5.me_ref, ...), custom_call_target="tpu_custom_call", output_to_operand_aliasing={{0}: (15, {}), {1}: (14, {})} | custom-call | flops 10000000 | bytes 64000000 | tf_op jit(solution)/shard_map/assemble_keys/pallas_call | solution.py:410
  442.7 1.7 collective-permute-start.94
  444.3 8.8 %assemble_keys.3 = (bf16[3,4096,4,256]{3,2,1,0:T(4,128)(2,1)}, f32[4,8,16384]{2,1,0:T(8,128)}) custom-call(s32[1,256]{1,0:T(1,128)} %get-tuple-element.474.code_ref, s32[1,256]{1,0:T(1,128)} %get-tuple-element.475.idx_ref, s32[3]{0:T(128)} %get-tuple-element.465.n_ref, s32[1]{0:T(128)} %bitcast.5.me_ref, ...), custom_call_target="tpu_custom_call", output_to_operand_aliasing={{0}: (29, {}), {1}: (28, {})} | custom-call | flops 10000000 | bytes 64000000 | tf_op jit(solution)/shard_map/assemble_keys/pallas_call | solution.py:410
  453.2 2.0 reduce_max.19
  455.9 22.3 %collective-permute-done.96.refs_0_ = bf16[96,64,256]{2,1,0:T(8,128)(2,1)} collective-permute-done((bf16[96,64,256]{2,1,0:T(8,128)(2,1)}, bf16[96,64,256]{2,1,0:T(8,128)(2,1)}, u32[]{:S(2)}, u32[]{:S(2)}) %collective-permute-start.96) | collective-permute-done | bytes 3145760 | tf_op jit(solution)/shard_map/ppermute | solution.py:439
  478.2 1.7 collective-permute-start.74
  479.9 1.4 divide_convert_fusion.refs_23_.refs_5_
  481.9 9.5 %assemble_values.4 = (bf16[3,4096,4,256]{3,2,1,0:T(4,128)(2,1)}, f32[4,8,256]{2,1,0:T(8,128)}) custom-call(s32[1,256]{1,0:T(1,128)} %get-tuple-element.474.code_ref, s32[1,256]{1,0:T(1,128)} %get-tuple-element.475.idx_ref, s32[3]{0:T(128)} %get-tuple-element.465.n_ref, s32[1]{0:T(128)} %bitcast.5.me_ref, ...), custom_call_target="tpu_custom_call", output_to_operand_aliasing={{0}: (29, {})} | custom-call | flops 10000000 | bytes 64000000 | tf_op jit(solution)/shard_map/assemble_values/pallas_call | solution.py:410
  491.4 53.4 %collective-permute-done.97.refs_1_ = bf16[96,64,256]{2,1,0:T(8,128)(2,1)} collective-permute-done((bf16[96,64,256]{2,1,0:T(8,128)(2,1)}, bf16[96,64,256]{2,1,0:T(8,128)(2,1)}, u32[]{:S(2)}, u32[]{:S(2)}) %collective-permute-start.97) | collective-permute-done | bytes 3145760 | tf_op jit(solution)/shard_map/ppermute | solution.py:439
  544.8 20.0 %assemble_values.5 = (bf16[3,4096,4,256]{3,2,1,0:T(4,128)(2,1)}, f32[4,8,256]{2,1,0:T(8,128)}) custom-call(s32[1,256]{1,0:T(1,128)} %get-tuple-element.474.code_ref, s32[1,256]{1,0:T(1,128)} %get-tuple-element.475.idx_ref, s32[3]{0:T(128)} %get-tuple-element.465.n_ref, s32[1]{0:T(128)} %bitcast.5.me_ref, ...), custom_call_target="tpu_custom_call", output_to_operand_aliasing={{0}: (11, {})} | custom-call | flops 10000000 | bytes 48000000 | tf_op jit(solution)/shard_map/assemble_values/pallas_call | solution.py:410
  564.9 13.7 %collective-permute-done.95.refs_1_ = bf16[24,64,256]{2,1,0:T(8,128)(2,1)} collective-permute-done((bf16[24,64,256]{2,1,0:T(8,128)(2,1)}, bf16[24,64,256]{2,1,0:T(8,128)(2,1)}, u32[]{:S(2)}, u32[]{:S(2)}) %collective-permute-start.95) | collective-permute-done | bytes 786464 | tf_op jit(solution)/shard_map/ppermute | solution.py:439
  578.5 7.4 %assemble_values.6 = (bf16[3,4096,4,256]{3,2,1,0:T(4,128)(2,1)}, f32[4,8,256]{2,1,0:T(8,128)}) custom-call(s32[1,256]{1,0:T(1,128)} %get-tuple-element.474.code_ref, s32[1,256]{1,0:T(1,128)} %get-tuple-element.475.idx_ref, s32[3]{0:T(128)} %get-tuple-element.465.n_ref, s32[1]{0:T(128)} %bitcast.5.me_ref, ...), custom_call_target="tpu_custom_call", output_to_operand_aliasing={{0}: (11, {})} | custom-call | flops 10000000 | bytes 12000000 | tf_op jit(solution)/shard_map/assemble_values/pallas_call | solution.py:410
  586.0 3.4 collective-permute-done.75.refs_1_
  589.4 4.8 assemble_values.7
  595.0 5.6 fusion
  (123 shorter events, 22.2 us)
Async XLA Ops:
  93.9 0.7 copy-start.7
  93.9 0.7 copy-start.1
  94.6 6.0 %copy-start.2 = (f32[2304]{0:T(1024)}, f32[2304]{0:T(1024)S(1)}, u32[]{:S(2)}) copy-start(f32[2304]{0:T(1024)S(1)} %convert_element_type.450) | copy-start | bytes 27652
  94.8 5.9 copy-start.6
  94.8 5.1 copy-start.8
  111.4 4.0 copy-start.3
  111.4 4.6 copy-start.4
  111.4 4.6 copy-start.5
  111.4 5.8 copy-start.9
  111.4 5.8 copy-start.10
  111.4 5.8 copy-start.11
  117.3 52.2 %collective-permute-start.24 = (bf16[64,64,256]{2,1,0:T(8,128)(2,1)S(1)}, bf16[64,64,256]{2,1,0:T(8,128)(2,1)}, u32[]{:S(2)}, u32[]{:S(2)}) collective-permute-start(bf16[64,64,256]{2,1,0:T(8,128)(2,1)S(1)} %get-tuple-element.172), channel_id=1, source_target_pairs={{0,2},{1,3},{2,0},{3,1},{4,6},{5,7},{6,4},{7,5}} | collective-permute-start | bytes 6291464 | tf_op jit(solution)/shard_map/cond/branch_8_fun/ppermute | solution.py:439
  122.9 84.7 %collective-permute-start.25 = (bf16[64,64,256]{2,1,0:T(8,128)(2,1)}, bf16[64,64,256]{2,1,0:T(8,128)(2,1)}, u32[]{:S(2)}, u32[]{:S(2)}) collective-permute-start(bf16[64,64,256]{2,1,0:T(8,128)(2,1)} %get-tuple-element.173), channel_id=1, source_target_pairs={{0,3},{1,2},{2,1},{3,0},{4,7},{5,6},{6,5},{7,4}} | collective-permute-start | bytes 6291464 | tf_op jit(solution)/shard_map/cond/branch_8_fun/ppermute | solution.py:439
  207.6 201.5 %collective-permute-start.87 = (bf16[192,64,256]{2,1,0:T(8,128)(2,1)}, bf16[192,64,256]{2,1,0:T(8,128)(2,1)}, u32[]{:S(2)}, u32[]{:S(2)}) collective-permute-start(bf16[192,64,256]{2,1,0:T(8,128)(2,1)} %get-tuple-element.376), channel_id=1, source_target_pairs={{0,1},{1,0},{2,3},{3,2},{4,5},{5,4},{6,7},{7,6}} | collective-permute-start | bytes 18874376 | tf_op jit(solution)/shard_map/ppermute | solution.py:439
  211.4 9.5 %collective-permute-start.88 = (bf16[8,64,256]{2,1,0:T(8,128)(2,1)}, bf16[8,64,256]{2,1,0:T(8,128)(2,1)}, u32[]{:S(2)}, u32[]{:S(2)}) collective-permute-start(bf16[8,64,256]{2,1,0:T(8,128)(2,1)} %get-tuple-element.380), channel_id=1, source_target_pairs={{0,2},{1,3},{2,0},{3,1},{4,6},{5,7},{6,4},{7,5}} | collective-permute-start | bytes 786440 | tf_op jit(solution)/shard_map/ppermute | solution.py:439
  213.1 11.7 %collective-permute-start.89 = (bf16[8,64,256]{2,1,0:T(8,128)(2,1)}, bf16[8,64,256]{2,1,0:T(8,128)(2,1)}, u32[]{:S(2)}, u32[]{:S(2)}) collective-permute-start(bf16[8,64,256]{2,1,0:T(8,128)(2,1)} %get-tuple-element.381), channel_id=1, source_target_pairs={{0,3},{1,2},{2,1},{3,0},{4,7},{5,6},{6,5},{7,4}} | collective-permute-start | bytes 786440 | tf_op jit(solution)/shard_map/ppermute | solution.py:439
  213.1 12.2 %collective-permute-start.83 = (bf16[8,64,256]{2,1,0:T(8,128)(2,1)}, bf16[8,64,256]{2,1,0:T(8,128)(2,1)}, u32[]{:S(2)}, u32[]{:S(2)}) collective-permute-start(bf16[8,64,256]{2,1,0:T(8,128)(2,1)} %get-tuple-element.373.refs_7_), channel_id=1, source_target_pairs={{0,1},{1,0},{2,3},{3,2},{4,5},{5,4},{6,7},{7,6}} | collective-permute-start | bytes 786440 | tf_op jit(solution)/shard_map/ppermute | solution.py:439
  213.5 266.4 %collective-permute-start.76 = (bf16[192,64,256]{2,1,0:T(8,128)(2,1)}, bf16[192,64,256]{2,1,0:T(8,128)(2,1)}, u32[]{:S(2)}, u32[]{:S(2)}) collective-permute-start(bf16[192,64,256]{2,1,0:T(8,128)(2,1)} %get-tuple-element.363), channel_id=1, source_target_pairs={{0,1},{1,0},{2,3},{3,2},{4,5},{5,4},{6,7},{7,6}} | collective-permute-start | bytes 18874376 | tf_op jit(solution)/shard_map/ppermute | solution.py:439
  220.9 7.2 %collective-permute-start.84 = (bf16[8,64,256]{2,1,0:T(8,128)(2,1)}, bf16[8,64,256]{2,1,0:T(8,128)(2,1)}, u32[]{:S(2)}, u32[]{:S(2)}) collective-permute-start(bf16[8,64,256]{2,1,0:T(8,128)(2,1)} %get-tuple-element.372.refs_6_), channel_id=1, source_target_pairs={{0,1},{1,0},{2,3},{3,2},{4,5},{5,4},{6,7},{7,6}} | collective-permute-start | bytes 786440 | tf_op jit(solution)/shard_map/ppermute | solution.py:439
  224.8 3.6 collective-permute-start.85
  225.4 7.4 %collective-permute-start.86 = (bf16[8,64,256]{2,1,0:T(8,128)(2,1)}, bf16[8,64,256]{2,1,0:T(8,128)(2,1)}, u32[]{:S(2)}, u32[]{:S(2)}) collective-permute-start(bf16[8,64,256]{2,1,0:T(8,128)(2,1)} %get-tuple-element.374.refs_8_), channel_id=1, source_target_pairs={{0,1},{1,0},{2,3},{3,2},{4,5},{5,4},{6,7},{7,6}} | collective-permute-start | bytes 786440 | tf_op jit(solution)/shard_map/ppermute | solution.py:439
  228.1 15.2 %collective-permute-start.81 = (bf16[16,64,256]{2,1,0:T(8,128)(2,1)}, bf16[16,64,256]{2,1,0:T(8,128)(2,1)}, u32[]{:S(2)}, u32[]{:S(2)}) collective-permute-start(bf16[16,64,256]{2,1,0:T(8,128)(2,1)} %get-tuple-element.371.refs_5_), channel_id=1, source_target_pairs={{0,1},{1,0},{2,3},{3,2},{4,5},{5,4},{6,7},{7,6}} | collective-permute-start | bytes 1572872 | tf_op jit(solution)/shard_map/ppermute | solution.py:439
  228.4 15.0 %collective-permute-start.82 = (bf16[16,64,256]{2,1,0:T(8,128)(2,1)}, bf16[16,64,256]{2,1,0:T(8,128)(2,1)}, u32[]{:S(2)}, u32[]{:S(2)}) collective-permute-start(bf16[16,64,256]{2,1,0:T(8,128)(2,1)} %get-tuple-element.370.refs_4_), channel_id=1, source_target_pairs={{0,1},{1,0},{2,3},{3,2},{4,5},{5,4},{6,7},{7,6}} | collective-permute-start | bytes 1572872 | tf_op jit(solution)/shard_map/ppermute | solution.py:439
  232.8 20.8 %collective-permute-start.90 = (bf16[24,64,256]{2,1,0:T(8,128)(2,1)}, bf16[24,64,256]{2,1,0:T(8,128)(2,1)}, u32[]{:S(2)}, u32[]{:S(2)}) collective-permute-start(bf16[24,64,256]{2,1,0:T(8,128)(2,1)} %get-tuple-element.382), channel_id=1, source_target_pairs={{0,2},{1,3},{2,0},{3,1},{4,6},{5,7},{6,4},{7,5}} | collective-permute-start | bytes 2359304 | tf_op jit(solution)/shard_map/ppermute | solution.py:439
  243.3 165.4 %collective-permute-start.92 = (bf16[96,64,256]{2,1,0:T(8,128)(2,1)}, bf16[96,64,256]{2,1,0:T(8,128)(2,1)}, u32[]{:S(2)}, u32[]{:S(2)}) collective-permute-start(bf16[96,64,256]{2,1,0:T(8,128)(2,1)} %get-tuple-element.384), channel_id=1, source_target_pairs={{0,2},{1,3},{2,0},{3,1},{4,6},{5,7},{6,4},{7,5}} | collective-permute-start | bytes 9437192 | tf_op jit(solution)/shard_map/ppermute | solution.py:439
  243.4 165.3 %collective-permute-start.93 = (bf16[96,64,256]{2,1,0:T(8,128)(2,1)}, bf16[96,64,256]{2,1,0:T(8,128)(2,1)}, u32[]{:S(2)}, u32[]{:S(2)}) collective-permute-start(bf16[96,64,256]{2,1,0:T(8,128)(2,1)} %get-tuple-element.385), channel_id=1, source_target_pairs={{0,3},{1,2},{2,1},{3,0},{4,7},{5,6},{6,5},{7,4}} | collective-permute-start | bytes 9437192 | tf_op jit(solution)/shard_map/ppermute | solution.py:439
  253.5 150.3 %collective-permute-start.91 = (bf16[24,64,256]{2,1,0:T(8,128)(2,1)}, bf16[24,64,256]{2,1,0:T(8,128)(2,1)}, u32[]{:S(2)}, u32[]{:S(2)}) collective-permute-start(bf16[24,64,256]{2,1,0:T(8,128)(2,1)} %get-tuple-element.383), channel_id=1, source_target_pairs={{0,3},{1,2},{2,1},{3,0},{4,7},{5,6},{6,5},{7,4}} | collective-permute-start | bytes 2359304 | tf_op jit(solution)/shard_map/ppermute | solution.py:439
  403.8 3.2 collective-permute-start.79
  407.0 71.3 %collective-permute-start.96 = (bf16[96,64,256]{2,1,0:T(8,128)(2,1)}, bf16[96,64,256]{2,1,0:T(8,128)(2,1)}, u32[]{:S(2)}, u32[]{:S(2)}) collective-permute-start(bf16[96,64,256]{2,1,0:T(8,128)(2,1)} %get-tuple-element.393), channel_id=1, source_target_pairs={{0,2},{1,3},{2,0},{3,1},{4,6},{5,7},{6,4},{7,5}} | collective-permute-start | bytes 9437192 | tf_op jit(solution)/shard_map/ppermute | solution.py:439
  408.6 34.0 %collective-permute-start.77 = (bf16[64,64,256]{2,1,0:T(8,128)(2,1)}, bf16[64,64,256]{2,1,0:T(8,128)(2,1)}, u32[]{:S(2)}, u32[]{:S(2)}) collective-permute-start(bf16[64,64,256]{2,1,0:T(8,128)(2,1)} %get-tuple-element.367.refs_1_), channel_id=1, source_target_pairs={{0,1},{1,0},{2,3},{3,2},{4,5},{5,4},{6,7},{7,6}} | collective-permute-start | bytes 6291464 | tf_op jit(solution)/shard_map/ppermute | solution.py:439
  408.7 35.6 %collective-permute-start.78 = (bf16[64,64,256]{2,1,0:T(8,128)(2,1)}, bf16[64,64,256]{2,1,0:T(8,128)(2,1)}, u32[]{:S(2)}, u32[]{:S(2)}) collective-permute-start(bf16[64,64,256]{2,1,0:T(8,128)(2,1)} %get-tuple-element.366.refs_0_), channel_id=1, source_target_pairs={{0,1},{1,0},{2,3},{3,2},{4,5},{5,4},{6,7},{7,6}} | collective-permute-start | bytes 6291464 | tf_op jit(solution)/shard_map/ppermute | solution.py:439
  409.1 33.1 %collective-permute-start.80 = (bf16[32,64,256]{2,1,0:T(8,128)(2,1)}, bf16[32,64,256]{2,1,0:T(8,128)(2,1)}, u32[]{:S(2)}, u32[]{:S(2)}) collective-permute-start(bf16[32,64,256]{2,1,0:T(8,128)(2,1)} %get-tuple-element.368.refs_2_), channel_id=1, source_target_pairs={{0,1},{1,0},{2,3},{3,2},{4,5},{5,4},{6,7},{7,6}} | collective-permute-start | bytes 3145736 | tf_op jit(solution)/shard_map/ppermute | solution.py:439
  442.3 102.6 %collective-permute-start.97 = (bf16[96,64,256]{2,1,0:T(8,128)(2,1)}, bf16[96,64,256]{2,1,0:T(8,128)(2,1)}, u32[]{:S(2)}, u32[]{:S(2)}) collective-permute-start(bf16[96,64,256]{2,1,0:T(8,128)(2,1)} %get-tuple-element.394), channel_id=1, source_target_pairs={{0,3},{1,2},{2,1},{3,0},{4,7},{5,6},{6,5},{7,4}} | collective-permute-start | bytes 9437192 | tf_op jit(solution)/shard_map/ppermute | solution.py:439
  442.7 122.2 %collective-permute-start.94 = (bf16[24,64,256]{2,1,0:T(8,128)(2,1)}, bf16[24,64,256]{2,1,0:T(8,128)(2,1)}, u32[]{:S(2)}, u32[]{:S(2)}) collective-permute-start(bf16[24,64,256]{2,1,0:T(8,128)(2,1)} %get-tuple-element.391), channel_id=1, source_target_pairs={{0,2},{1,3},{2,0},{3,1},{4,6},{5,7},{6,4},{7,5}} | collective-permute-start | bytes 2359304 | tf_op jit(solution)/shard_map/ppermute | solution.py:439
  444.3 134.2 %collective-permute-start.95 = (bf16[24,64,256]{2,1,0:T(8,128)(2,1)}, bf16[24,64,256]{2,1,0:T(8,128)(2,1)}, u32[]{:S(2)}, u32[]{:S(2)}) collective-permute-start(bf16[24,64,256]{2,1,0:T(8,128)(2,1)} %get-tuple-element.392), channel_id=1, source_target_pairs={{0,3},{1,2},{2,1},{3,0},{4,7},{5,6},{6,5},{7,4}} | collective-permute-start | bytes 2359304 | tf_op jit(solution)/shard_map/ppermute | solution.py:439
  453.2 2.2 copy-start
  478.2 107.7 %collective-permute-start.74 = (bf16[8,64,256]{2,1,0:T(8,128)(2,1)}, bf16[8,64,256]{2,1,0:T(8,128)(2,1)}, u32[]{:S(2)}, u32[]{:S(2)}) collective-permute-start(bf16[8,64,256]{2,1,0:T(8,128)(2,1)} %get-tuple-element.361), channel_id=1, source_target_pairs={{0,2},{1,3},{2,0},{3,1},{4,6},{5,7},{6,4},{7,5}} | collective-permute-start | bytes 786440 | tf_op jit(solution)/shard_map/ppermute | solution.py:439
  479.9 109.5 %collective-permute-start.75 = (bf16[8,64,256]{2,1,0:T(8,128)(2,1)}, bf16[8,64,256]{2,1,0:T(8,128)(2,1)}, u32[]{:S(2)}, u32[]{:S(2)}) collective-permute-start(bf16[8,64,256]{2,1,0:T(8,128)(2,1)} %get-tuple-element.362), channel_id=1, source_target_pairs={{0,3},{1,2},{2,1},{3,0},{4,7},{5,6},{6,5},{7,4}} | collective-permute-start | bytes 786440 | tf_op jit(solution)/shard_map/ppermute | solution.py:439

commit v3 on v2

--- a/solution.py
+++ b/solution.py
@@ -21,9 +21,22 @@
 LEVELS = SPARE // QUANTUM + 1
 K_PIECES = (8, 24, 96)
 V_PIECES = (96, 24, 8)
+CROSS = 32
+ELSEWHERE = 1 << 20
 WAYS, ROWS = 4, 3
 VMEM_LIMIT = 67_043_328
+HALF = CROSS // 2
+KV = (True, False)
+BOTH = range(2)
+SERIAL = pltpu.CompilerParams(dimension_semantics=("arbitrary",), vmem_limit_bytes=VMEM_LIMIT)
 ANYWHERE = pl.BlockSpec(memory_space=pl.ANY)
+
+
+beside = functools.partial(jnp.concatenate, axis=1)
+
+
+def cost(moved):
+    return pl.CostEstimate(flops=10_000_000, bytes_accessed=moved, transcendentals=0)
 
 
 def starts_of(sizes):
@@ -80,7 +93,7 @@
             scratch_shapes=[pltpu.VMEM((GRAN, WAYS, 256), jnp.bfloat16), pltpu.SemaphoreType.DMA]),
         out_shape=[jax.ShapeDtypeStruct(shape, jnp.bfloat16)] * 2,
         compiler_params=pltpu.CompilerParams(vmem_limit_bytes=VMEM_LIMIT),
-        cost_estimate=pl.CostEstimate(flops=10_000_000, bytes_accessed=20_000_000, transcendentals=0),
+        cost_estimate=cost(20_000_000),
         name="cleared",
     )(n)
 
@@ -112,10 +125,10 @@
         return src, jnp.where(g == cut // GRAN, (mixed + 1) * GRAN + cut % GRAN, -1)
 
 
-def pack_kernel(base, size, steps, source, *refs):
+def pack_kernel(base, size, steps, source, extra, *refs):
     num = source.num_scalars
     scalars, refs = refs[:num], refs[num:]
-    prefills, outs, (buf, older, sems) = refs[:-5], refs[-5:-3], refs[-3:]
+    prefills, extras, outs, (buf, older, sems) = refs[:-5 - extra], refs[-5 - extra:-5], refs[-5:-3], refs[-3:]
     at = source.reader(*scalars)
     i = pl.program_id(0)
     total = steps * len(prefills)
@@ -124,17 +137,28 @@
 
     def by_tensor(step, do):
         for k, ref in enumerate(prefills):
-            pl.when((step >= k * steps) & (step < (k + 1) * steps))(functools.partial(do, ref))
+            pl.when((step >= k * steps) & (step < (k + 1) * steps))(functools.partial(do, k, ref))
 
     def fetch(step):
         first = base + lax.rem(step, steps) * size
         to = lax.rem(step, slots)
 
-        def from_ref(ref):
-            for a in range(2):
+        def from_ref(k, ref):
+            for a in BOTH:
                 def one(t, found):
                     src, code = at(a, first + t)
-                    pltpu.make_async_copy(ref.at[src], buf.at[to, a, t], sems.at[0, to]).start()
+                    if not extras:
+                        pltpu.make_async_copy(ref.at[src], buf.at[to, a, t], sems.at[0, to]).start()
+                    else:
+                        @pl.when(src < ELSEWHERE)
+                        def _():
+                            pltpu.make_async_copy(ref.at[src], buf.at[to, a, t], sems.at[0, to]).start()
+
+                        for e, other in enumerate(extras):
+
+                            @pl.when((src >= ELSEWHERE + e * HALF) & (src < ELSEWHERE + (e + 1) * HALF))
+                            def _():
+                                pltpu.make_async_copy(other.at[src - ELSEWHERE + (k - e) * HALF], buf.at[to, a, t], sems.at[0, to]).start()
                     mixed = code >= GRAN
 
                     @pl.when(mixed)
@@ -149,7 +173,7 @@
 
     def stores(step):
         to = lax.rem(step, slots)
-        return [pltpu.make_async_copy(buf.at[to, a], outs[a].at[pl.ds(step * size, size)], sems.at[1, to]) for a in range(2)]
+        return [pltpu.make_async_copy(buf.at[to, a], outs[a].at[pl.ds(step * size, size)], sems.at[1, to]) for a in BOTH]
 
     @pl.when(i == 0)
     def _():
@@ -167,7 +191,7 @@
 
     pltpu.make_async_copy(buf.at[slot], buf.at[slot], sems.at[0, slot]).wait()
     first = base + lax.rem(i, steps) * size
-    for a in range(2):
+    for a in BOTH:
         def patch(t, found):
             code = at(a, first + t)[1]
             mixed = code >= GRAN
@@ -236,24 +260,24 @@
         return at
 
 
-def pack(prefills, source, base, count):
+def pack(prefills, source, base, count, extras=()):
     size = next(x for x in (16, 8, 4) if count % x == 0)
     steps = count // size
     total = count * len(prefills)
     return pl.pallas_call(
-        functools.partial(pack_kernel, base, size, steps, source),
+        functools.partial(pack_kernel, base, size, steps, source, len(extras)),
         grid_spec=pltpu.PrefetchScalarGridSpec(
             num_scalar_prefetch=source.num_scalars,
             grid=(steps * len(prefills),),
-            in_specs=[ANYWHERE] * len(prefills),
+            in_specs=[ANYWHERE] * (len(prefills) + len(extras)),
             out_specs=[ANYWHERE] * 2,
             scratch_shapes=[pltpu.VMEM((3, 2, size, GRAN, 256), jnp.bfloat16), pltpu.VMEM((3, 2, 2 * ROWS + 1, GRAN, 256), jnp.bfloat16), pltpu.SemaphoreType.DMA((3, 3))],
         ),
         out_shape=[jax.ShapeDtypeStruct((total, GRAN, 256), jnp.bfloat16)] * 2,
-        compiler_params=pltpu.CompilerParams(dimension_semantics=("arbitrary",), vmem_limit_bytes=VMEM_LIMIT),
-        cost_estimate=pl.CostEstimate(flops=10_000_000, bytes_accessed=total * 130_000, transcendentals=0),
+        compiler_params=SERIAL,
+        cost_estimate=cost(total * 130_000),
         name="pack",
-    )(*source.scalars, *prefills)
+    )(*source.scalars, *prefills, *extras)
 
 
 def assemble_kernel(is_key, base, size, steps, segments, code_ref, idx_ref, n_ref, me_ref, *refs):
@@ -273,11 +297,11 @@
     def read(step, buf):
         @pl.when(active_at(step))
         def _():
-            for begin, end, entry, offset, count, place in segments:
+            for begin, end, entry, offsets, count, place in segments:
                 @pl.when((step >= begin) & (step < end))
                 def _():
-                    for d in range(2):
-                        pltpu.make_async_copy(far_refs[2 * entry + d].at[pl.ds(offset + (step - begin) * size, count)], xb.at[buf, me ^ (2 + d), pl.ds(place, count)], sems.at[0, buf]).start()
+                    for d in BOTH:
+                        pltpu.make_async_copy(far_refs[2 * entry + d].at[pl.ds(offsets[d] + (step - begin) * size, count)], xb.at[buf, me ^ (2 + d), pl.ds(place, count)], sems.at[0, buf]).start()
 
             def one(t, carry):
                 at = idx_ref[0, base + step * size + t]
@@ -345,9 +369,9 @@
             def _():
                 for h in range(WAYS):
                     x = xb[slot, h, t].astype(jnp.float32)
-                    for half in range(2):
+                    for half in BOTH:
                         mix[half, pl.ds(h, GRAN, stride=WAYS), :] = x[:, half * 128:(half + 1) * 128]
-                joined = jnp.concatenate([mix[half].astype(jnp.bfloat16) for half in range(2)], axis=1)
+                joined = beside([mix[half].astype(jnp.bfloat16) for half in BOTH])
                 ob[slot, t] = joined.reshape(GRAN, WAYS, 256)
                 write(i, t, slot).start()
 
@@ -391,11 +415,11 @@
     size = min(STEP, total)
     steps = total // size
     segments, at = [], 0
-    for entry, (_, _, offset, count) in enumerate(far):
+    for entry, (_, _, offsets, count) in enumerate(far):
         if count >= size:
-            segments.append((at // size, (at + count) // size, entry, offset, size, 0))
+            segments.append((at // size, (at + count) // size, entry, offsets, size, 0))
         else:
-            segments.append((at // size, at // size + 1, entry, offset, count, at % size))
+            segments.append((at // size, at // size + 1, entry, offsets, count, at % size))
         at += count
     whole = lambda *shape: pl.BlockSpec(shape, lambda i, *_: (0,) * len(shape))
     by_step = pl.BlockSpec((WAYS, 8, size * GRAN), lambda i, *_: (0, 0, base // size + i))
@@ -424,10 +448,53 @@
         ),
         out_shape=[jax.ShapeDtypeStruct(cache.shape, cache.dtype), jax.ShapeDtypeStruct(prev.shape, prev.dtype)],
         input_output_aliases=aliases,
-        compiler_params=pltpu.CompilerParams(dimension_semantics=("arbitrary",), vmem_limit_bytes=VMEM_LIMIT),
-        cost_estimate=pl.CostEstimate(flops=10_000_000, bytes_accessed=steps * 4_000_000, transcendentals=0),
+        compiler_params=SERIAL,
+        cost_estimate=cost(steps * 4_000_000),
         name="assemble_keys" if is_key else "assemble_values",
     )(codes, places, n, me, *[x for f in far for x in f[:2]], near, own, new, qp, prev, cache)
+
+
+def hand_back_kernel(table_ref, *refs):
+    outs, sem = refs[-3:-1], refs[-1]
+    arrays = refs[:-3]
+    units = len(arrays) // 2
+
+    def one(t, carry):
+        for u in range(units):
+            size = UNITS[u % len(UNITS)]
+
+            @pl.when(table_ref[0, t] == u)
+            def _():
+                for k in BOTH:
+                    for d in BOTH:
+                        pltpu.make_async_copy(arrays[2 * u + d].at[table_ref[1, t] + k * size], outs[k].at[d * HALF + t], sem).start()
+        return carry
+
+    def wait(t, carry):
+        @pl.when(table_ref[0, t] >= 0)
+        def _():
+            for k in BOTH:
+                for d in BOTH:
+                    pltpu.make_async_copy(outs[k].at[d * HALF + t], outs[k].at[d * HALF + t], sem).wait()
+
+        return carry
+
+    lax.fori_loop(0, HALF, one, 0)
+    lax.fori_loop(0, HALF, wait, 0)
+
+
+def hand_back(table, pairs):
+    arrays = [x for pair in pairs for x in pair]
+    return pl.pallas_call(
+        hand_back_kernel,
+        grid_spec=pltpu.PrefetchScalarGridSpec(
+            num_scalar_prefetch=1, grid=(1,), in_specs=[ANYWHERE] * len(arrays),
+            out_specs=[pl.BlockSpec((CROSS, GRAN, 256), lambda i, t_ref: (0, 0, 0))] * 2, scratch_shapes=[pltpu.SemaphoreType.DMA]),
+        out_shape=[jax.ShapeDtypeStruct((CROSS, GRAN, 256), jnp.bfloat16)] * 2,
+        compiler_params=pltpu.CompilerParams(vmem_limit_bytes=VMEM_LIMIT),
+        cost_estimate=cost(8_000_000),
+        name="hand_back",
+    )(table, *arrays)
 
 
 def solution(mesh):
@@ -437,6 +504,9 @@
 
     def send(x, d):
         return lax.ppermute(x, 'sh', [(i, i ^ d) for i in range(WAYS)])
+
+    def across(x):
+        return lax.ppermute(x, 'dp', [(0, 1), (1, 0)])
 
     def step(k_prefill, v_prefill, lengths, residual, norm_gain, w_query, w_key, w_value, w_out):
         seq_g = k_prefill.shape[1] // GRAN
@@ -450,20 +520,30 @@
             return Lists(jnp.stack([by_peer[d] for d in ds]), jnp.stack([(me ^ d) * ROWS for d in ds])[:, None], seq_g)
 
         def span(count):
-            return jnp.arange(count, dtype=jnp.int32)[None, :]
+            return lax.broadcasted_iota(jnp.int32, (1, count), 1)
 
         def held(which, i):
             src, mixed = which.source(i)
             valid = i < which.size
             return jnp.where(valid, src, 0), jnp.where(valid, mixed, -1)
 
-        far, far_other, close, self_list = lists(2, 3), lists(3, 2), lists(1, 0), lists(0)
+        far, close, self_list = lists(2, 3), lists(1, 0), lists(0)
         fixed_src, fixed_mix = held(far, span(FIXED))
         close_src, close_mix = held(close, span(ROWS * WIN_G))
 
-        sizes = jnp.sum(jnp.minimum(lengths // GRAN + 1, WIN_G).reshape(WAYS, ROWS), axis=1)
-        excess = jnp.max(jnp.sum(jnp.maximum(sizes - FIXED, 0).reshape(WAYS // 2, 2), axis=1))
-        level = lax.pmax((excess + 2 * QUANTUM - 1) // (2 * QUANTUM), 'dp')
+        chip, core = me // 2, me % 2
+
+        def rests(lens):
+            sizes = jnp.sum(jnp.minimum(lens // GRAN + 1, WIN_G).reshape(WAYS, ROWS), axis=1)
+            return jnp.maximum(sizes - FIXED, 0).reshape(WAYS // 2, 2)
+
+        def of_chip(x, c):
+            return jnp.where(c == 0, x[0], x[1])
+
+        other_lengths = across(lengths)
+        rest, other_rest = rests(lengths), rests(other_lengths)
+        need, other_need = jnp.sum(rest, axis=1), jnp.sum(other_rest, axis=1)
+        level = jnp.max(jnp.maximum((need + other_need + 4 * QUANTUM - 1) // (4 * QUANTUM), (jnp.maximum(need, other_need) - CROSS + 2 * QUANTUM - 1) // (2 * QUANTUM)))
         spare = QUANTUM * level
         on = active_units(level)
         column = span(SPARE)
@@ -473,23 +553,59 @@
             used = jnp.where(unit == u, on[u], used)
             place = jnp.where(unit == u, column - skipped, place)
             skipped = skipped + jnp.where(on[u], 0, size)
-        own_at, other_at = FIXED + place, FIXED + 2 * spare - 1 - place
-        src_a, mix_a = held(far, own_at)
-        src_b, mix_b = held(far_other, other_at)
-        is_own = used & (own_at < far.size)
-        is_other = used & (own_at >= far.size) & (other_at < far_other.size)
-        spare_src = jnp.where(is_own, src_a, jnp.where(is_other, src_b, 0))
-        spare_mix = jnp.where(is_own, mix_a, jnp.where(is_other, mix_b, -1))
+        far_n = lax.dynamic_slice_in_dim(lengths, (1 - chip) * 2 * ROWS, 2 * ROWS).reshape(2, ROWS)
+        far_lists = Lists(far_n, ((1 - chip) * 2 + jnp.arange(2, dtype=jnp.int32))[:, None] * ROWS, seq_g)
+        far_first, far_need = of_chip(rest, 1 - chip)[0], of_chip(need, 1 - chip)
+        far_guests = jnp.maximum(of_chip(other_need, 1 - chip) - 2 * spare, 0)
+
+        def from_rest(c):
+            second = c >= far_first
+            src, mixed = far_lists.source(FIXED + c - jnp.where(second, far_first, 0))
+            return tuple(jnp.where(second[0], x[1], x[0]) for x in (src, mixed))
+
+        both_used = beside([used, used])[0]
+        z = beside([place + (core ^ a) * spare for a in BOTH])
+        src, mixed = from_rest(z)
+        order = z[0] - far_need
+        hosted, guest = both_used & (order < 0), both_used & (order >= 0) & (order < far_guests)
+        spare_src = jnp.where(hosted, src, jnp.where(guest, ELSEWHERE + order, 0)).reshape(2, SPARE)
+        spare_mix = jnp.where(hosted, mixed, -1).reshape(2, SPARE)
+        z = 2 * spare + span(CROSS)
+        src, mixed = from_rest(z)
+        hosted = z[0] < far_need
+        cross_src, cross_mix = jnp.where(hosted, src, 0).reshape(2, HALF), jnp.where(hosted, mixed, -1).reshape(2, HALF)
+
+        own_first, own_need = of_chip(rest, chip)[0], of_chip(need, chip)
 
         def belongs(i, valid):
             r, g = self_list.at(i)
             return jnp.where(valid & (i < self_list.size), r * WIN_G + g, -1), jnp.clip(i, 0, ROWS * WIN_G - 1)
 
-        parts = [belongs(span(FIXED), True), belongs(own_at, used), belongs(other_at, used)]
-        codes = jnp.concatenate([p[0] for p in parts], axis=1)
-        places = jnp.concatenate([p[1] for p in parts], axis=1)
-
-        fixed_from, close_from, spare_from = FromTable(fixed_src, fixed_mix), FromTable(close_src, close_mix), FromTable(spare_src, spare_mix)
+        def rest_belongs(c, valid):
+            second = c >= own_first
+            return belongs(FIXED + c - jnp.where(second, own_first, 0), valid & (c < own_need) & (second == (core == 1)))
+
+        half_span = span(HALF)
+        parts = [belongs(span(FIXED), True), rest_belongs(place + core * spare, used), rest_belongs(place + (1 - core) * spare, used)]
+        parts += [rest_belongs(2 * spare + x * (HALF) + half_span, True) for x in (core, 1 - core)]
+        codes = beside([p[0] for p in parts])
+        places = beside([p[1] for p in parts])
+
+        w = core * (HALF) + half_span
+        z = own_need + w
+        high = (z >= spare).astype(jnp.int32)
+        u = z - high * spare
+        back_unit, back_at, begin = jnp.full_like(u, -1), jnp.zeros_like(u), 0
+        for k, size in enumerate(UNITS):
+            inside = (u >= begin) & (u < begin + jnp.where(on[k], size, 0))
+            back_unit = jnp.where(inside, k, back_unit)
+            back_at = jnp.where(inside, u - begin, back_at)
+            begin = begin + jnp.where(on[k], size, 0)
+        back_unit = jnp.where(w < jnp.maximum(of_chip(other_need, chip) - 2 * spare, 0), back_unit + len(UNITS) * (high != core).astype(jnp.int32), -1)
+        back_table = jnp.concatenate([back_unit, back_at], axis=0)
+
+        fixed_from, close_from = FromTable(fixed_src, fixed_mix), FromTable(close_src, close_mix)
+        spare_from, cross_from = FromTable(spare_src, spare_mix), FromTable(cross_src, cross_mix)
         fixed_got = {True: [], False: []}
         packed_values = []
         for i, (base, count) in enumerate(zip(starts_of(K_PIECES), K_PIECES)):
@@ -497,11 +613,15 @@
             a = send(out[0], 2)
             b = send(out[1], 3)
             fixed_got[True].append((a, b))
+        cross = pack([prefill[True], prefill[False]], cross_from, 0, HALF)
+        guests = []
+        for e in BOTH:
+            guests.append(across(cross[e]))
         close_got = {}
-        for is_key in (True, False):
+        for is_key in KV:
             near, own = pack([prefill[is_key]], close_from, 0, ROWS * WIN_G)
             close_got[is_key] = (send(near, 1), own)
-        spare_packed = [pack([prefill[True], prefill[False]], spare_from, base, count) for base, count in zip(starts_of(UNITS), UNITS)]
+        spare_packed = [pack([prefill[True], prefill[False]], spare_from, base, count, guests) for base, count in zip(starts_of(UNITS), UNITS)]
         for base, count in zip(starts_of(V_PIECES), V_PIECES):
             packed_values.append(pack([prefill[False]], fixed_from, base, count))
 
@@ -537,6 +657,11 @@
             b = send(b, 3)
             fixed_got[False].append((a, b))
         forwarded = [(send(b, 1), send(a, 1)) for a, b in spare_got]
+        found = hand_back(back_table, spare_got + forwarded)
+        handed, handed_on = [], []
+        for k in BOTH:
+            handed.append(across(found[k]))
+            handed_on.append(send(handed[k], 1))
 
         me1 = me.reshape(1)
 
@@ -544,17 +669,24 @@
             return assemble(is_key, base, codes, places, mine, me1, far_parts, close_got[is_key][0], own[is_key], new[is_key], qp, prev, cache)
 
         def fixed(pieces, got):
-            return [(a, b, 0, count) for (a, b), count in zip(got, pieces)]
+            return [(a, b, (0, 0), count) for (a, b), count in zip(got, pieces)]
 
         def spares(is_key):
-            return [(a, b, 0 if is_key else count, count) for got in (spare_got, forwarded) for (a, b), count in zip(got, UNITS)]
+            return [(a, b, (0, 0) if is_key else (count, count), count) for got in (spare_got, forwarded) for (a, b), count in zip(got, UNITS)]
+
+        def returned(is_key):
+            own_half, other_half = handed[0 if is_key else 1], handed_on[0 if is_key else 1]
+            return [(own_half, own_half, (0, HALF), HALF), (other_half, other_half, (HALF, 0), HALF)]
+
 
         k_cache, scores = run(True, 0, fixed(K_PIECES, fixed_got[True]), q_pad, scores, k_cache)
         k_cache, scores = run(True, FIXED, spares(True), q_pad, scores, k_cache)
+        k_cache, scores = run(True, FIXED + 2 * SPARE, returned(True), q_pad, scores, k_cache)
         exp_scores = jnp.exp(scores - jnp.max(scores, axis=-1, keepdims=True))
         weights = (exp_scores / jnp.sum(exp_scores, axis=-1, keepdims=True)).astype(jnp.bfloat16)
         sums = jnp.zeros((WAYS, 8, 256), jnp.float32)
         v_cache, sums = run(False, FIXED, spares(False), weights, sums, v_cache)
+        v_cache, sums = run(False, FIXED + 2 * SPARE, returned(False), weights, sums, v_cache)
         for base, part in zip(starts_of(V_PIECES), fixed(V_PIECES, fixed_got[False])):
             v_cache, sums = run(False, base, [part], weights, sums, v_cache)
         attn_out = sums[:, :ROWS * q_group].astype(jnp.bfloat16).reshape(WAYS, ROWS, q_group * 256).transpose(1, 0, 2).reshape(ROWS, WAYS * q_group * 256)

time: 607 us -> 648 us (1.068)
  Pallas kernels: 174 us -> 188 us
  starting transfers between devices: 19.5 us -> 31.8 us
  other arithmetic: 13.6 us -> 25.6 us
  local copies, waits for them, and re-layouts: 9.2 us -> 16 us
    ppermute x26 -> x30, waiting for transfers between devices: 353 us -> 290 us  [send(): return lax.ppermute(x, 'sh', [(i, i ^ d) for i in range(WAYS)])]
    ppermute x0 -> x5, waiting for transfers between devices: none -> 59.5 us  [across(): return lax.ppermute(x, 'dp', [(0, 1), (1, 0)])]
    pallas_call x13 -> x15, Pallas kernels: 89.8 us -> 98.9 us  [the longest x14 94.9 us: pack(): pl.pallas_call(functools.partial(pack_kernel, base, size, steps, source,...]
    ppermute x26 -> x30, starting transfers between devices: 19.5 us -> 25.6 us  [send(): return lax.ppermute(x, 'sh', [(i, i ^ d) for i in range(WAYS)])]
    pallas_call x6 -> x8, Pallas kernels: 77.6 us -> 82.4 us  [assemble(): pl.pallas_call(functools.partial(assemble_kernel, is_key, base, size, ste...]
  transfers between devices with their start and end apart: 26 -> 35, of which waited for: 12 -> 18; matrix products, arithmetic and copies ran while one was open for 1% -> 7% of each run, Pallas kernels for 15% -> 24%
where the time goes in v3:
time: 648 us; the launch traced here: 641 us
  waiting for transfers between devices  349 us (54%)
  Pallas kernels  188 us (29%)
  starting transfers between devices  31.8 us (5%)
  other arithmetic  25.6 us (4%)
  matrix products  16.9 us (3%)
  local copies, waits for them, and re-layouts  16 us (2%)
  between operations  13.5 us (2%)
    ppermute x30, waiting for transfers between devices, send(): return lax.ppermute(x, 'sh', [(i, i ^ d) for i in range(WAYS)])  290 us
    pallas_call x14, Pallas kernels, pack(): pl.pallas_call(functools.partial(pack_kernel, base, size, steps, source,...  94.9 us
    pallas_call x8, Pallas kernels, assemble(): pl.pallas_call(functools.partial(assemble_kernel, is_key, base, size, ste...  82.4 us
    ppermute x5, waiting for transfers between devices, across(): return lax.ppermute(x, 'dp', [(0, 1), (1, 0)])  59.5 us
    ppermute x30, starting transfers between devices, send(): return lax.ppermute(x, 'sh', [(i, i ^ d) for i in range(WAYS)])  25.6 us
  transfers between devices with their start and end apart: 35, of which 18 were waited for; matrix products, arithmetic and copies ran while one was open for 7% of the time, Pallas kernels for 24%

profile of v3, /device:TPU:0, one launch (start us, length us, event | category | flops | bytes accessed | tf_op | source)
XLA Modules:
  0.0 640.6 jit_solution(2995495525663517644)
XLA Ops:
  0.6 3.4 collective-permute-start.74
  12.9 8.4 %pack.20 = (bf16[96,64,256]{2,1,0:T(8,128)(2,1)}, bf16[96,64,256]{2,1,0:T(8,128)(2,1)}) custom-call(s32[2,128]{1,0:T(2,128)} %get-tuple-element.472.refs_0_, s32[2,128]{1,0:T(2,128)} %get-tuple-element.471.refs_1_, bf16[1920,64,256]{2,1,0:T(8,128)(2,1)} %bitcast.41), custom_call_target="tpu_custom_call" | custom-call | flops 10000000 | bytes 12480000 | tf_op jit(solution)/shard_map/pack/pallas_call | solution.py:267
  21.4 3.8 pack.21
  25.2 2.7 pack.22
  29.9 15.4 %pack.24 = (bf16[192,64,256]{2,1,0:T(8,128)(2,1)}, bf16[192,64,256]{2,1,0:T(8,128)(2,1)}) custom-call(s32[2,192]{1,0:T(2,128)} %get-tuple-element.470.refs_0_, s32[2,192]{1,0:T(2,128)} %get-tuple-element.469.refs_1_, bf16[1920,64,256]{2,1,0:T(8,128)(2,1)} %bitcast.44), custom_call_target="tpu_custom_call" | custom-call | flops 10000000 | bytes 24960000 | tf_op jit(solution)/shard_map/pack/pallas_call | solution.py:267
  45.3 18.0 %pack.23 = (bf16[192,64,256]{2,1,0:T(8,128)(2,1)}, bf16[192,64,256]{2,1,0:T(8,128)(2,1)}) custom-call(s32[2,192]{1,0:T(2,128)} %get-tuple-element.470.refs_0_, s32[2,192]{1,0:T(2,128)} %get-tuple-element.469.refs_1_, bf16[1920,64,256]{2,1,0:T(8,128)(2,1)} %bitcast.51), custom_call_target="tpu_custom_call" | custom-call | flops 10000000 | bytes 24960000 | tf_op jit(solution)/shard_map/pack/pallas_call | solution.py:267
  63.3 4.0 pack.26
  73.9 5.1 convolution_convert_fusion
  79.8 3.1 convolution_convert_fusion.1
  84.2 6.3 cleared.1
  90.7 3.1 fusion.2
  105.3 6.1 pack.14
  111.5 2.0 collective-permute-start.76
  121.6 16.3 %collective-permute-done.75.refs_4_ = bf16[32,64,256]{2,1,0:T(8,128)(2,1)} collective-permute-done((bf16[32,64,256]{2,1,0:T(8,128)(2,1)}, bf16[32,64,256]{2,1,0:T(8,128)(2,1)}, u32[]{:S(2)}, u32[]{:S(2)}) %collective-permute-start.75) | collective-permute-done | bytes 1048608 | tf_op jit(solution)/shard_map/ppermute | solution.py:509
  137.8 18.5 %collective-permute-done.76.refs_5_ = bf16[32,64,256]{2,1,0:T(8,128)(2,1)} collective-permute-done((bf16[32,64,256]{2,1,0:T(8,128)(2,1)}, bf16[32,64,256]{2,1,0:T(8,128)(2,1)}, u32[]{:S(2)}, u32[]{:S(2)}) %collective-permute-start.76) | collective-permute-done | bytes 1048608 | tf_op jit(solution)/shard_map/ppermute | solution.py:509
  156.3 5.2 pack.16
  161.5 9.8 %pack.15 = (bf16[64,64,256]{2,1,0:T(8,128)(2,1)}, bf16[64,64,256]{2,1,0:T(8,128)(2,1)}) custom-call(s32[2,64]{1,0:T(2,128)} %get-tuple-element.486.refs_0_, s32[2,64]{1,0:T(2,128)} %get-tuple-element.485.refs_1_, bf16[1920,64,256]{2,1,0:T(8,128)(2,1)} %bitcast.55, bf16[1920,64,256]{2,1,0:T(8,128)(2,1)} %bitcast.47, ...), custom_call_target="tpu_custom_call" | custom-call | flops 10000000 | bytes 8320000 | tf_op jit(solution)/shard_map/pack/pallas_call | solution.py:267
  171.3 3.6 pack.17
  174.9 3.0 pack.18
  177.9 3.0 pack.19
  180.9 67.7 %conditional.1 = (bf16[64,64,256]{2,1,0:T(8,128)(2,1)}, bf16[64,64,256]{2,1,0:T(8,128)(2,1)}, bf16[32,64,256]{2,1,0:T(8,128)(2,1)}, bf16[32,64,256]{2,1,0:T(8,12...) conditional(s32[]{:T(128)} %clamp.48, () %tuple.78, ...), branch_computations={%region_6.7_spmd, %region_7.8_spmd, %region_8.9_spmd, %region_9.10... | conditional | bytes 33554912 | solution.py:653
  180.9 4.7 collective-permute-start.14
  187.3 56.3 %collective-permute-done.16 = bf16[16,64,256]{2,1,0:T(8,128)(2,1)} collective-permute-done((bf16[16,64,256]{2,1,0:T(8,128)(2,1)}, bf16[16,64,256]{2,1,0:T(8,128)(2,1)}, u32[]{:S(2)}, u32[]{:S(2)}) %collective-permute-start.16) | collective-permute-done | bytes 524320 | tf_op jit(solution)/shard_map/cond/branch_6_fun/ppermute | solution.py:506
  243.6 5.0 collective-permute-done.17
  250.8 3.2 pack.25
  255.7 36.2 %collective-permute-done.93.refs_0_ = bf16[8,64,256]{2,1,0:T(8,128)(2,1)} collective-permute-done((bf16[8,64,256]{2,1,0:T(8,128)(2,1)}, bf16[8,64,256]{2,1,0:T(8,128)(2,1)}, u32[]{:S(2)}, u32[]{:S(2)}) %collective-permute-start.93) | collective-permute-done | bytes 262176 | tf_op jit(solution)/shard_map/ppermute | solution.py:506
  291.8 4.8 collective-permute-done.94.refs_1_
  301.5 8.8 %pack.27 = (bf16[96,64,256]{2,1,0:T(8,128)(2,1)}, bf16[96,64,256]{2,1,0:T(8,128)(2,1)}) custom-call(s32[2,128]{1,0:T(2,128)} %get-tuple-element.472.refs_0_, s32[2,128]{1,0:T(2,128)} %get-tuple-element.471.refs_1_, bf16[1920,64,256]{2,1,0:T(8,128)(2,1)} %bitcast.60), custom_call_target="tpu_custom_call" | custom-call | flops 10000000 | bytes 12480000 | tf_op jit(solution)/shard_map/pack/pallas_call | solution.py:267
  310.3 2.1 collective-permute-done.82.refs_12_
  315.1 10.8 %collective-permute-done.81.refs_11_ = bf16[64,64,256]{2,1,0:T(8,128)(2,1)} collective-permute-done((bf16[64,64,256]{2,1,0:T(8,128)(2,1)}, bf16[64,64,256]{2,1,0:T(8,128)(2,1)}, u32[]{:S(2)}, u32[]{:S(2)}) %collective-permute-start.81) | collective-permute-done | bytes 2097184 | tf_op jit(solution)/shard_map/ppermute | solution.py:506
  328.9 4.0 hand_back.1
  332.9 50.8 %collective-permute-done.97.refs_4_ = bf16[96,64,256]{2,1,0:T(8,128)(2,1)} collective-permute-done((bf16[96,64,256]{2,1,0:T(8,128)(2,1)}, bf16[96,64,256]{2,1,0:T(8,128)(2,1)}, u32[]{:S(2)}, u32[]{:S(2)}) %collective-permute-start.97) | collective-permute-done | bytes 3145760 | tf_op jit(solution)/shard_map/ppermute | solution.py:506
  384.1 65.6 %collective-permute-done.98.refs_5_ = bf16[96,64,256]{2,1,0:T(8,128)(2,1)} collective-permute-done((bf16[96,64,256]{2,1,0:T(8,128)(2,1)}, bf16[96,64,256]{2,1,0:T(8,128)(2,1)}, u32[]{:S(2)}, u32[]{:S(2)}) %collective-permute-start.98) | collective-permute-done | bytes 3145760 | tf_op jit(solution)/shard_map/ppermute | solution.py:506
  451.0 24.7 %collective-permute-done.103.refs_0_.refs_1_ = bf16[32,64,256]{2,1,0:T(8,128)(2,1)} collective-permute-done((bf16[32,64,256]{2,1,0:T(8,128)(2,1)}, bf16[32,64,256]{2,1,0:T(8,128)(2,1)}, u32[]{:S(2)}, u32[]{:S(2)}) %collective-permute-start.103) | collective-permute-done | bytes 1048608 | tf_op jit(solution)/shard_map/ppermute | solution.py:509
  483.8 27.1 %assemble_keys.3 = (bf16[3,4096,4,256]{3,2,1,0:T(4,128)(2,1)}, f32[4,8,18432]{2,1,0:T(8,128)}) custom-call(s32[1,288]{1,0:T(1,128)} %concatenate.48.code_ref, s32[1,288]{1,0:T(1,128)} %concatenate.49.idx_ref, s32[3]{0:T(128)} %get-tuple-element.496.n_ref, s32[1]{0:T(128)} %bitcast.8.me_ref, ...), custom_call_target="tpu_custom_call", output_to_operand_aliasing={{0}: (15, {}), {1}: (14, {})} | custom-call | flops 10000000 | bytes 64000000 | tf_op jit(solution)/shard_map/assemble_keys/pallas_call | solution.py:434
  510.9 8.3 %assemble_keys.4 = (bf16[3,4096,4,256]{3,2,1,0:T(4,128)(2,1)}, f32[4,8,18432]{2,1,0:T(8,128)}) custom-call(s32[1,288]{1,0:T(1,128)} %concatenate.48.code_ref, s32[1,288]{1,0:T(1,128)} %concatenate.49.idx_ref, s32[3]{0:T(128)} %get-tuple-element.496.n_ref, s32[1]{0:T(128)} %bitcast.8.me_ref, ...), custom_call_target="tpu_custom_call", output_to_operand_aliasing={{0}: (29, {}), {1}: (28, {})} | custom-call | flops 10000000 | bytes 64000000 | tf_op jit(solution)/shard_map/assemble_keys/pallas_call | solution.py:434
  520.8 3.0 assemble_keys.5
  523.8 2.1 reduce_max.19
  526.7 6.4 collective-permute-start.99
  535.2 8.8 %assemble_values.5 = (bf16[3,4096,4,256]{3,2,1,0:T(4,128)(2,1)}, f32[4,8,256]{2,1,0:T(8,128)}) custom-call(s32[1,288]{1,0:T(1,128)} %concatenate.48.code_ref, s32[1,288]{1,0:T(1,128)} %concatenate.49.idx_ref, s32[3]{0:T(128)} %get-tuple-element.496.n_ref, s32[1]{0:T(128)} %bitcast.8.me_ref, ...), custom_call_target="tpu_custom_call", output_to_operand_aliasing={{0}: (29, {})} | custom-call | flops 10000000 | bytes 64000000 | tf_op jit(solution)/shard_map/assemble_values/pallas_call | solution.py:434
  544.1 3.0 assemble_values.6
  547.0 37.5 %collective-permute-done.102.refs_1_ = bf16[96,64,256]{2,1,0:T(8,128)(2,1)} collective-permute-done((bf16[96,64,256]{2,1,0:T(8,128)(2,1)}, bf16[96,64,256]{2,1,0:T(8,128)(2,1)}, u32[]{:S(2)}, u32[]{:S(2)}) %collective-permute-start.102) | collective-permute-done | bytes 3145760 | tf_op jit(solution)/shard_map/ppermute | solution.py:506
  584.5 20.0 %assemble_values.7 = (bf16[3,4096,4,256]{3,2,1,0:T(4,128)(2,1)}, f32[4,8,256]{2,1,0:T(8,128)}) custom-call(s32[1,288]{1,0:T(1,128)} %concatenate.48.code_ref, s32[1,288]{1,0:T(1,128)} %concatenate.49.idx_ref, s32[3]{0:T(128)} %get-tuple-element.496.n_ref, s32[1]{0:T(128)} %bitcast.8.me_ref, ...), custom_call_target="tpu_custom_call", output_to_operand_aliasing={{0}: (11, {})} | custom-call | flops 10000000 | bytes 48000000 | tf_op jit(solution)/shard_map/assemble_values/pallas_call | solution.py:434
  604.6 15.1 %collective-permute-done.99.refs_0_ = bf16[24,64,256]{2,1,0:T(8,128)(2,1)} collective-permute-done((bf16[24,64,256]{2,1,0:T(8,128)(2,1)}, bf16[24,64,256]{2,1,0:T(8,128)(2,1)}, u32[]{:S(2)}, u32[]{:S(2)}) %collective-permute-start.99) | collective-permute-done | bytes 786464 | tf_op jit(solution)/shard_map/ppermute | solution.py:506
  619.6 7.4 %assemble_values.8 = (bf16[3,4096,4,256]{3,2,1,0:T(4,128)(2,1)}, f32[4,8,256]{2,1,0:T(8,128)}) custom-call(s32[1,288]{1,0:T(1,128)} %concatenate.48.code_ref, s32[1,288]{1,0:T(1,128)} %concatenate.49.idx_ref, s32[3]{0:T(128)} %get-tuple-element.496.n_ref, s32[1]{0:T(128)} %bitcast.8.me_ref, ...), custom_call_target="tpu_custom_call", output_to_operand_aliasing={{0}: (11, {})} | custom-call | flops 10000000 | bytes 12000000 | tf_op jit(solution)/shard_map/assemble_values/pallas_call | solution.py:434
  627.1 2.3 collective-permute-done.78.refs_1_
  629.4 4.8 assemble_values.9
  635.0 5.6 fusion
  (211 shorter events, 58.0 us)
Async XLA Ops:
  0.6 96.8 %collective-permute-start.74 = (s32[12]{0:T(128)}, s32[12]{0:T(128)}, u32[]{:S(2)}, u32[]{:S(2)}) collective-permute-start(s32[12]{0:T(128)} %refs_0_.1), channel_id=1, source_target_pairs={{0,4},{4,0},{1,5},{5,1},{2,6},{6,2},{3,7},{7,3}} | collective-permute-start | bytes 152 | tf_op jit(solution)/shard_map/ppermute | solution.py:509
  73.0 6.8 %copy-start.2 = (f32[2304]{0:T(1024)}, f32[2304]{0:T(1024)S(1)}, u32[]{:S(2)}) copy-start(f32[2304]{0:T(1024)S(1)} %convert_element_type.522) | copy-start | bytes 27652
  90.5 6.3 copy-start.4
  90.6 8.0 %copy-start.22 = (s32[2]{0:T(128)S(1)}, s32[2]{0:T(128)}, u32[]{:S(2)}) copy-start(s32[2]{0:T(128)} %copy-done.21) | copy-start | bytes 28
  90.6 13.0 %copy-start.9 = (s32[2]{0:T(128)S(1)}, s32[2]{0:T(128)}, u32[]{:S(2)}) copy-start(s32[2]{0:T(128)} %get-tuple-element.497) | copy-start | bytes 28
  90.6 13.1 %copy-start.13 = (s32[2]{0:T(128)S(1)}, s32[2]{0:T(128)}, u32[]{:S(2)}) copy-start(s32[2]{0:T(128)} %get-tuple-element.447) | copy-start | bytes 28
  90.6 13.1 %copy-start.14 = (s32[2]{0:T(128)S(1)}, s32[2]{0:T(128)}, u32[]{:S(2)}) copy-start(s32[2]{0:T(128)} %get-tuple-element.448) | copy-start | bytes 28
  90.6 13.1 %copy-start.15 = (s32[2]{0:T(128)S(1)}, s32[2]{0:T(128)}, u32[]{:S(2)}) copy-start(s32[2]{0:T(128)} %get-tuple-element.449) | copy-start | bytes 28
  90.6 13.1 %copy-start.16 = (s32[2]{0:T(128)S(1)}, s32[2]{0:T(128)}, u32[]{:S(2)}) copy-start(s32[2]{0:T(128)} %get-tuple-element.452) | copy-start | bytes 28
  90.6 13.1 %copy-start.17 = (s32[2]{0:T(128)S(1)}, s32[2]{0:T(128)}, u32[]{:S(2)}) copy-start(s32[2]{0:T(128)} %get-tuple-element.453) | copy-start | bytes 28
  90.6 13.1 %copy-start.18 = (s32[2]{0:T(128)S(1)}, s32[2]{0:T(128)}, u32[]{:S(2)}) copy-start(s32[2]{0:T(128)} %get-tuple-element.454) | copy-start | bytes 28
  90.6 13.1 %copy-start.19 = (s32[2]{0:T(128)S(1)}, s32[2]{0:T(128)}, u32[]{:S(2)}) copy-start(s32[2]{0:T(128)} %get-tuple-element.450) | copy-start | bytes 28
  90.6 13.1 %copy-start.20 = (s32[2]{0:T(128)S(1)}, s32[2]{0:T(128)}, u32[]{:S(2)}) copy-start(s32[2]{0:T(128)} %get-tuple-element.451) | copy-start | bytes 28
  90.7 13.1 %copy-start.23 = (s32[2]{0:T(128)S(1)}, s32[2]{0:T(128)}, u32[]{:S(2)}) copy-start(s32[2]{0:T(128)} %add_multiply_fusion.4) | copy-start | bytes 28
  111.4 26.4 %collective-permute-start.75 = (bf16[32,64,256]{2,1,0:T(8,128)(2,1)}, bf16[32,64,256]{2,1,0:T(8,128)(2,1)}, u32[]{:S(2)}, u32[]{:S(2)}) collective-permute-start(bf16[32,64,256]{2,1,0:T(8,128)(2,1)} %get-tuple-element.323), channel_id=1, source_target_pairs={{0,4},{4,0},{1,5},{5,1},{2,6},{6,2},{3,7},{7,3}} | collective-permute-start | bytes 3145736 | tf_op jit(solution)/shard_map/ppermute | solution.py:509
  111.5 44.8 %collective-permute-start.76 = (bf16[32,64,256]{2,1,0:T(8,128)(2,1)}, bf16[32,64,256]{2,1,0:T(8,128)(2,1)}, u32[]{:S(2)}, u32[]{:S(2)}) collective-permute-start(bf16[32,64,256]{2,1,0:T(8,128)(2,1)} %get-tuple-element.324), channel_id=1, source_target_pairs={{0,4},{4,0},{1,5},{5,1},{2,6},{6,2},{3,7},{7,3}} | collective-permute-start | bytes 3145736 | tf_op jit(solution)/shard_map/ppermute | solution.py:509
  180.9 67.7 %collective-permute-start.14 = (bf16[32,64,256]{2,1,0:T(8,128)(2,1)}, bf16[32,64,256]{2,1,0:T(8,128)(2,1)}, u32[]{:S(2)}, u32[]{:S(2)}) collective-permute-start(bf16[32,64,256]{2,1,0:T(8,128)(2,1)} %get-tuple-element.162), channel_id=1, source_target_pairs={{0,2},{1,3},{2,0},{3,1},{4,6},{5,7},{6,4},{7,5}} | collective-permute-start | bytes 3145736 | tf_op jit(solution)/shard_map/cond/branch_6_fun/ppermute | solution.py:506
  185.6 63.0 %collective-permute-start.15 = (bf16[32,64,256]{2,1,0:T(8,128)(2,1)}, bf16[32,64,256]{2,1,0:T(8,128)(2,1)}, u32[]{:S(2)}, u32[]{:S(2)}) collective-permute-start(bf16[32,64,256]{2,1,0:T(8,128)(2,1)} %get-tuple-element.163), channel_id=1, source_target_pairs={{0,3},{1,2},{2,1},{3,0},{4,7},{5,6},{6,5},{7,4}} | collective-permute-start | bytes 3145736 | tf_op jit(solution)/shard_map/cond/branch_6_fun/ppermute | solution.py:506
  185.6 58.0 %collective-permute-start.16 = (bf16[16,64,256]{2,1,0:T(8,128)(2,1)}, bf16[16,64,256]{2,1,0:T(8,128)(2,1)}, u32[]{:S(2)}, u32[]{:S(2)}) collective-permute-start(bf16[16,64,256]{2,1,0:T(8,128)(2,1)} %get-tuple-element.164), channel_id=1, source_target_pairs={{0,2},{1,3},{2,0},{3,1},{4,6},{5,7},{6,4},{7,5}} | collective-permute-start | bytes 1572872 | tf_op jit(solution)/shard_map/cond/branch_6_fun/ppermute | solution.py:506
  185.7 62.9 %collective-permute-start.17 = (bf16[16,64,256]{2,1,0:T(8,128)(2,1)}, bf16[16,64,256]{2,1,0:T(8,128)(2,1)}, u32[]{:S(2)}, u32[]{:S(2)}) collective-permute-start(bf16[16,64,256]{2,1,0:T(8,128)(2,1)} %get-tuple-element.165), channel_id=1, source_target_pairs={{0,3},{1,2},{2,1},{3,0},{4,7},{5,6},{6,5},{7,4}} | collective-permute-start | bytes 1572872 | tf_op jit(solution)/shard_map/cond/branch_6_fun/ppermute | solution.py:506
  248.6 48.3 %collective-permute-start.95 = (bf16[24,64,256]{2,1,0:T(8,128)(2,1)}, bf16[24,64,256]{2,1,0:T(8,128)(2,1)}, u32[]{:S(2)}, u32[]{:S(2)}) collective-permute-start(bf16[24,64,256]{2,1,0:T(8,128)(2,1)} %get-tuple-element.393), channel_id=1, source_target_pairs={{0,2},{1,3},{2,0},{3,1},{4,6},{5,7},{6,4},{7,5}} | collective-permute-start | bytes 2359304 | tf_op jit(solution)/shard_map/ppermute | solution.py:506
  248.9 48.3 %collective-permute-start.96 = (bf16[24,64,256]{2,1,0:T(8,128)(2,1)}, bf16[24,64,256]{2,1,0:T(8,128)(2,1)}, u32[]{:S(2)}, u32[]{:S(2)}) collective-permute-start(bf16[24,64,256]{2,1,0:T(8,128)(2,1)} %get-tuple-element.394), channel_id=1, source_target_pairs={{0,3},{1,2},{2,1},{3,0},{4,7},{5,6},{6,5},{7,4}} | collective-permute-start | bytes 2359304 | tf_op jit(solution)/shard_map/ppermute | solution.py:506
  250.6 63.5 %collective-permute-start.80 = (bf16[64,64,256]{2,1,0:T(8,128)(2,1)}, bf16[64,64,256]{2,1,0:T(8,128)(2,1)}, u32[]{:S(2)}, u32[]{:S(2)}) collective-permute-start(bf16[64,64,256]{2,1,0:T(8,128)(2,1)} %get-tuple-element.377.refs_1_), channel_id=1, source_target_pairs={{0,1},{1,0},{2,3},{3,2},{4,5},{5,4},{6,7},{7,6}} | collective-permute-start | bytes 6291464 | tf_op jit(solution)/shard_map/ppermute | solution.py:506
  254.0 37.9 %collective-permute-start.93 = (bf16[8,64,256]{2,1,0:T(8,128)(2,1)}, bf16[8,64,256]{2,1,0:T(8,128)(2,1)}, u32[]{:S(2)}, u32[]{:S(2)}) collective-permute-start(bf16[8,64,256]{2,1,0:T(8,128)(2,1)} %get-tuple-element.391), channel_id=1, source_target_pairs={{0,2},{1,3},{2,0},{3,1},{4,6},{5,7},{6,4},{7,5}} | collective-permute-start | bytes 786440 | tf_op jit(solution)/shard_map/ppermute | solution.py:506
  255.5 41.1 %collective-permute-start.94 = (bf16[8,64,256]{2,1,0:T(8,128)(2,1)}, bf16[8,64,256]{2,1,0:T(8,128)(2,1)}, u32[]{:S(2)}, u32[]{:S(2)}) collective-permute-start(bf16[8,64,256]{2,1,0:T(8,128)(2,1)} %get-tuple-element.392), channel_id=1, source_target_pairs={{0,3},{1,2},{2,1},{3,0},{4,7},{5,6},{6,5},{7,4}} | collective-permute-start | bytes 786440 | tf_op jit(solution)/shard_map/ppermute | solution.py:506
  291.8 5.6 collective-permute-start.86
  296.6 1.9 collective-permute-start.87
  296.9 4.1 collective-permute-start.84
  297.2 4.1 collective-permute-start.85
  297.4 3.0 collective-permute-start.88
  298.5 2.2 collective-permute-start.89
  300.4 182.8 %collective-permute-start.92 = (bf16[192,64,256]{2,1,0:T(8,128)(2,1)}, bf16[192,64,256]{2,1,0:T(8,128)(2,1)}, u32[]{:S(2)}, u32[]{:S(2)}) collective-permute-start(bf16[192,64,256]{2,1,0:T(8,128)(2,1)} %get-tuple-element.387), channel_id=1, source_target_pairs={{0,1},{1,0},{2,3},{3,2},{4,5},{5,4},{6,7},{7,6}} | collective-permute-start | bytes 18874376 | tf_op jit(solution)/shard_map/ppermute | solution.py:506
  300.8 11.6 %collective-permute-start.82 = (bf16[32,64,256]{2,1,0:T(8,128)(2,1)}, bf16[32,64,256]{2,1,0:T(8,128)(2,1)}, u32[]{:S(2)}, u32[]{:S(2)}) collective-permute-start(bf16[32,64,256]{2,1,0:T(8,128)(2,1)} %get-tuple-element.379.refs_3_), channel_id=1, source_target_pairs={{0,1},{1,0},{2,3},{3,2},{4,5},{5,4},{6,7},{7,6}} | collective-permute-start | bytes 3145736 | tf_op jit(solution)/shard_map/ppermute | solution.py:506
  301.0 12.9 %collective-permute-start.83 = (bf16[32,64,256]{2,1,0:T(8,128)(2,1)}, bf16[32,64,256]{2,1,0:T(8,128)(2,1)}, u32[]{:S(2)}, u32[]{:S(2)}) collective-permute-start(bf16[32,64,256]{2,1,0:T(8,128)(2,1)} %get-tuple-element.378.refs_2_), channel_id=1, source_target_pairs={{0,1},{1,0},{2,3},{3,2},{4,5},{5,4},{6,7},{7,6}} | collective-permute-start | bytes 3145736 | tf_op jit(solution)/shard_map/ppermute | solution.py:506
  301.3 231.8 %collective-permute-start.79 = (bf16[192,64,256]{2,1,0:T(8,128)(2,1)}, bf16[192,64,256]{2,1,0:T(8,128)(2,1)}, u32[]{:S(2)}, u32[]{:S(2)}) collective-permute-start(bf16[192,64,256]{2,1,0:T(8,128)(2,1)} %get-tuple-element.373), channel_id=1, source_target_pairs={{0,1},{1,0},{2,3},{3,2},{4,5},{5,4},{6,7},{7,6}} | collective-permute-start | bytes 18874376 | tf_op jit(solution)/shard_map/ppermute | solution.py:506
  312.4 71.3 %collective-permute-start.97 = (bf16[96,64,256]{2,1,0:T(8,128)(2,1)}, bf16[96,64,256]{2,1,0:T(8,128)(2,1)}, u32[]{:S(2)}, u32[]{:S(2)}) collective-permute-start(bf16[96,64,256]{2,1,0:T(8,128)(2,1)} %get-tuple-element.395), channel_id=1, source_target_pairs={{0,2},{1,3},{2,0},{3,1},{4,6},{5,7},{6,4},{7,5}} | collective-permute-start | bytes 9437192 | tf_op jit(solution)/shard_map/ppermute | solution.py:506
  313.9 12.0 %collective-permute-start.81 = (bf16[64,64,256]{2,1,0:T(8,128)(2,1)}, bf16[64,64,256]{2,1,0:T(8,128)(2,1)}, u32[]{:S(2)}, u32[]{:S(2)}) collective-permute-start(bf16[64,64,256]{2,1,0:T(8,128)(2,1)} %get-tuple-element.376.refs_0_), channel_id=1, source_target_pairs={{0,1},{1,0},{2,3},{3,2},{4,5},{5,4},{6,7},{7,6}} | collective-permute-start | bytes 6291464 | tf_op jit(solution)/shard_map/ppermute | solution.py:506
  314.1 135.6 %collective-permute-start.98 = (bf16[96,64,256]{2,1,0:T(8,128)(2,1)}, bf16[96,64,256]{2,1,0:T(8,128)(2,1)}, u32[]{:S(2)}, u32[]{:S(2)}) collective-permute-start(bf16[96,64,256]{2,1,0:T(8,128)(2,1)} %get-tuple-element.396), channel_id=1, source_target_pairs={{0,3},{1,2},{2,1},{3,0},{4,7},{5,6},{6,5},{7,4}} | collective-permute-start | bytes 9437192 | tf_op jit(solution)/shard_map/ppermute | solution.py:506
  325.9 200.8 %collective-permute-start.101 = (bf16[96,64,256]{2,1,0:T(8,128)(2,1)}, bf16[96,64,256]{2,1,0:T(8,128)(2,1)}, u32[]{:S(2)}, u32[]{:S(2)}) collective-permute-start(bf16[96,64,256]{2,1,0:T(8,128)(2,1)} %get-tuple-element.406), channel_id=1, source_target_pairs={{0,2},{1,3},{2,0},{3,1},{4,6},{5,7},{6,4},{7,5}} | collective-permute-start | bytes 9437192 | tf_op jit(solution)/shard_map/ppermute | solution.py:506
  383.7 66.4 %collective-permute-start.90 = (bf16[32,64,256]{2,1,0:T(8,128)(2,1)}, bf16[32,64,256]{2,1,0:T(8,128)(2,1)}, u32[]{:S(2)}, u32[]{:S(2)}) collective-permute-start(bf16[32,64,256]{2,1,0:T(8,128)(2,1)} %get-tuple-element.386), channel_id=1, source_target_pairs={{0,4},{4,0},{1,5},{5,1},{2,6},{6,2},{3,7},{7,3}} | collective-permute-start | bytes 3145736 | tf_op jit(solution)/shard_map/ppermute | solution.py:509
  449.7 26.1 %collective-permute-start.103 = (bf16[32,64,256]{2,1,0:T(8,128)(2,1)}, bf16[32,64,256]{2,1,0:T(8,128)(2,1)}, u32[]{:S(2)}, u32[]{:S(2)}) collective-permute-start(bf16[32,64,256]{2,1,0:T(8,128)(2,1)} %get-tuple-element.408), channel_id=1, source_target_pairs={{0,4},{4,0},{1,5},{5,1},{2,6},{6,2},{3,7},{7,3}} | collective-permute-start | bytes 3145736 | tf_op jit(solution)/shard_map/ppermute | solution.py:509
  450.1 69.2 %collective-permute-start.91 = (bf16[32,64,256]{2,1,0:T(8,128)(2,1)}, bf16[32,64,256]{2,1,0:T(8,128)(2,1)}, u32[]{:S(2)}, u32[]{:S(2)}) collective-permute-start(bf16[32,64,256]{2,1,0:T(8,128)(2,1)} %collective-permute-done.90.refs_0_.refs_1_), channel_id=1, source_target_pairs={{0,1},{1,0},{2,3},{3,2},{4,5},{5,4},{6,7},{7,6}} | collective-permute-start | bytes 3145736 | tf_op jit(solution)/shard_map/ppermute | solution.py:506
  475.8 57.3 %collective-permute-start.104 = (bf16[32,64,256]{2,1,0:T(8,128)(2,1)}, bf16[32,64,256]{2,1,0:T(8,128)(2,1)}, u32[]{:S(2)}, u32[]{:S(2)}) collective-permute-start(bf16[32,64,256]{2,1,0:T(8,128)(2,1)} %collective-permute-done.103.refs_0_.refs_1_), channel_id=1, source_target_pairs={{0,1},{1,0},{2,3},{3,2},{4,5},{5,4},{6,7},{7,6}} | collective-permute-start | bytes 3145736 | tf_op jit(solution)/shard_map/ppermute | solution.py:506
  483.2 101.3 %collective-permute-start.102 = (bf16[96,64,256]{2,1,0:T(8,128)(2,1)}, bf16[96,64,256]{2,1,0:T(8,128)(2,1)}, u32[]{:S(2)}, u32[]{:S(2)}) collective-permute-start(bf16[96,64,256]{2,1,0:T(8,128)(2,1)} %get-tuple-element.407), channel_id=1, source_target_pairs={{0,3},{1,2},{2,1},{3,0},{4,7},{5,6},{6,5},{7,4}} | collective-permute-start | bytes 9437192 | tf_op jit(solution)/shard_map/ppermute | solution.py:506
  519.3 85.3 %collective-permute-start.100 = (bf16[24,64,256]{2,1,0:T(8,128)(2,1)}, bf16[24,64,256]{2,1,0:T(8,128)(2,1)}, u32[]{:S(2)}, u32[]{:S(2)}) collective-permute-start(bf16[24,64,256]{2,1,0:T(8,128)(2,1)} %get-tuple-element.405), channel_id=1, source_target_pairs={{0,3},{1,2},{2,1},{3,0},{4,7},{5,6},{6,5},{7,4}} | collective-permute-start | bytes 2359304 | tf_op jit(solution)/shard_map/ppermute | solution.py:506
  526.7 92.9 %collective-permute-start.99 = (bf16[24,64,256]{2,1,0:T(8,128)(2,1)}, bf16[24,64,256]{2,1,0:T(8,128)(2,1)}, u32[]{:S(2)}, u32[]{:S(2)}) collective-permute-start(bf16[24,64,256]{2,1,0:T(8,128)(2,1)} %get-tuple-element.404), channel_id=1, source_target_pairs={{0,2},{1,3},{2,0},{3,1},{4,6},{5,7},{6,4},{7,5}} | collective-permute-start | bytes 2359304 | tf_op jit(solution)/shard_map/ppermute | solution.py:506
  533.1 94.0 %collective-permute-start.77 = (bf16[8,64,256]{2,1,0:T(8,128)(2,1)}, bf16[8,64,256]{2,1,0:T(8,128)(2,1)}, u32[]{:S(2)}, u32[]{:S(2)}) collective-permute-start(bf16[8,64,256]{2,1,0:T(8,128)(2,1)} %get-tuple-element.371), channel_id=1, source_target_pairs={{0,2},{1,3},{2,0},{3,1},{4,6},{5,7},{6,4},{7,5}} | collective-permute-start | bytes 786440 | tf_op jit(solution)/shard_map/ppermute | solution.py:506
  533.1 96.2 %collective-permute-start.78 = (bf16[8,64,256]{2,1,0:T(8,128)(2,1)}, bf16[8,64,256]{2,1,0:T(8,128)(2,1)}, u32[]{:S(2)}, u32[]{:S(2)}) collective-permute-start(bf16[8,64,256]{2,1,0:T(8,128)(2,1)} %get-tuple-element.372), channel_id=1, source_target_pairs={{0,3},{1,2},{2,1},{3,0},{4,7},{5,6},{6,5},{7,4}} | collective-permute-start | bytes 786440 | tf_op jit(solution)/shard_map/ppermute | solution.py:506
  (13 other events, 52.5 us)

commit v4 on v3

--- a/solution.py
+++ b/solution.py
@@ -14,16 +14,16 @@
 GRAN = 64
 WIN_G = WINDOW // GRAN
 STEP = 8
-FIXED = 128
-UNITS = (32, 16, 8, 4, 4)
-SPARE = sum(UNITS)
+FIXED = 112
+UNITS = (64, 32, 16, 8, 4)
 QUANTUM = UNITS[-1]
-LEVELS = SPARE // QUANTUM + 1
-K_PIECES = (8, 24, 96)
-V_PIECES = (96, 24, 8)
-CROSS = 32
+SPARE = sum(UNITS) + QUANTUM
+K_PIECES = (8, 24, 80)
+V_PIECES = (80, 24, 8)
+CROSS = 48
 ELSEWHERE = 1 << 20
 WAYS, ROWS = 4, 3
+LEVELS = (ROWS * WIN_G - FIXED) // QUANTUM + 1
 VMEM_LIMIT = 67_043_328
 HALF = CROSS // 2
 KV = (True, False)
@@ -44,8 +44,7 @@
 
 
 def active_units(level):
-    full = level == LEVELS - 1
-    return [full | ((level & (size // QUANTUM)) != 0) for size in UNITS[:-1]] + [full]
+    return [(level & (size // QUANTUM)) != 0 for size in UNITS]
 
 
 def rotate(heads, positions):
@@ -553,6 +552,7 @@
             used = jnp.where(unit == u, on[u], used)
             place = jnp.where(unit == u, column - skipped, place)
             skipped = skipped + jnp.where(on[u], 0, size)
+        used = used & (column < sum(UNITS))
         far_n = lax.dynamic_slice_in_dim(lengths, (1 - chip) * 2 * ROWS, 2 * ROWS).reshape(2, ROWS)
         far_lists = Lists(far_n, ((1 - chip) * 2 + jnp.arange(2, dtype=jnp.int32))[:, None] * ROWS, seq_g)
         far_first, far_need = of_chip(rest, 1 - chip)[0], of_chip(need, 1 - chip)
@@ -647,8 +647,8 @@
 
             return run
 
-        spare_packed, packed_values, ready = lax.optimization_barrier((spare_packed, packed_values, (new, q_pad, k_cache, v_cache, scores, close_got[True][1], close_got[False][1])))
-        new, q_pad, k_cache, v_cache, scores, own_k, own_v = ready
+        spare_packed, packed_values, ready = lax.optimization_barrier((spare_packed, packed_values, (new, q_pad, scores, close_got[True][1], close_got[False][1])))
+        new, q_pad, scores, own_k, own_v = ready
         own = {True: own_k, False: own_v}
         spare_got = lax.switch(level, [branch(x) for x in range(LEVELS)], spare_packed)
         spare_got, packed_values = lax.optimization_barrier((spare_got, packed_values))
@@ -672,7 +672,11 @@
             return [(a, b, (0, 0), count) for (a, b), count in zip(got, pieces)]
 
         def spares(is_key):
-            return [(a, b, (0, 0) if is_key else (count, count), count) for got in (spare_got, forwarded) for (a, b), count in zip(got, UNITS)]
+            runs = []
+            for got in (spare_got, forwarded):
+                runs += [(a, b, (0, 0) if is_key else (count, count), count) for (a, b), count in zip(got, UNITS)]
+                runs.append(runs[-1])
+            return runs
 
         def returned(is_key):
             own_half, other_half = handed[0 if is_key else 1], handed_on[0 if is_key else 1]

time: 648 us -> 730 us (1.13)
  the two profiles are of different devices: /device:TPU:0 before, /device:TPU:1 now
where the time goes in v4:
time: 730 us; the launch traced here: 721 us
  waiting for transfers between devices  392 us (54%)
  Pallas kernels  224 us (31%)
  starting transfers between devices  33.5 us (5%)
  other arithmetic  26.3 us (4%)
  matrix products  16.9 us (2%)
  local copies, waits for them, and re-layouts  15.5 us (2%)
  between operations  13.4 us (2%)
    ppermute x30, waiting for transfers between devices, send(): return lax.ppermute(x, 'sh', [(i, i ^ d) for i in range(WAYS)])  270 us
    ppermute x5, waiting for transfers between devices, across(): return lax.ppermute(x, 'dp', [(0, 1), (1, 0)])  121 us
    pallas_call x14, Pallas kernels, pack(): pl.pallas_call(functools.partial(pack_kernel, base, size, steps, source,...  108 us
    pallas_call x8, Pallas kernels, assemble(): pl.pallas_call(functools.partial(assemble_kernel, is_key, base, size, ste...  107 us
    ppermute x30, starting transfers between devices, send(): return lax.ppermute(x, 'sh', [(i, i ^ d) for i in range(WAYS)])  28.4 us
  transfers between devices with their start and end apart: 35, of which 13 were waited for; matrix products, arithmetic and copies ran while one was open for 7% of the time, Pallas kernels for 24%

profile of v4, /device:TPU:1, one launch (start us, length us, event | category | flops | bytes accessed | tf_op | source)
XLA Modules:
  0.0 720.8 jit_solution(14676465970105235169)
XLA Ops:
  0.6 2.1 collective-permute-start.84
  11.7 7.3 %pack.20 = (bf16[80,64,256]{2,1,0:T(8,128)(2,1)}, bf16[80,64,256]{2,1,0:T(8,128)(2,1)}) custom-call(s32[2,112]{1,0:T(2,128)} %get-tuple-element.496.refs_0_, s32[2,112]{1,0:T(2,128)} %get-tuple-element.495.refs_1_, bf16[1920,64,256]{2,1,0:T(8,128)(2,1)} %bitcast.56), custom_call_target="tpu_custom_call" | custom-call | flops 10000000 | bytes 10400000 | tf_op jit(solution)/shard_map/pack/pallas_call | solution.py:266
  19.0 3.8 pack.21
  22.8 2.8 pack.22
  30.0 15.3 %pack.24 = (bf16[192,64,256]{2,1,0:T(8,128)(2,1)}, bf16[192,64,256]{2,1,0:T(8,128)(2,1)}) custom-call(s32[2,192]{1,0:T(2,128)} %get-tuple-element.494.refs_0_, s32[2,192]{1,0:T(2,128)} %get-tuple-element.493.refs_1_, bf16[1920,64,256]{2,1,0:T(8,128)(2,1)} %bitcast.59), custom_call_target="tpu_custom_call" | custom-call | flops 10000000 | bytes 24960000 | tf_op jit(solution)/shard_map/pack/pallas_call | solution.py:266
  45.3 17.7 %pack.23 = (bf16[192,64,256]{2,1,0:T(8,128)(2,1)}, bf16[192,64,256]{2,1,0:T(8,128)(2,1)}) custom-call(s32[2,192]{1,0:T(2,128)} %get-tuple-element.494.refs_0_, s32[2,192]{1,0:T(2,128)} %get-tuple-element.493.refs_1_, bf16[1920,64,256]{2,1,0:T(8,128)(2,1)} %bitcast.66), custom_call_target="tpu_custom_call" | custom-call | flops 10000000 | bytes 24960000 | tf_op jit(solution)/shard_map/pack/pallas_call | solution.py:266
  63.0 4.1 pack.26
  71.7 5.1 convolution_convert_fusion
  77.0 3.1 convolution_convert_fusion.1
  80.2 3.1 fusion.2
  91.3 8.2 %pack.14 = (bf16[48,64,256]{2,1,0:T(8,128)(2,1)}, bf16[48,64,256]{2,1,0:T(8,128)(2,1)}) custom-call(s32[2,24]{1,0:T(2,128)} %select_select_fusion.7.refs_0_, s32[2,24]{1,0:T(2,128)} %select_select_fusion.6.refs_1_, bf16[1920,64,256]{2,1,0:T(8,128)(2,1)} %bitcast.68, bf16[1920,64,256]{2,1,0:T(8,128)(2,1)} %bitcast.60), custom_call_target="tpu_custom_call" | custom-call | flops 10000000 | bytes 6240000 | tf_op jit(solution)/shard_map/pack/pallas_call | solution.py:266
  107.9 1.8 broadcast_clamp_fusion.3
  113.1 21.8 %collective-permute-done.85.refs_4_ = bf16[48,64,256]{2,1,0:T(8,128)(2,1)} collective-permute-done((bf16[48,64,256]{2,1,0:T(8,128)(2,1)}, bf16[48,64,256]{2,1,0:T(8,128)(2,1)}, u32[]{:S(2)}, u32[]{:S(2)}) %collective-permute-start.85) | collective-permute-done | bytes 1572896 | tf_op jit(solution)/shard_map/ppermute | solution.py:508
  134.9 33.7 %collective-permute-done.86.refs_5_ = bf16[48,64,256]{2,1,0:T(8,128)(2,1)} collective-permute-done((bf16[48,64,256]{2,1,0:T(8,128)(2,1)}, bf16[48,64,256]{2,1,0:T(8,128)(2,1)}, u32[]{:S(2)}, u32[]{:S(2)}) %collective-permute-start.86) | collective-permute-done | bytes 1572896 | tf_op jit(solution)/shard_map/ppermute | solution.py:508
  168.6 16.7 %pack.15 = (bf16[128,64,256]{2,1,0:T(8,128)(2,1)}, bf16[128,64,256]{2,1,0:T(8,128)(2,1)}) custom-call(s32[2,128]{1,0:T(2,128)} %get-tuple-element.504.refs_0_, s32[2,128]{1,0:T(2,128)} %get-tuple-element.503.refs_1_, bf16[1920,64,256]{2,1,0:T(8,128)(2,1)} %bitcast.69, bf16[1920,64,256]{2,1,0:T(8,128)(2,1)} %bitcast.61, ...), custom_call_target="tpu_custom_call" | custom-call | flops 10000000 | bytes 16640000 | tf_op jit(solution)/shard_map/pack/pallas_call | solution.py:266
  185.3 8.1 %pack.16 = (bf16[64,64,256]{2,1,0:T(8,128)(2,1)}, bf16[64,64,256]{2,1,0:T(8,128)(2,1)}) custom-call(s32[2,128]{1,0:T(2,128)} %get-tuple-element.504.refs_0_, s32[2,128]{1,0:T(2,128)} %get-tuple-element.503.refs_1_, bf16[1920,64,256]{2,1,0:T(8,128)(2,1)} %bitcast.70, bf16[1920,64,256]{2,1,0:T(8,128)(2,1)} %bitcast.62, ...), custom_call_target="tpu_custom_call" | custom-call | flops 10000000 | bytes 8320000 | tf_op jit(solution)/shard_map/pack/pallas_call | solution.py:266
  193.5 6.1 pack.17
  199.6 4.0 pack.18
  203.7 3.0 pack.19
  206.7 115.1 %conditional.1 = (bf16[128,64,256]{2,1,0:T(8,128)(2,1)}, bf16[128,64,256]{2,1,0:T(8,128)(2,1)}, bf16[64,64,256]{2,1,0:T(8,128)(2,1)}, bf16[64,64,256]{2,1,0:T(8,...) conditional(s32[]{:T(128)} %clamp.48, () %tuple.94, ...), branch_computations={%region_6.7_spmd, %region_7.8_spmd, %region_8.9_spmd, %region_9.10... | conditional | bytes 41943280 | solution.py:653
  207.9 2.9 collective-permute-start.31
  212.0 96.0 %collective-permute-done.32 = bf16[16,64,256]{2,1,0:T(8,128)(2,1)} collective-permute-done((bf16[16,64,256]{2,1,0:T(8,128)(2,1)}, bf16[16,64,256]{2,1,0:T(8,128)(2,1)}, u32[]{:S(2)}, u32[]{:S(2)}) %collective-permute-start.32) | collective-permute-done | bytes 524320 | tf_op jit(solution)/shard_map/cond/branch_10_fun/ppermute | solution.py:505
  308.0 13.8 %collective-permute-done.33 = bf16[16,64,256]{2,1,0:T(8,128)(2,1)} collective-permute-done((bf16[16,64,256]{2,1,0:T(8,128)(2,1)}, bf16[16,64,256]{2,1,0:T(8,128)(2,1)}, u32[]{:S(2)}, u32[]{:S(2)}) %collective-permute-start.33) | collective-permute-done | bytes 524320 | tf_op jit(solution)/shard_map/cond/branch_10_fun/ppermute | solution.py:505
  323.0 3.2 pack.25
  326.5 2.0 collective-permute-start.104
  328.6 17.8 %collective-permute-done.103.refs_0_ = bf16[8,64,256]{2,1,0:T(8,128)(2,1)} collective-permute-done((bf16[8,64,256]{2,1,0:T(8,128)(2,1)}, bf16[8,64,256]{2,1,0:T(8,128)(2,1)}, u32[]{:S(2)}, u32[]{:S(2)}) %collective-permute-start.103) | collective-permute-done | bytes 262176 | tf_op jit(solution)/shard_map/ppermute | solution.py:505
  346.4 2.3 collective-permute-start.94
  348.7 4.0 collective-permute-done.104.refs_1_
  357.4 13.0 %collective-permute-done.95.refs_15_.refs_17_ = bf16[32,64,256]{2,1,0:T(8,128)(2,1)} collective-permute-done((bf16[32,64,256]{2,1,0:T(8,128)(2,1)}, bf16[32,64,256]{2,1,0:T(8,128)(2,1)}, u32[]{:S(2)}, u32[]{:S(2)}) %collective-permute-start.95) | collective-permute-done | bytes 1048608 | tf_op jit(solution)/shard_map/ppermute | solution.py:505
  370.8 7.8 %pack.27 = (bf16[80,64,256]{2,1,0:T(8,128)(2,1)}, bf16[80,64,256]{2,1,0:T(8,128)(2,1)}) custom-call(s32[2,112]{1,0:T(2,128)} %get-tuple-element.496.refs_0_, s32[2,112]{1,0:T(2,128)} %get-tuple-element.495.refs_1_, bf16[1920,64,256]{2,1,0:T(8,128)(2,1)} %bitcast.75), custom_call_target="tpu_custom_call" | custom-call | flops 10000000 | bytes 10400000 | tf_op jit(solution)/shard_map/pack/pallas_call | solution.py:266
  382.9 5.2 hand_back.1
  388.1 122.5 %collective-permute-done.106.refs_3_ = bf16[24,64,256]{2,1,0:T(8,128)(2,1)} collective-permute-done((bf16[24,64,256]{2,1,0:T(8,128)(2,1)}, bf16[24,64,256]{2,1,0:T(8,128)(2,1)}, u32[]{:S(2)}, u32[]{:S(2)}) %collective-permute-start.106) | collective-permute-done | bytes 786464 | tf_op jit(solution)/shard_map/ppermute | solution.py:505
  512.6 34.0 %collective-permute-done.100.refs_0_.refs_1_ = bf16[48,64,256]{2,1,0:T(8,128)(2,1)} collective-permute-done((bf16[48,64,256]{2,1,0:T(8,128)(2,1)}, bf16[48,64,256]{2,1,0:T(8,128)(2,1)}, u32[]{:S(2)}, u32[]{:S(2)}) %collective-permute-start.100) | collective-permute-done | bytes 1572896 | tf_op jit(solution)/shard_map/ppermute | solution.py:508
  548.4 32.0 %collective-permute-done.113.refs_0_.refs_1_ = bf16[48,64,256]{2,1,0:T(8,128)(2,1)} collective-permute-done((bf16[48,64,256]{2,1,0:T(8,128)(2,1)}, bf16[48,64,256]{2,1,0:T(8,128)(2,1)}, u32[]{:S(2)}, u32[]{:S(2)}) %collective-permute-start.113) | collective-permute-done | bytes 1572896 | tf_op jit(solution)/shard_map/ppermute | solution.py:508
  581.4 3.6 cleared.1
  588.9 1.9 and_select_fusion.21
  592.1 5.9 collective-permute-start.112
  598.0 24.1 %assemble_keys.3 = (bf16[3,4096,4,256]{3,2,1,0:T(4,128)(2,1)}, f32[4,8,26624]{2,1,0:T(8,128)}) custom-call(s32[1,416]{1,0:T(1,128)} %concatenate.48.code_ref, s32[1,416]{1,0:T(1,128)} %concatenate.49.idx_ref, s32[3]{0:T(128)} %get-tuple-element.522.n_ref, s32[1]{0:T(128)} %bitcast.8.me_ref, ...), custom_call_target="tpu_custom_call", output_to_operand_aliasing={{0}: (15, {}), {1}: (14, {})} | custom-call | flops 10000000 | bytes 56000000 | tf_op jit(solution)/shard_map/assemble_keys/pallas_call | solution.py:433
  622.2 22.4 %assemble_keys.4 = (bf16[3,4096,4,256]{3,2,1,0:T(4,128)(2,1)}, f32[4,8,26624]{2,1,0:T(8,128)}) custom-call(s32[1,416]{1,0:T(1,128)} %concatenate.48.code_ref, s32[1,416]{1,0:T(1,128)} %concatenate.49.idx_ref, s32[3]{0:T(128)} %get-tuple-element.522.n_ref, s32[1]{0:T(128)} %bitcast.8.me_ref, ...), custom_call_target="tpu_custom_call", output_to_operand_aliasing={{0}: (33, {}), {1}: (32, {})} | custom-call | flops 10000000 | bytes 128000000 | tf_op jit(solution)/shard_map/assemble_keys/pallas_call | solution.py:433
  644.6 3.6 assemble_keys.5
  648.2 2.5 reduce_max.19
  653.5 2.0 collective-permute-start.88
  657.9 23.1 %assemble_values.5 = (bf16[3,4096,4,256]{3,2,1,0:T(4,128)(2,1)}, f32[4,8,256]{2,1,0:T(8,128)}) custom-call(s32[1,416]{1,0:T(1,128)} %concatenate.48.code_ref, s32[1,416]{1,0:T(1,128)} %concatenate.49.idx_ref, s32[3]{0:T(128)} %get-tuple-element.522.n_ref, s32[1]{0:T(128)} %bitcast.8.me_ref, ...), custom_call_target="tpu_custom_call", output_to_operand_aliasing={{0}: (33, {})} | custom-call | flops 10000000 | bytes 128000000 | tf_op jit(solution)/shard_map/assemble_values/pallas_call | solution.py:433
  681.0 3.7 assemble_values.6
  684.8 17.3 %assemble_values.7 = (bf16[3,4096,4,256]{3,2,1,0:T(4,128)(2,1)}, f32[4,8,256]{2,1,0:T(8,128)}) custom-call(s32[1,416]{1,0:T(1,128)} %concatenate.48.code_ref, s32[1,416]{1,0:T(1,128)} %concatenate.49.idx_ref, s32[3]{0:T(128)} %get-tuple-element.522.n_ref, s32[1]{0:T(128)} %bitcast.8.me_ref, ...), custom_call_target="tpu_custom_call", output_to_operand_aliasing={{0}: (11, {})} | custom-call | flops 10000000 | bytes 40000000 | tf_op jit(solution)/shard_map/assemble_values/pallas_call | solution.py:433
  702.1 7.5 %assemble_values.8 = (bf16[3,4096,4,256]{3,2,1,0:T(4,128)(2,1)}, f32[4,8,256]{2,1,0:T(8,128)}) custom-call(s32[1,416]{1,0:T(1,128)} %concatenate.48.code_ref, s32[1,416]{1,0:T(1,128)} %concatenate.49.idx_ref, s32[3]{0:T(128)} %get-tuple-element.522.n_ref, s32[1]{0:T(128)} %bitcast.8.me_ref, ...), custom_call_target="tpu_custom_call", output_to_operand_aliasing={{0}: (11, {})} | custom-call | flops 10000000 | bytes 12000000 | tf_op jit(solution)/shard_map/assemble_values/pallas_call | solution.py:433
  709.5 4.8 assemble_values.9
  715.2 5.6 fusion
  (189 shorter events, 54.8 us)
Async XLA Ops:
  0.6 86.4 %collective-permute-start.84 = (s32[12]{0:T(128)}, s32[12]{0:T(128)}, u32[]{:S(2)}, u32[]{:S(2)}) collective-permute-start(s32[12]{0:T(128)} %refs_0_.1), channel_id=1, source_target_pairs={{0,4},{4,0},{1,5},{5,1},{2,6},{6,2},{3,7},{7,3}} | collective-permute-start | bytes 152 | tf_op jit(solution)/shard_map/ppermute | solution.py:508
  68.2 21.3 %copy-start.5 = (s32[2]{0:T(128)}, s32[2]{0:T(128)S(1)}, u32[]{:S(2)}) copy-start(s32[2]{0:T(128)S(1)} %get-tuple-element.469) | copy-start | bytes 28
  68.2 21.3 %copy-start.6 = (s32[2]{0:T(128)}, s32[2]{0:T(128)S(1)}, u32[]{:S(2)}) copy-start(s32[2]{0:T(128)S(1)} %get-tuple-element.470) | copy-start | bytes 28
  68.2 21.3 %copy-start.7 = (s32[2]{0:T(128)}, s32[2]{0:T(128)S(1)}, u32[]{:S(2)}) copy-start(s32[2]{0:T(128)S(1)} %get-tuple-element.471) | copy-start | bytes 28
  68.4 21.1 %copy-start.8 = (s32[2]{0:T(128)}, s32[2]{0:T(128)S(1)}, u32[]{:S(2)}) copy-start(s32[2]{0:T(128)S(1)} %get-tuple-element.474) | copy-start | bytes 28
  68.4 21.1 %copy-start.9 = (s32[2]{0:T(128)}, s32[2]{0:T(128)S(1)}, u32[]{:S(2)}) copy-start(s32[2]{0:T(128)S(1)} %get-tuple-element.475) | copy-start | bytes 28
  68.4 21.1 %copy-start.10 = (s32[2]{0:T(128)}, s32[2]{0:T(128)S(1)}, u32[]{:S(2)}) copy-start(s32[2]{0:T(128)S(1)} %get-tuple-element.476) | copy-start | bytes 28
  68.6 20.9 %copy-start.11 = (s32[2]{0:T(128)}, s32[2]{0:T(128)S(1)}, u32[]{:S(2)}) copy-start(s32[2]{0:T(128)S(1)} %get-tuple-element.472) | copy-start | bytes 28
  68.6 20.9 %copy-start.12 = (s32[2]{0:T(128)}, s32[2]{0:T(128)S(1)}, u32[]{:S(2)}) copy-start(s32[2]{0:T(128)S(1)} %get-tuple-element.473) | copy-start | bytes 28
  68.7 20.9 %copy-start.16 = (s32[2]{0:T(128)}, s32[2]{0:T(128)S(1)}, u32[]{:S(2)}) copy-start(s32[2]{0:T(128)S(1)} %add_multiply_fusion.4) | copy-start | bytes 28
  71.6 5.2 copy-start.18
  71.6 5.3 copy-start.1
  77.0 11.1 %copy-start.14 = (s32[2]{0:T(128)S(1)}, s32[2]{0:T(128)}, u32[]{:S(2)}) copy-start(s32[2]{0:T(128)} %copy-done.13) | copy-start | bytes 28
  77.0 12.4 %copy-start.2 = (s32[2]{0:T(128)S(1)}, s32[2]{0:T(128)}, u32[]{:S(2)}) copy-start(s32[2]{0:T(128)} %get-tuple-element.523) | copy-start | bytes 28
  99.5 35.4 %collective-permute-start.85 = (bf16[48,64,256]{2,1,0:T(8,128)(2,1)}, bf16[48,64,256]{2,1,0:T(8,128)(2,1)}, u32[]{:S(2)}, u32[]{:S(2)}) collective-permute-start(bf16[48,64,256]{2,1,0:T(8,128)(2,1)} %get-tuple-element.351), channel_id=1, source_target_pairs={{0,4},{4,0},{1,5},{5,1},{2,6},{6,2},{3,7},{7,3}} | collective-permute-start | bytes 4718600 | tf_op jit(solution)/shard_map/ppermute | solution.py:508
  99.5 69.1 %collective-permute-start.86 = (bf16[48,64,256]{2,1,0:T(8,128)(2,1)}, bf16[48,64,256]{2,1,0:T(8,128)(2,1)}, u32[]{:S(2)}, u32[]{:S(2)}) collective-permute-start(bf16[48,64,256]{2,1,0:T(8,128)(2,1)} %get-tuple-element.352), channel_id=1, source_target_pairs={{0,4},{4,0},{1,5},{5,1},{2,6},{6,2},{3,7},{7,3}} | collective-permute-start | bytes 4718600 | tf_op jit(solution)/shard_map/ppermute | solution.py:508
  206.7 115.1 %collective-permute-start.30 = (bf16[64,64,256]{2,1,0:T(8,128)(2,1)}, bf16[64,64,256]{2,1,0:T(8,128)(2,1)}, u32[]{:S(2)}, u32[]{:S(2)}) collective-permute-start(bf16[64,64,256]{2,1,0:T(8,128)(2,1)} %get-tuple-element.198), channel_id=1, source_target_pairs={{0,2},{1,3},{2,0},{3,1},{4,6},{5,7},{6,4},{7,5}} | collective-permute-start | bytes 6291464 | tf_op jit(solution)/shard_map/cond/branch_10_fun/ppermute | solution.py:505
  207.9 114.0 %collective-permute-start.31 = (bf16[64,64,256]{2,1,0:T(8,128)(2,1)}, bf16[64,64,256]{2,1,0:T(8,128)(2,1)}, u32[]{:S(2)}, u32[]{:S(2)}) collective-permute-start(bf16[64,64,256]{2,1,0:T(8,128)(2,1)} %get-tuple-element.199), channel_id=1, source_target_pairs={{0,3},{1,2},{2,1},{3,0},{4,7},{5,6},{6,5},{7,4}} | collective-permute-start | bytes 6291464 | tf_op jit(solution)/shard_map/cond/branch_10_fun/ppermute | solution.py:505
  210.8 97.2 %collective-permute-start.32 = (bf16[16,64,256]{2,1,0:T(8,128)(2,1)}, bf16[16,64,256]{2,1,0:T(8,128)(2,1)}, u32[]{:S(2)}, u32[]{:S(2)}) collective-permute-start(bf16[16,64,256]{2,1,0:T(8,128)(2,1)} %get-tuple-element.200), channel_id=1, source_target_pairs={{0,2},{1,3},{2,0},{3,1},{4,6},{5,7},{6,4},{7,5}} | collective-permute-start | bytes 1572872 | tf_op jit(solution)/shard_map/cond/branch_10_fun/ppermute | solution.py:505
  211.7 110.1 %collective-permute-start.33 = (bf16[16,64,256]{2,1,0:T(8,128)(2,1)}, bf16[16,64,256]{2,1,0:T(8,128)(2,1)}, u32[]{:S(2)}, u32[]{:S(2)}) collective-permute-start(bf16[16,64,256]{2,1,0:T(8,128)(2,1)} %get-tuple-element.201), channel_id=1, source_target_pairs={{0,3},{1,2},{2,1},{3,0},{4,7},{5,6},{6,5},{7,4}} | collective-permute-start | bytes 1572872 | tf_op jit(solution)/shard_map/cond/branch_10_fun/ppermute | solution.py:505
  321.8 57.4 %collective-permute-start.90 = (bf16[128,64,256]{2,1,0:T(8,128)(2,1)}, bf16[128,64,256]{2,1,0:T(8,128)(2,1)}, u32[]{:S(2)}, u32[]{:S(2)}) collective-permute-start(bf16[128,64,256]{2,1,0:T(8,128)(2,1)} %get-tuple-element.403.refs_1_), channel_id=1, source_target_pairs={{0,1},{1,0},{2,3},{3,2},{4,5},{5,4},{6,7},{7,6}} | collective-permute-start | bytes 12582920 | tf_op jit(solution)/shard_map/ppermute | solution.py:505
  321.9 30.8 %collective-permute-start.105 = (bf16[24,64,256]{2,1,0:T(8,128)(2,1)}, bf16[24,64,256]{2,1,0:T(8,128)(2,1)}, u32[]{:S(2)}, u32[]{:S(2)}) collective-permute-start(bf16[24,64,256]{2,1,0:T(8,128)(2,1)} %get-tuple-element.419), channel_id=1, source_target_pairs={{0,2},{1,3},{2,0},{3,1},{4,6},{5,7},{6,4},{7,5}} | collective-permute-start | bytes 2359304 | tf_op jit(solution)/shard_map/ppermute | solution.py:505
  326.2 20.3 %collective-permute-start.103 = (bf16[8,64,256]{2,1,0:T(8,128)(2,1)}, bf16[8,64,256]{2,1,0:T(8,128)(2,1)}, u32[]{:S(2)}, u32[]{:S(2)}) collective-permute-start(bf16[8,64,256]{2,1,0:T(8,128)(2,1)} %get-tuple-element.417), channel_id=1, source_target_pairs={{0,2},{1,3},{2,0},{3,1},{4,6},{5,7},{6,4},{7,5}} | collective-permute-start | bytes 786440 | tf_op jit(solution)/shard_map/ppermute | solution.py:505
  326.5 26.2 %collective-permute-start.104 = (bf16[8,64,256]{2,1,0:T(8,128)(2,1)}, bf16[8,64,256]{2,1,0:T(8,128)(2,1)}, u32[]{:S(2)}, u32[]{:S(2)}) collective-permute-start(bf16[8,64,256]{2,1,0:T(8,128)(2,1)} %get-tuple-element.418), channel_id=1, source_target_pairs={{0,3},{1,2},{2,1},{3,0},{4,7},{5,6},{6,5},{7,4}} | collective-permute-start | bytes 786440 | tf_op jit(solution)/shard_map/ppermute | solution.py:505
  328.6 26.5 %collective-permute-start.96 = (bf16[16,64,256]{2,1,0:T(8,128)(2,1)}, bf16[16,64,256]{2,1,0:T(8,128)(2,1)}, u32[]{:S(2)}, u32[]{:S(2)}) collective-permute-start(bf16[16,64,256]{2,1,0:T(8,128)(2,1)} %get-tuple-element.409.refs_7_), channel_id=1, source_target_pairs={{0,1},{1,0},{2,3},{3,2},{4,5},{5,4},{6,7},{7,6}} | collective-permute-start | bytes 1572872 | tf_op jit(solution)/shard_map/ppermute | solution.py:505
  346.4 10.5 %collective-permute-start.94 = (bf16[32,64,256]{2,1,0:T(8,128)(2,1)}, bf16[32,64,256]{2,1,0:T(8,128)(2,1)}, u32[]{:S(2)}, u32[]{:S(2)}) collective-permute-start(bf16[32,64,256]{2,1,0:T(8,128)(2,1)} %get-tuple-element.407.refs_5_), channel_id=1, source_target_pairs={{0,1},{1,0},{2,3},{3,2},{4,5},{5,4},{6,7},{7,6}} | collective-permute-start | bytes 3145736 | tf_op jit(solution)/shard_map/ppermute | solution.py:505
  352.7 1.9 collective-permute-start.98
  352.7 2.2 collective-permute-start.99
  354.6 2.3 collective-permute-start.97
  355.0 15.5 %collective-permute-start.92 = (bf16[64,64,256]{2,1,0:T(8,128)(2,1)}, bf16[64,64,256]{2,1,0:T(8,128)(2,1)}, u32[]{:S(2)}, u32[]{:S(2)}) collective-permute-start(bf16[64,64,256]{2,1,0:T(8,128)(2,1)} %get-tuple-element.405.refs_3_), channel_id=1, source_target_pairs={{0,1},{1,0},{2,3},{3,2},{4,5},{5,4},{6,7},{7,6}} | collective-permute-start | bytes 6291464 | tf_op jit(solution)/shard_map/ppermute | solution.py:505
  355.1 25.2 %collective-permute-start.91 = (bf16[128,64,256]{2,1,0:T(8,128)(2,1)}, bf16[128,64,256]{2,1,0:T(8,128)(2,1)}, u32[]{:S(2)}, u32[]{:S(2)}) collective-permute-start(bf16[128,64,256]{2,1,0:T(8,128)(2,1)} %get-tuple-element.402.refs_0_), channel_id=1, source_target_pairs={{0,1},{1,0},{2,3},{3,2},{4,5},{5,4},{6,7},{7,6}} | collective-permute-start | bytes 12582920 | tf_op jit(solution)/shard_map/ppermute | solution.py:505
  356.8 21.8 %collective-permute-start.93 = (bf16[64,64,256]{2,1,0:T(8,128)(2,1)}, bf16[64,64,256]{2,1,0:T(8,128)(2,1)}, u32[]{:S(2)}, u32[]{:S(2)}) collective-permute-start(bf16[64,64,256]{2,1,0:T(8,128)(2,1)} %get-tuple-element.404.refs_2_), channel_id=1, source_target_pairs={{0,1},{1,0},{2,3},{3,2},{4,5},{5,4},{6,7},{7,6}} | collective-permute-start | bytes 6291464 | tf_op jit(solution)/shard_map/ppermute | solution.py:505
  357.0 13.4 %collective-permute-start.95 = (bf16[32,64,256]{2,1,0:T(8,128)(2,1)}, bf16[32,64,256]{2,1,0:T(8,128)(2,1)}, u32[]{:S(2)}, u32[]{:S(2)}) collective-permute-start(bf16[32,64,256]{2,1,0:T(8,128)(2,1)} %get-tuple-element.406.refs_4_), channel_id=1, source_target_pairs={{0,1},{1,0},{2,3},{3,2},{4,5},{5,4},{6,7},{7,6}} | collective-permute-start | bytes 3145736 | tf_op jit(solution)/shard_map/ppermute | solution.py:505
  370.3 221.8 %collective-permute-start.102 = (bf16[192,64,256]{2,1,0:T(8,128)(2,1)}, bf16[192,64,256]{2,1,0:T(8,128)(2,1)}, u32[]{:S(2)}, u32[]{:S(2)}) collective-permute-start(bf16[192,64,256]{2,1,0:T(8,128)(2,1)} %get-tuple-element.413), channel_id=1, source_target_pairs={{0,1},{1,0},{2,3},{3,2},{4,5},{5,4},{6,7},{7,6}} | collective-permute-start | bytes 18874376 | tf_op jit(solution)/shard_map/ppermute | solution.py:505
  370.5 281.5 %collective-permute-start.89 = (bf16[192,64,256]{2,1,0:T(8,128)(2,1)}, bf16[192,64,256]{2,1,0:T(8,128)(2,1)}, u32[]{:S(2)}, u32[]{:S(2)}) collective-permute-start(bf16[192,64,256]{2,1,0:T(8,128)(2,1)} %get-tuple-element.399), channel_id=1, source_target_pairs={{0,1},{1,0},{2,3},{3,2},{4,5},{5,4},{6,7},{7,6}} | collective-permute-start | bytes 18874376 | tf_op jit(solution)/shard_map/ppermute | solution.py:505
  378.6 132.0 %collective-permute-start.107 = (bf16[80,64,256]{2,1,0:T(8,128)(2,1)}, bf16[80,64,256]{2,1,0:T(8,128)(2,1)}, u32[]{:S(2)}, u32[]{:S(2)}) collective-permute-start(bf16[80,64,256]{2,1,0:T(8,128)(2,1)} %get-tuple-element.421), channel_id=1, source_target_pairs={{0,2},{1,3},{2,0},{3,1},{4,6},{5,7},{6,4},{7,5}} | collective-permute-start | bytes 7864328 | tf_op jit(solution)/shard_map/ppermute | solution.py:505
  379.2 132.8 %collective-permute-start.108 = (bf16[80,64,256]{2,1,0:T(8,128)(2,1)}, bf16[80,64,256]{2,1,0:T(8,128)(2,1)}, u32[]{:S(2)}, u32[]{:S(2)}) collective-permute-start(bf16[80,64,256]{2,1,0:T(8,128)(2,1)} %get-tuple-element.422), channel_id=1, source_target_pairs={{0,3},{1,2},{2,1},{3,0},{4,7},{5,6},{6,5},{7,4}} | collective-permute-start | bytes 7864328 | tf_op jit(solution)/shard_map/ppermute | solution.py:505
  380.3 130.3 %collective-permute-start.106 = (bf16[24,64,256]{2,1,0:T(8,128)(2,1)}, bf16[24,64,256]{2,1,0:T(8,128)(2,1)}, u32[]{:S(2)}, u32[]{:S(2)}) collective-permute-start(bf16[24,64,256]{2,1,0:T(8,128)(2,1)} %get-tuple-element.420), channel_id=1, source_target_pairs={{0,3},{1,2},{2,1},{3,0},{4,7},{5,6},{6,5},{7,4}} | collective-permute-start | bytes 2359304 | tf_op jit(solution)/shard_map/ppermute | solution.py:505
  510.6 36.1 %collective-permute-start.100 = (bf16[48,64,256]{2,1,0:T(8,128)(2,1)}, bf16[48,64,256]{2,1,0:T(8,128)(2,1)}, u32[]{:S(2)}, u32[]{:S(2)}) collective-permute-start(bf16[48,64,256]{2,1,0:T(8,128)(2,1)} %get-tuple-element.412), channel_id=1, source_target_pairs={{0,4},{4,0},{1,5},{5,1},{2,6},{6,2},{3,7},{7,3}} | collective-permute-start | bytes 4718600 | tf_op jit(solution)/shard_map/ppermute | solution.py:508
  510.6 69.8 %collective-permute-start.113 = (bf16[48,64,256]{2,1,0:T(8,128)(2,1)}, bf16[48,64,256]{2,1,0:T(8,128)(2,1)}, u32[]{:S(2)}, u32[]{:S(2)}) collective-permute-start(bf16[48,64,256]{2,1,0:T(8,128)(2,1)} %get-tuple-element.434), channel_id=1, source_target_pairs={{0,4},{4,0},{1,5},{5,1},{2,6},{6,2},{3,7},{7,3}} | collective-permute-start | bytes 4718600 | tf_op jit(solution)/shard_map/ppermute | solution.py:508
  512.1 139.9 %collective-permute-start.111 = (bf16[80,64,256]{2,1,0:T(8,128)(2,1)}, bf16[80,64,256]{2,1,0:T(8,128)(2,1)}, u32[]{:S(2)}, u32[]{:S(2)}) collective-permute-start(bf16[80,64,256]{2,1,0:T(8,128)(2,1)} %get-tuple-element.432), channel_id=1, source_target_pairs={{0,2},{1,3},{2,0},{3,1},{4,6},{5,7},{6,4},{7,5}} | collective-permute-start | bytes 7864328 | tf_op jit(solution)/shard_map/ppermute | solution.py:505
  546.6 97.9 %collective-permute-start.101 = (bf16[48,64,256]{2,1,0:T(8,128)(2,1)}, bf16[48,64,256]{2,1,0:T(8,128)(2,1)}, u32[]{:S(2)}, u32[]{:S(2)}) collective-permute-start(bf16[48,64,256]{2,1,0:T(8,128)(2,1)} %collective-permute-done.100.refs_0_.refs_1_), channel_id=1, source_target_pairs={{0,1},{1,0},{2,3},{3,2},{4,5},{5,4},{6,7},{7,6}} | collective-permute-start | bytes 4718600 | tf_op jit(solution)/shard_map/ppermute | solution.py:505
  580.3 73.1 %collective-permute-start.114 = (bf16[48,64,256]{2,1,0:T(8,128)(2,1)}, bf16[48,64,256]{2,1,0:T(8,128)(2,1)}, u32[]{:S(2)}, u32[]{:S(2)}) collective-permute-start(bf16[48,64,256]{2,1,0:T(8,128)(2,1)} %collective-permute-done.113.refs_0_.refs_1_), channel_id=1, source_target_pairs={{0,1},{1,0},{2,3},{3,2},{4,5},{5,4},{6,7},{7,6}} | collective-permute-start | bytes 4718600 | tf_op jit(solution)/shard_map/ppermute | solution.py:505
  592.1 92.6 %collective-permute-start.112 = (bf16[80,64,256]{2,1,0:T(8,128)(2,1)}, bf16[80,64,256]{2,1,0:T(8,128)(2,1)}, u32[]{:S(2)}, u32[]{:S(2)}) collective-permute-start(bf16[80,64,256]{2,1,0:T(8,128)(2,1)} %get-tuple-element.433), channel_id=1, source_target_pairs={{0,3},{1,2},{2,1},{3,0},{4,7},{5,6},{6,5},{7,4}} | collective-permute-start | bytes 7864328 | tf_op jit(solution)/shard_map/ppermute | solution.py:505
  644.5 57.5 %collective-permute-start.109 = (bf16[24,64,256]{2,1,0:T(8,128)(2,1)}, bf16[24,64,256]{2,1,0:T(8,128)(2,1)}, u32[]{:S(2)}, u32[]{:S(2)}) collective-permute-start(bf16[24,64,256]{2,1,0:T(8,128)(2,1)} %get-tuple-element.430), channel_id=1, source_target_pairs={{0,2},{1,3},{2,0},{3,1},{4,6},{5,7},{6,4},{7,5}} | collective-permute-start | bytes 2359304 | tf_op jit(solution)/shard_map/ppermute | solution.py:505
  652.0 50.0 %collective-permute-start.110 = (bf16[24,64,256]{2,1,0:T(8,128)(2,1)}, bf16[24,64,256]{2,1,0:T(8,128)(2,1)}, u32[]{:S(2)}, u32[]{:S(2)}) collective-permute-start(bf16[24,64,256]{2,1,0:T(8,128)(2,1)} %get-tuple-element.431), channel_id=1, source_target_pairs={{0,3},{1,2},{2,1},{3,0},{4,7},{5,6},{6,5},{7,4}} | collective-permute-start | bytes 2359304 | tf_op jit(solution)/shard_map/ppermute | solution.py:505
  652.0 57.5 %collective-permute-start.87 = (bf16[8,64,256]{2,1,0:T(8,128)(2,1)}, bf16[8,64,256]{2,1,0:T(8,128)(2,1)}, u32[]{:S(2)}, u32[]{:S(2)}) collective-permute-start(bf16[8,64,256]{2,1,0:T(8,128)(2,1)} %get-tuple-element.397), channel_id=1, source_target_pairs={{0,2},{1,3},{2,0},{3,1},{4,6},{5,7},{6,4},{7,5}} | collective-permute-start | bytes 786440 | tf_op jit(solution)/shard_map/ppermute | solution.py:505
  653.5 56.1 %collective-permute-start.88 = (bf16[8,64,256]{2,1,0:T(8,128)(2,1)}, bf16[8,64,256]{2,1,0:T(8,128)(2,1)}, u32[]{:S(2)}, u32[]{:S(2)}) collective-permute-start(bf16[8,64,256]{2,1,0:T(8,128)(2,1)} %get-tuple-element.398), channel_id=1, source_target_pairs={{0,3},{1,2},{2,1},{3,0},{4,7},{5,6},{6,5},{7,4}} | collective-permute-start | bytes 786440 | tf_op jit(solution)/shard_map/ppermute | solution.py:505
  (6 other events, 14.7 us)

commit v5 on v4

--- a/solution.py
+++ b/solution.py
@@ -625,6 +625,7 @@
         for base, count in zip(starts_of(V_PIECES), V_PIECES):
             packed_values.append(pack([prefill[False]], fixed_from, base, count))
 
+        residual, cross = lax.optimization_barrier((residual, cross))
         resid_f32 = residual.astype(jnp.float32)
         inv_rms = lax.rsqrt(jnp.mean(resid_f32 * resid_f32, axis=-1, keepdims=True) + EPS)
         normed = (resid_f32 * inv_rms * norm_gain.astype(jnp.float32)).astype(jnp.bfloat16)
@@ -636,7 +637,7 @@
         k_new = rotate(k_new, mine)
         new = {True: k_new.astype(jnp.float32).reshape(-1, 1, 256), False: v_new.astype(jnp.float32).reshape(-1, 1, 256)}
         q_pad = jnp.pad(q_heads.transpose(1, 0, 2, 3).reshape(WAYS, ROWS * q_group, 256), ((0, 0), (0, 8 - ROWS * q_group), (0, 0)))
-        k_cache, v_cache = cleared(mine, (ROWS, WINDOW, WAYS, 256))
+        caches = cleared(mine, (ROWS, WINDOW, WAYS, 256))
         scores = blank((WAYS, 8, codes.shape[1] * GRAN), jnp.float32)
 
         def branch(lvl):
@@ -647,8 +648,8 @@
 
             return run
 
-        spare_packed, packed_values, ready = lax.optimization_barrier((spare_packed, packed_values, (new, q_pad, scores, close_got[True][1], close_got[False][1])))
-        new, q_pad, scores, own_k, own_v = ready
+        spare_packed, packed_values, ready = lax.optimization_barrier((spare_packed, packed_values, (new, q_pad, scores, caches, close_got[True][1], close_got[False][1])))
+        new, q_pad, scores, (k_cache, v_cache), own_k, own_v = ready
         own = {True: own_k, False: own_v}
         spare_got = lax.switch(level, [branch(x) for x in range(LEVELS)], spare_packed)
         spare_got, packed_values = lax.optimization_barrier((spare_got, packed_values))

time: 730 us -> 725 us (level)
  the two profiles are of different devices: /device:TPU:1 before, /device:TPU:5 now
where the time goes in v5:
time: 725 us; the launch traced here: 716 us
  waiting for transfers between devices  377 us (52%)
  Pallas kernels  226 us (31%)
  starting transfers between devices  38 us (5%)
  other arithmetic  28.9 us (4%)
  matrix products  16.9 us (2%)
  local copies, waits for them, and re-layouts  15.1 us (2%)
  between operations  13.2 us (2%)
    ppermute x30, waiting for transfers between devices, send(): return lax.ppermute(x, 'sh', [(i, i ^ d) for i in range(WAYS)])  266 us
    pallas_call x8, Pallas kernels, assemble(): pl.pallas_call(functools.partial(assemble_kernel, is_key, base, size, ste...  114 us
    ppermute x5, waiting for transfers between devices, across(): return lax.ppermute(x, 'dp', [(0, 1), (1, 0)])  112 us
    pallas_call x14, Pallas kernels, pack(): pl.pallas_call(functools.partial(pack_kernel, base, size, steps, source,...  104 us
    ppermute x30, starting transfers between devices, send(): return lax.ppermute(x, 'sh', [(i, i ^ d) for i in range(WAYS)])  32.7 us
  transfers between devices with their start and end apart: 35, of which 13 were waited for; matrix products, arithmetic and copies ran while one was open for 7% of the time, Pallas kernels for 25%

profile of v5, /device:TPU:5, one launch (start us, length us, event | category | flops | bytes accessed | tf_op | source)
XLA Modules:
  0.0 715.9 jit_solution(8840874043549380821)
XLA Ops:
  10.1 7.3 %pack.20 = (bf16[80,64,256]{2,1,0:T(8,128)(2,1)}, bf16[80,64,256]{2,1,0:T(8,128)(2,1)}) custom-call(s32[2,112]{1,0:T(2,128)} %get-tuple-element.502.refs_0_, s32[2,112]{1,0:T(2,128)} %get-tuple-element.501.refs_1_, bf16[1920,64,256]{2,1,0:T(8,128)(2,1)} %bitcast.56), custom_call_target="tpu_custom_call" | custom-call | flops 10000000 | bytes 10400000 | tf_op jit(solution)/shard_map/pack/pallas_call | solution.py:266
  17.3 4.0 pack.21
  21.4 2.6 pack.22
  27.8 15.4 %pack.24 = (bf16[192,64,256]{2,1,0:T(8,128)(2,1)}, bf16[192,64,256]{2,1,0:T(8,128)(2,1)}) custom-call(s32[2,192]{1,0:T(2,128)} %get-tuple-element.500.refs_0_, s32[2,192]{1,0:T(2,128)} %get-tuple-element.499.refs_1_, bf16[1920,64,256]{2,1,0:T(8,128)(2,1)} %bitcast.59), custom_call_target="tpu_custom_call" | custom-call | flops 10000000 | bytes 24960000 | tf_op jit(solution)/shard_map/pack/pallas_call | solution.py:266
  43.1 16.9 %pack.23 = (bf16[192,64,256]{2,1,0:T(8,128)(2,1)}, bf16[192,64,256]{2,1,0:T(8,128)(2,1)}) custom-call(s32[2,192]{1,0:T(2,128)} %get-tuple-element.500.refs_0_, s32[2,192]{1,0:T(2,128)} %get-tuple-element.499.refs_1_, bf16[1920,64,256]{2,1,0:T(8,128)(2,1)} %bitcast.66), custom_call_target="tpu_custom_call" | custom-call | flops 10000000 | bytes 24960000 | tf_op jit(solution)/shard_map/pack/pallas_call | solution.py:266
  60.1 4.2 pack.26
  70.6 2.7 cleared.1
  86.5 7.8 %pack.14 = (bf16[48,64,256]{2,1,0:T(8,128)(2,1)}, bf16[48,64,256]{2,1,0:T(8,128)(2,1)}) custom-call(s32[2,24]{1,0:T(2,128)} %select_select_fusion.7.refs_0_, s32[2,24]{1,0:T(2,128)} %select_select_fusion.6.refs_1_, bf16[1920,64,256]{2,1,0:T(8,128)(2,1)} %bitcast.68, bf16[1920,64,256]{2,1,0:T(8,128)(2,1)} %bitcast.60), custom_call_target="tpu_custom_call" | custom-call | flops 10000000 | bytes 6240000 | tf_op jit(solution)/shard_map/pack/pallas_call | solution.py:266
  94.4 3.4 collective-permute-start.85
  98.7 5.1 convolution_convert_fusion
  104.0 3.1 convolution_convert_fusion.1
  107.8 3.1 fusion.2
  117.4 11.9 %collective-permute-done.85.refs_4_ = bf16[48,64,256]{2,1,0:T(8,128)(2,1)} collective-permute-done((bf16[48,64,256]{2,1,0:T(8,128)(2,1)}, bf16[48,64,256]{2,1,0:T(8,128)(2,1)}, u32[]{:S(2)}, u32[]{:S(2)}) %collective-permute-start.85) | collective-permute-done | bytes 1572896 | tf_op jit(solution)/shard_map/ppermute | solution.py:508
  129.2 33.7 %collective-permute-done.86.refs_5_ = bf16[48,64,256]{2,1,0:T(8,128)(2,1)} collective-permute-done((bf16[48,64,256]{2,1,0:T(8,128)(2,1)}, bf16[48,64,256]{2,1,0:T(8,128)(2,1)}, u32[]{:S(2)}, u32[]{:S(2)}) %collective-permute-start.86) | collective-permute-done | bytes 1572896 | tf_op jit(solution)/shard_map/ppermute | solution.py:508
  162.9 16.8 %pack.15 = (bf16[128,64,256]{2,1,0:T(8,128)(2,1)}, bf16[128,64,256]{2,1,0:T(8,128)(2,1)}) custom-call(s32[2,128]{1,0:T(2,128)} %get-tuple-element.510.refs_0_, s32[2,128]{1,0:T(2,128)} %get-tuple-element.509.refs_1_, bf16[1920,64,256]{2,1,0:T(8,128)(2,1)} %bitcast.69, bf16[1920,64,256]{2,1,0:T(8,128)(2,1)} %bitcast.61, ...), custom_call_target="tpu_custom_call" | custom-call | flops 10000000 | bytes 16640000 | tf_op jit(solution)/shard_map/pack/pallas_call | solution.py:266
  179.7 6.9 pack.16
  186.6 6.1 pack.17
  192.7 3.1 pack.18
  195.8 3.0 pack.19
  198.8 119.1 %conditional.1 = (bf16[128,64,256]{2,1,0:T(8,128)(2,1)}, bf16[128,64,256]{2,1,0:T(8,128)(2,1)}, bf16[64,64,256]{2,1,0:T(8,128)(2,1)}, bf16[64,64,256]{2,1,0:T(8,...) conditional(s32[]{:T(128)} %clamp.48, () %tuple.96, ...), branch_computations={%region_6.7_spmd, %region_7.8_spmd, %region_8.9_spmd, %region_9.10... | conditional | bytes 41943280 | solution.py:654
  198.8 5.5 collective-permute-start.30
  204.3 4.9 collective-permute-start.31
  211.2 90.7 %collective-permute-done.32 = bf16[16,64,256]{2,1,0:T(8,128)(2,1)} collective-permute-done((bf16[16,64,256]{2,1,0:T(8,128)(2,1)}, bf16[16,64,256]{2,1,0:T(8,128)(2,1)}, u32[]{:S(2)}, u32[]{:S(2)}) %collective-permute-start.32) | collective-permute-done | bytes 524320 | tf_op jit(solution)/shard_map/cond/branch_10_fun/ppermute | solution.py:505
  301.9 16.1 %collective-permute-done.33 = bf16[16,64,256]{2,1,0:T(8,128)(2,1)} collective-permute-done((bf16[16,64,256]{2,1,0:T(8,128)(2,1)}, bf16[16,64,256]{2,1,0:T(8,128)(2,1)}, u32[]{:S(2)}, u32[]{:S(2)}) %collective-permute-start.33) | collective-permute-done | bytes 524320 | tf_op jit(solution)/shard_map/cond/branch_10_fun/ppermute | solution.py:505
  319.4 3.2 pack.25
  322.7 2.7 collective-permute-start.104
  325.4 17.1 %collective-permute-done.103.refs_0_ = bf16[8,64,256]{2,1,0:T(8,128)(2,1)} collective-permute-done((bf16[8,64,256]{2,1,0:T(8,128)(2,1)}, bf16[8,64,256]{2,1,0:T(8,128)(2,1)}, u32[]{:S(2)}, u32[]{:S(2)}) %collective-permute-start.103) | collective-permute-done | bytes 262176 | tf_op jit(solution)/shard_map/ppermute | solution.py:505
  342.5 2.3 collective-permute-start.94
  344.8 4.0 collective-permute-done.104.refs_1_
  353.4 13.0 %collective-permute-done.95.refs_15_.refs_17_ = bf16[32,64,256]{2,1,0:T(8,128)(2,1)} collective-permute-done((bf16[32,64,256]{2,1,0:T(8,128)(2,1)}, bf16[32,64,256]{2,1,0:T(8,128)(2,1)}, u32[]{:S(2)}, u32[]{:S(2)}) %collective-permute-start.95) | collective-permute-done | bytes 1048608 | tf_op jit(solution)/shard_map/ppermute | solution.py:505
  366.9 7.1 pack.27
  379.4 5.3 hand_back.1
  384.7 121.7 %collective-permute-done.106.refs_3_ = bf16[24,64,256]{2,1,0:T(8,128)(2,1)} collective-permute-done((bf16[24,64,256]{2,1,0:T(8,128)(2,1)}, bf16[24,64,256]{2,1,0:T(8,128)(2,1)}, u32[]{:S(2)}, u32[]{:S(2)}) %collective-permute-start.106) | collective-permute-done | bytes 786464 | tf_op jit(solution)/shard_map/ppermute | solution.py:505
  506.3 1.8 collective-permute-start.100
  509.3 33.7 %collective-permute-done.100.refs_0_.refs_1_ = bf16[48,64,256]{2,1,0:T(8,128)(2,1)} collective-permute-done((bf16[48,64,256]{2,1,0:T(8,128)(2,1)}, bf16[48,64,256]{2,1,0:T(8,128)(2,1)}, u32[]{:S(2)}, u32[]{:S(2)}) %collective-permute-start.100) | collective-permute-done | bytes 1572896 | tf_op jit(solution)/shard_map/ppermute | solution.py:508
  544.2 32.5 %collective-permute-done.113.refs_0_.refs_1_ = bf16[48,64,256]{2,1,0:T(8,128)(2,1)} collective-permute-done((bf16[48,64,256]{2,1,0:T(8,128)(2,1)}, bf16[48,64,256]{2,1,0:T(8,128)(2,1)}, u32[]{:S(2)}, u32[]{:S(2)}) %collective-permute-start.113) | collective-permute-done | bytes 1572896 | tf_op jit(solution)/shard_map/ppermute | solution.py:508
  581.1 1.8 and_select_fusion.16
  585.1 24.1 %assemble_keys.3 = (bf16[3,4096,4,256]{3,2,1,0:T(4,128)(2,1)}, f32[4,8,26624]{2,1,0:T(8,128)}) custom-call(s32[1,416]{1,0:T(1,128)} %concatenate.48.code_ref, s32[1,416]{1,0:T(1,128)} %concatenate.49.idx_ref, s32[3]{0:T(128)} %get-tuple-element.528.n_ref, s32[1]{0:T(128)} %bitcast.11.me_ref, ...), custom_call_target="tpu_custom_call", output_to_operand_aliasing={{0}: (15, {}), {1}: (14, {})} | custom-call | flops 10000000 | bytes 56000000 | tf_op jit(solution)/shard_map/assemble_keys/pallas_call | solution.py:433
  609.2 24.4 %assemble_keys.4 = (bf16[3,4096,4,256]{3,2,1,0:T(4,128)(2,1)}, f32[4,8,26624]{2,1,0:T(8,128)}) custom-call(s32[1,416]{1,0:T(1,128)} %concatenate.48.code_ref, s32[1,416]{1,0:T(1,128)} %concatenate.49.idx_ref, s32[3]{0:T(128)} %get-tuple-element.528.n_ref, s32[1]{0:T(128)} %bitcast.11.me_ref, ...), custom_call_target="tpu_custom_call", output_to_operand_aliasing={{0}: (33, {}), {1}: (32, {})} | custom-call | flops 10000000 | bytes 128000000 | tf_op jit(solution)/shard_map/assemble_keys/pallas_call | solution.py:433
  633.7 5.6 assemble_keys.5
  639.3 2.5 reduce_max.19
  646.9 1.8 divide_convert_fusion.refs_27_.refs_7_.refs_5_
  649.3 24.8 %assemble_values.5 = (bf16[3,4096,4,256]{3,2,1,0:T(4,128)(2,1)}, f32[4,8,256]{2,1,0:T(8,128)}) custom-call(s32[1,416]{1,0:T(1,128)} %concatenate.48.code_ref, s32[1,416]{1,0:T(1,128)} %concatenate.49.idx_ref, s32[3]{0:T(128)} %get-tuple-element.528.n_ref, s32[1]{0:T(128)} %bitcast.11.me_ref, ...), custom_call_target="tpu_custom_call", output_to_operand_aliasing={{0}: (33, {})} | custom-call | flops 10000000 | bytes 128000000 | tf_op jit(solution)/shard_map/assemble_values/pallas_call | solution.py:433
  674.2 5.7 assemble_values.6
  679.9 17.2 %assemble_values.7 = (bf16[3,4096,4,256]{3,2,1,0:T(4,128)(2,1)}, f32[4,8,256]{2,1,0:T(8,128)}) custom-call(s32[1,416]{1,0:T(1,128)} %concatenate.48.code_ref, s32[1,416]{1,0:T(1,128)} %concatenate.49.idx_ref, s32[3]{0:T(128)} %get-tuple-element.528.n_ref, s32[1]{0:T(128)} %bitcast.11.me_ref, ...), custom_call_target="tpu_custom_call", output_to_operand_aliasing={{0}: (11, {})} | custom-call | flops 10000000 | bytes 40000000 | tf_op jit(solution)/shard_map/assemble_values/pallas_call | solution.py:433
  697.1 7.5 %assemble_values.8 = (bf16[3,4096,4,256]{3,2,1,0:T(4,128)(2,1)}, f32[4,8,256]{2,1,0:T(8,128)}) custom-call(s32[1,416]{1,0:T(1,128)} %concatenate.48.code_ref, s32[1,416]{1,0:T(1,128)} %concatenate.49.idx_ref, s32[3]{0:T(128)} %get-tuple-element.528.n_ref, s32[1]{0:T(128)} %bitcast.11.me_ref, ...), custom_call_target="tpu_custom_call", output_to_operand_aliasing={{0}: (11, {})} | custom-call | flops 10000000 | bytes 12000000 | tf_op jit(solution)/shard_map/assemble_values/pallas_call | solution.py:433
  704.6 4.8 assemble_values.9
  710.3 5.6 fusion
  (189 shorter events, 58.5 us)
Async XLA Ops:
  0.6 75.8 %collective-permute-start.84 = (s32[12]{0:T(128)}, s32[12]{0:T(128)}, u32[]{:S(2)}, u32[]{:S(2)}) collective-permute-start(s32[12]{0:T(128)} %refs_0_.1), channel_id=1, source_target_pairs={{0,4},{4,0},{1,5},{5,1},{2,6},{6,2},{3,7},{7,3}} | collective-permute-start | bytes 152 | tf_op jit(solution)/shard_map/ppermute | solution.py:508
  94.4 34.9 %collective-permute-start.85 = (bf16[48,64,256]{2,1,0:T(8,128)(2,1)}, bf16[48,64,256]{2,1,0:T(8,128)(2,1)}, u32[]{:S(2)}, u32[]{:S(2)}) collective-permute-start(bf16[48,64,256]{2,1,0:T(8,128)(2,1)} %get-tuple-element.354), channel_id=1, source_target_pairs={{0,4},{4,0},{1,5},{5,1},{2,6},{6,2},{3,7},{7,3}} | collective-permute-start | bytes 4718600 | tf_op jit(solution)/shard_map/ppermute | solution.py:508
  97.8 65.1 %collective-permute-start.86 = (bf16[48,64,256]{2,1,0:T(8,128)(2,1)}, bf16[48,64,256]{2,1,0:T(8,128)(2,1)}, u32[]{:S(2)}, u32[]{:S(2)}) collective-permute-start(bf16[48,64,256]{2,1,0:T(8,128)(2,1)} %get-tuple-element.355), channel_id=1, source_target_pairs={{0,4},{4,0},{1,5},{5,1},{2,6},{6,2},{3,7},{7,3}} | collective-permute-start | bytes 4718600 | tf_op jit(solution)/shard_map/ppermute | solution.py:508
  103.9 7.0 copy-start.3
  103.9 10.8 %copy-start.5 = (s32[2]{0:T(128)S(1)}, s32[2]{0:T(128)}, u32[]{:S(2)}) copy-start(s32[2]{0:T(128)} %get-tuple-element.530) | copy-start | bytes 28
  103.9 12.0 %copy-start.6 = (s32[2]{0:T(128)S(1)}, s32[2]{0:T(128)}, u32[]{:S(2)}) copy-start(s32[2]{0:T(128)} %get-tuple-element.529) | copy-start | bytes 28
  103.9 12.7 %copy-start.9 = (s32[2]{0:T(128)S(1)}, s32[2]{0:T(128)}, u32[]{:S(2)}) copy-start(s32[2]{0:T(128)} %get-tuple-element.475) | copy-start | bytes 28
  103.9 12.6 %copy-start.10 = (s32[2]{0:T(128)S(1)}, s32[2]{0:T(128)}, u32[]{:S(2)}) copy-start(s32[2]{0:T(128)} %get-tuple-element.476) | copy-start | bytes 28
  103.9 12.6 %copy-start.11 = (s32[2]{0:T(128)S(1)}, s32[2]{0:T(128)}, u32[]{:S(2)}) copy-start(s32[2]{0:T(128)} %get-tuple-element.477) | copy-start | bytes 28
  104.0 12.6 %copy-start.12 = (s32[2]{0:T(128)S(1)}, s32[2]{0:T(128)}, u32[]{:S(2)}) copy-start(s32[2]{0:T(128)} %get-tuple-element.480) | copy-start | bytes 28
  104.0 12.6 %copy-start.13 = (s32[2]{0:T(128)S(1)}, s32[2]{0:T(128)}, u32[]{:S(2)}) copy-start(s32[2]{0:T(128)} %get-tuple-element.481) | copy-start | bytes 28
  104.0 12.6 %copy-start.14 = (s32[2]{0:T(128)S(1)}, s32[2]{0:T(128)}, u32[]{:S(2)}) copy-start(s32[2]{0:T(128)} %get-tuple-element.482) | copy-start | bytes 28
  104.0 12.6 %copy-start.15 = (s32[2]{0:T(128)S(1)}, s32[2]{0:T(128)}, u32[]{:S(2)}) copy-start(s32[2]{0:T(128)} %get-tuple-element.478) | copy-start | bytes 28
  104.0 12.6 %copy-start.16 = (s32[2]{0:T(128)S(1)}, s32[2]{0:T(128)}, u32[]{:S(2)}) copy-start(s32[2]{0:T(128)} %get-tuple-element.479) | copy-start | bytes 28
  104.0 12.6 %copy-start.18 = (s32[2]{0:T(128)S(1)}, s32[2]{0:T(128)}, u32[]{:S(2)}) copy-start(s32[2]{0:T(128)} %add_multiply_fusion.4) | copy-start | bytes 28
  115.8 13.4 %copy-start.8 = (pred[1,128]{1,0:T(4,128)(4,1)}, pred[1,128]{1,0:T(4,128)(4,1)S(1)}, u32[]{:S(2)}) copy-start(pred[1,128]{1,0:T(4,128)(4,1)S(1)} %get-tuple-element.535) | copy-start | bytes 388
  198.8 119.1 %collective-permute-start.30 = (bf16[64,64,256]{2,1,0:T(8,128)(2,1)}, bf16[64,64,256]{2,1,0:T(8,128)(2,1)}, u32[]{:S(2)}, u32[]{:S(2)}) collective-permute-start(bf16[64,64,256]{2,1,0:T(8,128)(2,1)} %get-tuple-element.198), channel_id=1, source_target_pairs={{0,2},{1,3},{2,0},{3,1},{4,6},{5,7},{6,4},{7,5}} | collective-permute-start | bytes 6291464 | tf_op jit(solution)/shard_map/cond/branch_10_fun/ppermute | solution.py:505
  204.3 113.6 %collective-permute-start.31 = (bf16[64,64,256]{2,1,0:T(8,128)(2,1)}, bf16[64,64,256]{2,1,0:T(8,128)(2,1)}, u32[]{:S(2)}, u32[]{:S(2)}) collective-permute-start(bf16[64,64,256]{2,1,0:T(8,128)(2,1)} %get-tuple-element.199), channel_id=1, source_target_pairs={{0,3},{1,2},{2,1},{3,0},{4,7},{5,6},{6,5},{7,4}} | collective-permute-start | bytes 6291464 | tf_op jit(solution)/shard_map/cond/branch_10_fun/ppermute | solution.py:505
  209.2 92.7 %collective-permute-start.32 = (bf16[16,64,256]{2,1,0:T(8,128)(2,1)}, bf16[16,64,256]{2,1,0:T(8,128)(2,1)}, u32[]{:S(2)}, u32[]{:S(2)}) collective-permute-start(bf16[16,64,256]{2,1,0:T(8,128)(2,1)} %get-tuple-element.200), channel_id=1, source_target_pairs={{0,2},{1,3},{2,0},{3,1},{4,6},{5,7},{6,4},{7,5}} | collective-permute-start | bytes 1572872 | tf_op jit(solution)/shard_map/cond/branch_10_fun/ppermute | solution.py:505
  210.9 107.0 %collective-permute-start.33 = (bf16[16,64,256]{2,1,0:T(8,128)(2,1)}, bf16[16,64,256]{2,1,0:T(8,128)(2,1)}, u32[]{:S(2)}, u32[]{:S(2)}) collective-permute-start(bf16[16,64,256]{2,1,0:T(8,128)(2,1)} %get-tuple-element.201), channel_id=1, source_target_pairs={{0,3},{1,2},{2,1},{3,0},{4,7},{5,6},{6,5},{7,4}} | collective-permute-start | bytes 1572872 | tf_op jit(solution)/shard_map/cond/branch_10_fun/ppermute | solution.py:505
  317.9 57.9 %collective-permute-start.90 = (bf16[128,64,256]{2,1,0:T(8,128)(2,1)}, bf16[128,64,256]{2,1,0:T(8,128)(2,1)}, u32[]{:S(2)}, u32[]{:S(2)}) collective-permute-start(bf16[128,64,256]{2,1,0:T(8,128)(2,1)} %get-tuple-element.409.refs_1_), channel_id=1, source_target_pairs={{0,1},{1,0},{2,3},{3,2},{4,5},{5,4},{6,7},{7,6}} | collective-permute-start | bytes 12582920 | tf_op jit(solution)/shard_map/ppermute | solution.py:505
  318.0 30.8 %collective-permute-start.105 = (bf16[24,64,256]{2,1,0:T(8,128)(2,1)}, bf16[24,64,256]{2,1,0:T(8,128)(2,1)}, u32[]{:S(2)}, u32[]{:S(2)}) collective-permute-start(bf16[24,64,256]{2,1,0:T(8,128)(2,1)} %get-tuple-element.425), channel_id=1, source_target_pairs={{0,2},{1,3},{2,0},{3,1},{4,6},{5,7},{6,4},{7,5}} | collective-permute-start | bytes 2359304 | tf_op jit(solution)/shard_map/ppermute | solution.py:505
  322.7 19.9 %collective-permute-start.103 = (bf16[8,64,256]{2,1,0:T(8,128)(2,1)}, bf16[8,64,256]{2,1,0:T(8,128)(2,1)}, u32[]{:S(2)}, u32[]{:S(2)}) collective-permute-start(bf16[8,64,256]{2,1,0:T(8,128)(2,1)} %get-tuple-element.423), channel_id=1, source_target_pairs={{0,2},{1,3},{2,0},{3,1},{4,6},{5,7},{6,4},{7,5}} | collective-permute-start | bytes 786440 | tf_op jit(solution)/shard_map/ppermute | solution.py:505
  322.7 26.1 %collective-permute-start.104 = (bf16[8,64,256]{2,1,0:T(8,128)(2,1)}, bf16[8,64,256]{2,1,0:T(8,128)(2,1)}, u32[]{:S(2)}, u32[]{:S(2)}) collective-permute-start(bf16[8,64,256]{2,1,0:T(8,128)(2,1)} %get-tuple-element.424), channel_id=1, source_target_pairs={{0,3},{1,2},{2,1},{3,0},{4,7},{5,6},{6,5},{7,4}} | collective-permute-start | bytes 786440 | tf_op jit(solution)/shard_map/ppermute | solution.py:505
  325.4 25.7 %collective-permute-start.96 = (bf16[16,64,256]{2,1,0:T(8,128)(2,1)}, bf16[16,64,256]{2,1,0:T(8,128)(2,1)}, u32[]{:S(2)}, u32[]{:S(2)}) collective-permute-start(bf16[16,64,256]{2,1,0:T(8,128)(2,1)} %get-tuple-element.415.refs_7_), channel_id=1, source_target_pairs={{0,1},{1,0},{2,3},{3,2},{4,5},{5,4},{6,7},{7,6}} | collective-permute-start | bytes 1572872 | tf_op jit(solution)/shard_map/ppermute | solution.py:505
  342.5 10.5 %collective-permute-start.94 = (bf16[32,64,256]{2,1,0:T(8,128)(2,1)}, bf16[32,64,256]{2,1,0:T(8,128)(2,1)}, u32[]{:S(2)}, u32[]{:S(2)}) collective-permute-start(bf16[32,64,256]{2,1,0:T(8,128)(2,1)} %get-tuple-element.413.refs_5_), channel_id=1, source_target_pairs={{0,1},{1,0},{2,3},{3,2},{4,5},{5,4},{6,7},{7,6}} | collective-permute-start | bytes 3145736 | tf_op jit(solution)/shard_map/ppermute | solution.py:505
  348.8 1.9 collective-permute-start.98
  348.8 2.2 collective-permute-start.99
  350.7 2.3 collective-permute-start.97
  351.0 15.5 %collective-permute-start.92 = (bf16[64,64,256]{2,1,0:T(8,128)(2,1)}, bf16[64,64,256]{2,1,0:T(8,128)(2,1)}, u32[]{:S(2)}, u32[]{:S(2)}) collective-permute-start(bf16[64,64,256]{2,1,0:T(8,128)(2,1)} %get-tuple-element.411.refs_3_), channel_id=1, source_target_pairs={{0,1},{1,0},{2,3},{3,2},{4,5},{5,4},{6,7},{7,6}} | collective-permute-start | bytes 6291464 | tf_op jit(solution)/shard_map/ppermute | solution.py:505
  351.2 24.8 %collective-permute-start.91 = (bf16[128,64,256]{2,1,0:T(8,128)(2,1)}, bf16[128,64,256]{2,1,0:T(8,128)(2,1)}, u32[]{:S(2)}, u32[]{:S(2)}) collective-permute-start(bf16[128,64,256]{2,1,0:T(8,128)(2,1)} %get-tuple-element.408.refs_0_), channel_id=1, source_target_pairs={{0,1},{1,0},{2,3},{3,2},{4,5},{5,4},{6,7},{7,6}} | collective-permute-start | bytes 12582920 | tf_op jit(solution)/shard_map/ppermute | solution.py:505
  352.9 21.1 %collective-permute-start.93 = (bf16[64,64,256]{2,1,0:T(8,128)(2,1)}, bf16[64,64,256]{2,1,0:T(8,128)(2,1)}, u32[]{:S(2)}, u32[]{:S(2)}) collective-permute-start(bf16[64,64,256]{2,1,0:T(8,128)(2,1)} %get-tuple-element.410.refs_2_), channel_id=1, source_target_pairs={{0,1},{1,0},{2,3},{3,2},{4,5},{5,4},{6,7},{7,6}} | collective-permute-start | bytes 6291464 | tf_op jit(solution)/shard_map/ppermute | solution.py:505
  353.1 13.4 %collective-permute-start.95 = (bf16[32,64,256]{2,1,0:T(8,128)(2,1)}, bf16[32,64,256]{2,1,0:T(8,128)(2,1)}, u32[]{:S(2)}, u32[]{:S(2)}) collective-permute-start(bf16[32,64,256]{2,1,0:T(8,128)(2,1)} %get-tuple-element.412.refs_4_), channel_id=1, source_target_pairs={{0,1},{1,0},{2,3},{3,2},{4,5},{5,4},{6,7},{7,6}} | collective-permute-start | bytes 3145736 | tf_op jit(solution)/shard_map/ppermute | solution.py:505
  366.4 217.6 %collective-permute-start.102 = (bf16[192,64,256]{2,1,0:T(8,128)(2,1)}, bf16[192,64,256]{2,1,0:T(8,128)(2,1)}, u32[]{:S(2)}, u32[]{:S(2)}) collective-permute-start(bf16[192,64,256]{2,1,0:T(8,128)(2,1)} %get-tuple-element.419), channel_id=1, source_target_pairs={{0,1},{1,0},{2,3},{3,2},{4,5},{5,4},{6,7},{7,6}} | collective-permute-start | bytes 18874376 | tf_op jit(solution)/shard_map/ppermute | solution.py:505
  366.6 277.8 %collective-permute-start.89 = (bf16[192,64,256]{2,1,0:T(8,128)(2,1)}, bf16[192,64,256]{2,1,0:T(8,128)(2,1)}, u32[]{:S(2)}, u32[]{:S(2)}) collective-permute-start(bf16[192,64,256]{2,1,0:T(8,128)(2,1)} %get-tuple-element.405), channel_id=1, source_target_pairs={{0,1},{1,0},{2,3},{3,2},{4,5},{5,4},{6,7},{7,6}} | collective-permute-start | bytes 18874376 | tf_op jit(solution)/shard_map/ppermute | solution.py:505
  374.1 134.0 %collective-permute-start.107 = (bf16[80,64,256]{2,1,0:T(8,128)(2,1)}, bf16[80,64,256]{2,1,0:T(8,128)(2,1)}, u32[]{:S(2)}, u32[]{:S(2)}) collective-permute-start(bf16[80,64,256]{2,1,0:T(8,128)(2,1)} %get-tuple-element.427), channel_id=1, source_target_pairs={{0,2},{1,3},{2,0},{3,1},{4,6},{5,7},{6,4},{7,5}} | collective-permute-start | bytes 7864328 | tf_op jit(solution)/shard_map/ppermute | solution.py:505
  375.9 132.3 %collective-permute-start.108 = (bf16[80,64,256]{2,1,0:T(8,128)(2,1)}, bf16[80,64,256]{2,1,0:T(8,128)(2,1)}, u32[]{:S(2)}, u32[]{:S(2)}) collective-permute-start(bf16[80,64,256]{2,1,0:T(8,128)(2,1)} %get-tuple-element.428), channel_id=1, source_target_pairs={{0,3},{1,2},{2,1},{3,0},{4,7},{5,6},{6,5},{7,4}} | collective-permute-start | bytes 7864328 | tf_op jit(solution)/shard_map/ppermute | solution.py:505
  376.0 130.3 %collective-permute-start.106 = (bf16[24,64,256]{2,1,0:T(8,128)(2,1)}, bf16[24,64,256]{2,1,0:T(8,128)(2,1)}, u32[]{:S(2)}, u32[]{:S(2)}) collective-permute-start(bf16[24,64,256]{2,1,0:T(8,128)(2,1)} %get-tuple-element.426), channel_id=1, source_target_pairs={{0,3},{1,2},{2,1},{3,0},{4,7},{5,6},{6,5},{7,4}} | collective-permute-start | bytes 2359304 | tf_op jit(solution)/shard_map/ppermute | solution.py:505
  506.3 36.6 %collective-permute-start.100 = (bf16[48,64,256]{2,1,0:T(8,128)(2,1)}, bf16[48,64,256]{2,1,0:T(8,128)(2,1)}, u32[]{:S(2)}, u32[]{:S(2)}) collective-permute-start(bf16[48,64,256]{2,1,0:T(8,128)(2,1)} %get-tuple-element.418), channel_id=1, source_target_pairs={{0,4},{4,0},{1,5},{5,1},{2,6},{6,2},{3,7},{7,3}} | collective-permute-start | bytes 4718600 | tf_op jit(solution)/shard_map/ppermute | solution.py:508
  508.1 68.6 %collective-permute-start.113 = (bf16[48,64,256]{2,1,0:T(8,128)(2,1)}, bf16[48,64,256]{2,1,0:T(8,128)(2,1)}, u32[]{:S(2)}, u32[]{:S(2)}) collective-permute-start(bf16[48,64,256]{2,1,0:T(8,128)(2,1)} %get-tuple-element.440), channel_id=1, source_target_pairs={{0,4},{4,0},{1,5},{5,1},{2,6},{6,2},{3,7},{7,3}} | collective-permute-start | bytes 4718600 | tf_op jit(solution)/shard_map/ppermute | solution.py:508
  508.1 134.9 %collective-permute-start.111 = (bf16[80,64,256]{2,1,0:T(8,128)(2,1)}, bf16[80,64,256]{2,1,0:T(8,128)(2,1)}, u32[]{:S(2)}, u32[]{:S(2)}) collective-permute-start(bf16[80,64,256]{2,1,0:T(8,128)(2,1)} %get-tuple-element.438), channel_id=1, source_target_pairs={{0,2},{1,3},{2,0},{3,1},{4,6},{5,7},{6,4},{7,5}} | collective-permute-start | bytes 7864328 | tf_op jit(solution)/shard_map/ppermute | solution.py:505
  543.0 90.7 %collective-permute-start.101 = (bf16[48,64,256]{2,1,0:T(8,128)(2,1)}, bf16[48,64,256]{2,1,0:T(8,128)(2,1)}, u32[]{:S(2)}, u32[]{:S(2)}) collective-permute-start(bf16[48,64,256]{2,1,0:T(8,128)(2,1)} %collective-permute-done.100.refs_0_.refs_1_), channel_id=1, source_target_pairs={{0,1},{1,0},{2,3},{3,2},{4,5},{5,4},{6,7},{7,6}} | collective-permute-start | bytes 4718600 | tf_op jit(solution)/shard_map/ppermute | solution.py:505
  576.7 69.4 %collective-permute-start.114 = (bf16[48,64,256]{2,1,0:T(8,128)(2,1)}, bf16[48,64,256]{2,1,0:T(8,128)(2,1)}, u32[]{:S(2)}, u32[]{:S(2)}) collective-permute-start(bf16[48,64,256]{2,1,0:T(8,128)(2,1)} %collective-permute-done.113.refs_0_.refs_1_), channel_id=1, source_target_pairs={{0,1},{1,0},{2,3},{3,2},{4,5},{5,4},{6,7},{7,6}} | collective-permute-start | bytes 4718600 | tf_op jit(solution)/shard_map/ppermute | solution.py:505
  584.1 95.8 %collective-permute-start.112 = (bf16[80,64,256]{2,1,0:T(8,128)(2,1)}, bf16[80,64,256]{2,1,0:T(8,128)(2,1)}, u32[]{:S(2)}, u32[]{:S(2)}) collective-permute-start(bf16[80,64,256]{2,1,0:T(8,128)(2,1)} %get-tuple-element.439), channel_id=1, source_target_pairs={{0,3},{1,2},{2,1},{3,0},{4,7},{5,6},{6,5},{7,4}} | collective-permute-start | bytes 7864328 | tf_op jit(solution)/shard_map/ppermute | solution.py:505
  633.6 63.5 %collective-permute-start.109 = (bf16[24,64,256]{2,1,0:T(8,128)(2,1)}, bf16[24,64,256]{2,1,0:T(8,128)(2,1)}, u32[]{:S(2)}, u32[]{:S(2)}) collective-permute-start(bf16[24,64,256]{2,1,0:T(8,128)(2,1)} %get-tuple-element.436), channel_id=1, source_target_pairs={{0,2},{1,3},{2,0},{3,1},{4,6},{5,7},{6,4},{7,5}} | collective-permute-start | bytes 2359304 | tf_op jit(solution)/shard_map/ppermute | solution.py:505
  643.0 54.1 %collective-permute-start.110 = (bf16[24,64,256]{2,1,0:T(8,128)(2,1)}, bf16[24,64,256]{2,1,0:T(8,128)(2,1)}, u32[]{:S(2)}, u32[]{:S(2)}) collective-permute-start(bf16[24,64,256]{2,1,0:T(8,128)(2,1)} %get-tuple-element.437), channel_id=1, source_target_pairs={{0,3},{1,2},{2,1},{3,0},{4,7},{5,6},{6,5},{7,4}} | collective-permute-start | bytes 2359304 | tf_op jit(solution)/shard_map/ppermute | solution.py:505
  644.3 60.3 %collective-permute-start.87 = (bf16[8,64,256]{2,1,0:T(8,128)(2,1)}, bf16[8,64,256]{2,1,0:T(8,128)(2,1)}, u32[]{:S(2)}, u32[]{:S(2)}) collective-permute-start(bf16[8,64,256]{2,1,0:T(8,128)(2,1)} %get-tuple-element.403), channel_id=1, source_target_pairs={{0,2},{1,3},{2,0},{3,1},{4,6},{5,7},{6,4},{7,5}} | collective-permute-start | bytes 786440 | tf_op jit(solution)/shard_map/ppermute | solution.py:505
  646.1 58.6 %collective-permute-start.88 = (bf16[8,64,256]{2,1,0:T(8,128)(2,1)}, bf16[8,64,256]{2,1,0:T(8,128)(2,1)}, u32[]{:S(2)}, u32[]{:S(2)}) collective-permute-start(bf16[8,64,256]{2,1,0:T(8,128)(2,1)} %get-tuple-element.404), channel_id=1, source_target_pairs={{0,3},{1,2},{2,1},{3,0},{4,7},{5,6},{6,5},{7,4}} | collective-permute-start | bytes 786440 | tf_op jit(solution)/shard_map/ppermute | solution.py:505
  (6 other events, 25.6 us)
